TPU v7x, 8 devices: a whole 2x2x1 slice. The times are simulated.
8 devices in a mesh: dp: 1 (over z), tp: 2 (over y), cp: 4 (over x, core).
Axes of the slice: x: 2, y: 2, z: 1, core: 2. Of those that a mesh axis runs over, the one named last changes fastest.
Arguments:
- c_latent: bfloat16 [2048, 512], P(('dp', 'cp'))
- k_rope: bfloat16 [2048, 64], P(('dp', 'cp'))
- q_heads: bfloat16 [2048, 64, 192], P(('dp', 'cp'), 'tp')
- d_out: bfloat16 [2048, 64, 128], P(('dp', 'cp'), 'tp')
- w_uk: bfloat16 [512, 64, 128], P(None, 'tp')
- w_uv: bfloat16 [512, 64, 128], P(None, 'tp')
Outputs:
- output 1: bfloat16 [2048, 64, 128], P(('dp', 'cp'), 'tp')
- output 2: float32 [2048, 64, 192], P(('dp', 'cp'), 'tp')
- output 3: float32 [2048, 512], P(('dp', 'cp'))
- output 4: float32 [2048, 64], P(('dp', 'cp'))
- output 5: float32 [512, 64, 128], P('dp', 'tp')
- output 6: float32 [512, 64, 128], P('dp', 'tp')
All inputs are finite; a program needn't handle non-finite values.
Results may differ from a plain program's by a relative error of at most 0.0147516.
Values are sent between devices in bfloat16 or wider.
A program may use at most 1 GiB of HBM per device.

v0:
```python
import functools
import math

import jax
import jax.numpy as jnp
from jax import lax
from jax.experimental import pallas as pl
from jax.experimental.pallas import tpu as pltpu
from jax.sharding import PartitionSpec as P


NEG_BIG = -1.0e30
PIECE = 256
GROUP = 2
BATCH = 8
F32 = jnp.float32
BF16 = jnp.bfloat16


def dot(a, b):
    return jnp.dot(a, b, preferred_element_type=F32)


def dot_t(a, b):
    return lax.dot_general(a, b, (((1,), (1,)), ((), ())), preferred_element_type=F32)


def rows(i, n=1):
    return pl.ds(i * PIECE, n * PIECE)


def params(mib):
    return pltpu.CompilerParams(dimension_semantics=("arbitrary",), vmem_limit_bytes=mib * 2 ** 20)


def head_body(lens, scale, c_ref, ct_ref, w_s, wt_s, k_s, kt_s, v_s, vt_s, qt_s, do_s, s_s, p_s, ds_s,
              o_s, dqt_s, dw_ref, dkv_ref, dr_ref):
    n_max = max(lens)
    n_rows = n_max * PIECE
    d_n = v_s.shape[1]
    to_log2 = scale * math.log2(math.e)
    for j in range(0, n_max, 2):
        kv = dot(c_ref[rows(j, 2), :], w_s[...]).astype(BF16)
        k_s[rows(j, 2), 0:d_n] = kv[:, :d_n]
        v_s[rows(j, 2), :] = kv[:, d_n:]
        kv_t = dot(wt_s[...], ct_ref[:, rows(j, 2)]).astype(BF16)
        kt_s[0:d_n, rows(j, 2)] = kv_t[:d_n]
        vt_s[:, rows(j, 2)] = kv_t[d_n:]
    key_i = lax.broadcasted_iota(jnp.int32, (PIECE, PIECE), 0)
    qry_i = lax.broadcasted_iota(jnp.int32, (PIECE, PIECE), 1)
    for b, n in enumerate(lens):
        qt_b = qt_s[:, rows(b)]
        do_t = do_s[rows(b), :].T
        top8 = jnp.full((8, PIECE), NEG_BIG, F32)
        for j in range(n):
            s = dot(k_s[rows(j), :], qt_b)
            if j == n - 1:
                s = jnp.where(key_i <= qry_i, s, NEG_BIG)
            s_s[rows(j), :] = s
            top8 = jnp.maximum(top8, jnp.max(s.reshape(PIECE // 8, 8, PIECE), axis=0))
        top = jnp.max(top8, axis=0, keepdims=True) * to_log2
        sum8 = jnp.zeros((8, PIECE), F32)
        for j in range(n):
            p = jnp.exp2(s_s[rows(j), :] * to_log2 - top)
            sum8 = sum8 + jnp.sum(p.reshape(PIECE // 8, 8, PIECE), axis=0)
            s_s[rows(j), :] = p
            p_s[rows(j), rows(b)] = p.astype(BF16)
        inv = 1.0 / jnp.sum(sum8, axis=0, keepdims=True)
        o_t = dot(vt_s[:, 0:n * PIECE], p_s[0:n * PIECE, rows(b)]) * inv
        o_s[rows(b), :] = o_t.T.astype(BF16)
        d_dot = jnp.sum(o_t * do_t.astype(F32), axis=0, keepdims=True)
        for j in range(n):
            dp = dot(v_s[rows(j), :], do_t)
            p = s_s[rows(j), :] * inv
            p_s[rows(j), rows(b)] = p.astype(BF16)
            ds_s[rows(j), rows(b)] = (p * (dp - d_dot)).astype(BF16)
        dqt_s[:, rows(b)] = dot(kt_s[:, 0:n * PIECE], ds_s[0:n * PIECE, rows(b)]) * scale
    for j in range(n_max):
        w = PIECE * sum(1 for n in lens if n > j)
        dv = dot(p_s[rows(j), 0:w], do_s[0:w, :])
        dk = dot_t(ds_s[rows(j), 0:w], qt_s[:, 0:w]) * scale
        dkv_ref[rows(j), 0:d_n] = dk[:, :d_n].astype(BF16)
        dkv_ref[rows(j), d_n:] = dv.astype(BF16)
        dr_ref[rows(j), :] += dk[:, d_n:]
    if n_rows < dkv_ref.shape[0]:
        dkv_ref[n_rows:, :] = jnp.zeros((dkv_ref.shape[0] - n_rows, dkv_ref.shape[1]), BF16)
    dw_ref[0] = dot(ct_ref[:, 0:n_rows], dkv_ref[0:n_rows, :])


def group_kernel(cp_half, scale, n_alias, idx_ref, c_ref, ct_ref, r_ref, rt_ref, wk_ref, wv_ref, q_own, q_oth, do_own, do_oth, *rest):
    (o_own, o_oth, dq_own, dq_oth, dkv_ref, dw_ref, dr_ref,
     w_s, wt_s, k_s, kt_s, v_s, vt_s, qt_s, do_s, s_s, p_s, ds_s, o_s, dqt_s) = rest[n_alias:]
    d_n = v_s.shape[1]
    core = idx_ref[1]

    @pl.when(pl.program_id(0) == 0)
    def _():
        k_s[:, d_n:] = r_ref[...]
        kt_s[d_n:, :] = rt_ref[...]
        dr_ref[...] = jnp.zeros(dr_ref.shape, F32)

    w_s[:, 0:d_n] = wk_ref[0]
    w_s[:, d_n:] = wv_ref[0]
    wt_s[0:d_n, :] = wk_ref[0].T
    wt_s[d_n:, :] = wv_ref[0].T

    def at(i):
        return pl.ds(pl.multiple_of(i * PIECE, PIECE), PIECE)

    own_hi, own_lo, oth_hi, oth_lo = core, 3 - core, 1 - core, 2 + core
    lo, hi = pl.ds(0, PIECE), pl.ds(PIECE, PIECE)
    for pos, half, q_ref, do_ref in ((own_lo, lo, q_own, do_own), (own_hi, hi, q_own, do_own),
                                     (oth_lo, lo, q_oth, do_oth), (oth_hi, hi, q_oth, do_oth)):
        qt_s[:, at(pos)] = q_ref[0, :, half]
        do_s[at(pos), :] = do_ref[0, half, :]
    n_pieces = 4 * cp_half
    for chip in range(cp_half):
        dev_a, dev_b = 2 * chip, 2 * chip + 1
        lens = (n_pieces - dev_a, n_pieces - dev_b, dev_b + 1, dev_a + 1)
        pl.when(idx_ref[0] == chip)(functools.partial(
            head_body, lens, scale, c_ref, ct_ref, w_s, wt_s, k_s, kt_s, v_s, vt_s, qt_s, do_s, s_s, p_s, ds_s,
            o_s, dqt_s, dw_ref, dkv_ref, dr_ref))
    for pos, half, o_ref, dq_ref in ((own_lo, lo, o_own, dq_own), (own_hi, hi, o_own, dq_own),
                                     (oth_lo, lo, o_oth, dq_oth), (oth_hi, hi, o_oth, dq_oth)):
        o_ref[0, half, :] = o_s[at(pos), :]
        dq_ref[0, :, half] = dqt_s[:, at(pos)]


sds = jax.ShapeDtypeStruct


def group_call(count, cp_half, scale, idx, c_all, ct_all, r_all, rt_all, w_k, w_v, q_all, q_oth, do_all, do_oth, carried):
    seq, rank = c_all.shape
    d_r = r_all.shape[1]
    half_heads, d_qk, tok = q_oth.shape
    d_v = do_oth.shape[2]
    kv = w_k.shape[2] + w_v.shape[2]
    whole = lambda *shape: pl.BlockSpec(shape, lambda h, idx: (0,) * len(shape))
    mine = lambda *shape: pl.BlockSpec((1,) + shape, lambda h, idx: (idx[1] * half_heads + idx[2] + h, 0, 0))
    part = lambda *shape: pl.BlockSpec((1,) + shape, lambda h, idx: (idx[2] + h, 0, 0))
    in_specs = [whole(seq, rank), whole(rank, seq), whole(seq, d_r), whole(d_r, seq),
                mine(rank, w_k.shape[2]), mine(rank, d_v), mine(d_qk, tok), part(d_qk, tok), mine(tok, d_v), part(tok, d_v)]
    out_specs = [mine(tok, d_v), part(tok, d_v), mine(d_qk, tok), part(d_qk, tok),
                 pl.BlockSpec((seq, kv), lambda h, idx: (0, idx[2] + h)),
                 pl.BlockSpec((1, rank, kv), lambda h, idx: (h, 0, 0)),
                 whole(seq, d_r)]
    out_shape = [sds((2 * half_heads, tok, d_v), BF16), sds((half_heads, tok, d_v), BF16),
                 sds((2 * half_heads, d_qk, tok), F32), sds((half_heads, d_qk, tok), F32),
                 sds((seq, half_heads * kv), BF16), sds((count, rank, kv), F32), sds((seq, d_r), F32)]
    args = [idx, c_all, ct_all, r_all, rt_all, w_k, w_v, q_all, q_oth, do_all, do_oth]
    aliases = {}
    for i, arr in enumerate(carried):
        aliases[len(args)] = i
        args.append(arr)
        in_specs.append(pl.BlockSpec(memory_space=pl.ANY))
    pairs = 2 * tok * (seq // 2 + PIECE // 2)
    flops = count * (2 * pairs * (3 * d_qk + 3 * d_v) + 6 * seq * rank * kv)
    return pl.pallas_call(
        functools.partial(group_kernel, cp_half, scale, len(carried)),
        grid_spec=pltpu.PrefetchScalarGridSpec(
            num_scalar_prefetch=1, grid=(count,), in_specs=in_specs, out_specs=out_specs,
            scratch_shapes=[
                pltpu.VMEM((rank, kv), BF16), pltpu.VMEM((kv, rank), BF16),
                pltpu.VMEM((seq, d_qk), BF16), pltpu.VMEM((d_qk, seq), BF16),
                pltpu.VMEM((seq, d_v), BF16), pltpu.VMEM((d_v, seq), BF16),
                pltpu.VMEM((d_qk, 2 * tok), BF16), pltpu.VMEM((2 * tok, d_v), BF16),
                pltpu.VMEM((seq, PIECE), F32),
                pltpu.VMEM((seq, 2 * tok), BF16), pltpu.VMEM((seq, 2 * tok), BF16),
                pltpu.VMEM((2 * tok, d_v), BF16), pltpu.VMEM((d_qk, 2 * tok), F32)]),
        out_shape=out_shape,
        input_output_aliases=aliases,
        compiler_params=params(48),
        cost_estimate=pl.CostEstimate(flops=int(flops), bytes_accessed=count * 4 * 2 ** 20, transcendentals=count * pairs),
        name="heads",
    )(*args)


def dc_kernel(order, idx_ref, dkv_ref, wk_ref, wv_ref, dr_ref, out_ref, acc_s, w_s):
    rank, d_n = wk_ref.shape[1:]
    w_s[:, 0:d_n] = wk_ref[0]
    w_s[:, d_n:] = wv_ref[0]
    h = pl.program_id(0)

    @pl.when(h == 0)
    def _():
        acc_s[...] = jnp.zeros(acc_s.shape, F32)

    for j in range(len(order)):
        acc_s[rows(j), :] += dot_t(dkv_ref[rows(j), :], w_s[...])

    @pl.when(h == pl.num_programs(0) - 1)
    def _():
        for slot, piece in enumerate(order):
            out_ref[slot, :, 0:rank] = acc_s[rows(piece), :]
            dr = dr_ref[rows(piece), :]
            out_ref[slot, :, rank:] = jnp.concatenate([dr, jnp.zeros_like(dr)], axis=1)


def dc_call(idx, dkv, w_k, w_v, dr, order):
    seq, d_r = dr.shape
    half_heads = w_k.shape[0] // 2
    rank, d_n = w_k.shape[1:]
    kv = d_n + w_v.shape[2]
    mine = lambda *shape: pl.BlockSpec((1,) + shape, lambda h, idx: (idx[1] * half_heads + h, 0, 0))
    shape = (len(order), PIECE, rank + 2 * d_r)
    return pl.pallas_call(
        functools.partial(dc_kernel, order),
        grid_spec=pltpu.PrefetchScalarGridSpec(
            num_scalar_prefetch=1, grid=(half_heads,),
            in_specs=[pl.BlockSpec((seq, kv), lambda h, idx: (0, h)), mine(rank, d_n), mine(rank, d_n),
                      pl.BlockSpec((seq, d_r), lambda h, idx: (0, 0))],
            out_specs=pl.BlockSpec(shape, lambda h, idx: (0, 0, 0)),
            scratch_shapes=[pltpu.VMEM((seq, rank), F32), pltpu.VMEM((rank, kv), BF16)]),
        out_shape=sds(shape, F32),
        compiler_params=params(40),
        cost_estimate=pl.CostEstimate(flops=2 * seq * rank * kv * half_heads, bytes_accessed=30 * 2 ** 20, transcendentals=0),
        name="dc",
    )(idx, dkv, w_k, w_v, dr)


def place_kernel(idx_ref, part_ref, full_ref, out_ref):
    out_ref[...] = part_ref[...]


def place_call(idx, part, full, step):
    n, a, b = part.shape
    return pl.pallas_call(
        place_kernel,
        grid_spec=pltpu.PrefetchScalarGridSpec(
            num_scalar_prefetch=1, grid=(n // step,),
            in_specs=[pl.BlockSpec((step, a, b), lambda h, idx: (h, 0, 0)), pl.BlockSpec(memory_space=pl.ANY)],
            out_specs=pl.BlockSpec((step, a, b), lambda h, idx: ((1 - idx[1]) * (n // step) + h, 0, 0))),
        out_shape=sds(full.shape, full.dtype),
        input_output_aliases={2: 0},
        compiler_params=params(24),
        cost_estimate=pl.CostEstimate(flops=10 ** 9, bytes_accessed=2 * part.size * part.dtype.itemsize, transcendentals=0),
        name="place",
    )(idx, part, full)


def join_kernel(n_parts, idx_ref, *refs):
    a_refs, b_refs = refs[:n_parts], refs[n_parts:2 * n_parts]
    k_ref, v_ref = refs[-2:]
    d_n = k_ref.shape[2]
    for i, (a_ref, b_ref) in enumerate(zip(a_refs, b_refs)):
        for g in range(a_ref.shape[0]):
            s = a_ref[g] + b_ref[g]
            k_ref[:, i * a_ref.shape[0] + g, :] = s[:, :d_n]
            v_ref[:, i * a_ref.shape[0] + g, :] = s[:, d_n:]


def join_call(block, parts_a, parts_b, carried, n_heads):
    g, rank, kv = parts_a[0].shape
    n_parts = len(parts_a)
    r_blk = 128
    part = pl.BlockSpec((g, r_blk, kv), lambda i, idx: (0, i, 0))
    out = pl.BlockSpec((r_blk, g * n_parts, kv // 2), lambda i, idx: (i, idx[0], 0))
    args = [block, *parts_a, *parts_b, *carried]
    return pl.pallas_call(
        functools.partial(join_kernel, n_parts),
        grid_spec=pltpu.PrefetchScalarGridSpec(
            num_scalar_prefetch=1, grid=(rank // r_blk,),
            in_specs=[part] * (2 * n_parts) + [pl.BlockSpec(memory_space=pl.ANY)] * len(carried),
            out_specs=[out, out]),
        out_shape=[sds((rank, n_heads, kv // 2), F32)] * 2,
        input_output_aliases={1 + 2 * n_parts + i: i for i in range(len(carried))},
        compiler_params=params(24),
        cost_estimate=pl.CostEstimate(flops=10 ** 9, bytes_accessed=3 * n_parts * g * rank * kv * 4, transcendentals=0),
        name="join",
    )(*args)


def solution(mesh):
    n_cp = mesh.shape['cp']
    n_tp = mesh.shape['tp']
    cp_half = n_cp // 2
    x_perm = [(d, (d + 2) % n_cp) for d in range(n_cp)]
    core_perm = [(d, d ^ 1) for d in range(n_cp)]
    tp_perm = [(d, (d + 1) % n_tp) for d in range(n_tp)]
    seq_spec = P(('dp', 'cp'), None)
    head_spec = P(('dp', 'cp'), 'tp', None)
    weight_spec = P(None, 'tp', None)
    grad_spec = P('dp', 'tp', None)

    def device_fn(c_latent, k_rope, q_heads, d_out, w_uk, w_uv):
        _, rank = c_latent.shape
        n_heads = q_heads.shape[1]
        half_heads = n_heads // 2
        d_r = k_rope.shape[1]
        scale = q_heads.shape[2] ** -0.5
        me = lax.axis_index('cp')
        chip, core = me // 2, me % 2
        my_tp = lax.axis_index('tp')
        swap_x = lambda a: lax.ppermute(a, 'cp', x_perm)
        swap_core = lambda a: lax.ppermute(a, 'cp', core_perm)
        swap_tp = lambda a: lax.ppermute(a, 'tp', tp_perm)

        def gather(own, axis):
            far = swap_x(own)
            near, far_near = swap_core(own), swap_core(far)
            pick = lambda cond, a, b: jnp.where(cond, a, b)
            here = (pick(core == 0, own, near), pick(core == 0, near, own))
            there = (pick(core == 0, far, far_near), pick(core == 0, far_near, far))
            dev = [pick(chip == 0, here[0], there[0]), pick(chip == 0, here[1], there[1]),
                   pick(chip == 0, there[0], here[0]), pick(chip == 0, there[1], here[1])]
            cut = lambda a, i: lax.slice_in_dim(a, i * PIECE, (i + 1) * PIECE, axis=axis)
            return jnp.concatenate([cut(d, 0) for d in dev] + [cut(d, 1) for d in dev[::-1]], axis=axis)

        c_all, rt_all = gather(c_latent, 0), gather(k_rope.T, 1)
        ct_all, r_all = c_all.T, rt_all.T
        w_k, w_v = w_uk.transpose(1, 0, 2), w_uv.transpose(1, 0, 2)
        q_all = q_heads.transpose(1, 2, 0)
        do_all = d_out.transpose(1, 0, 2)
        away = (1 - core) * half_heads
        q_oth = swap_core(lax.dynamic_slice_in_dim(q_all, away, half_heads, 0))
        do_oth = swap_core(lax.dynamic_slice_in_dim(do_all, away, half_heads, 0))

        n_groups = half_heads // GROUP
        carried, own, far, near, far_near, dr = (), [], [], [], [], 0.0
        for g in range(n_groups):
            idx = jnp.stack([chip, core, jnp.int32(g * GROUP)]).astype(jnp.int32)
            outs = group_call(GROUP, cp_half, scale, idx, c_all, ct_all, r_all, rt_all, w_k, w_v,
                      q_all, q_oth, do_all, do_oth, carried)
            carried = outs[:5]
            own.append(outs[5])
            far.append(swap_x(outs[5]))
            near.append(swap_core(outs[5]))
            far_near.append(swap_core(far[-1]))
            dr = dr + outs[6]
        o_full, o_oth, dq_full, dq_oth, dkv = carried
        idx = jnp.stack([chip, core]).astype(jnp.int32)

        order = [piece for c in range(2) for x in range(cp_half)
                 for piece in (2 * x + c, 2 * n_cp - 1 - 2 * x - c)]
        by_dev = dc_call(idx, dkv, w_k, w_v, dr, order).reshape(2, cp_half, 2, PIECE, -1)
        dq = place_call(idx, swap_core(dq_oth), dq_full, 4).transpose(2, 0, 1)
        out = place_call(idx, swap_core(o_oth), o_full, 8).transpose(1, 0, 2)

        def fold(arr, axis, pos, swap):
            keep = lax.dynamic_index_in_dim(arr, pos, axis, keepdims=False)
            send = lax.dynamic_index_in_dim(arr, 1 - pos, axis, keepdims=False)
            return keep + swap(send)

        part = fold(by_dev, 0, core, swap_core)
        part = fold(part, 1, my_tp, swap_tp)
        part = fold(part, 0, chip, swap_x)
        mate = swap_tp(part)
        full = jnp.where(my_tp == 0, jnp.concatenate([part, mate], axis=0), jnp.concatenate([mate, part], axis=0))

        n_batch = half_heads // BATCH
        per = BATCH // GROUP
        dws = ()
        for i in range(n_batch):
            sel = slice(i * per, (i + 1) * per)
            for side, (a, b) in ((core, (own, far)), (1 - core, (near, far_near))):
                block = (side * n_batch + i).reshape(1).astype(jnp.int32)
                dws = join_call(block, a[sel], b[sel], dws, n_heads)
        return (out, dq, full[:, :rank], full[:, rank:rank + d_r], *dws)

    return jax.shard_map(device_fn, mesh=mesh,
                         in_specs=(seq_spec, seq_spec, head_spec, head_spec, weight_spec, weight_spec),
                         out_specs=(head_spec, head_spec, seq_spec, seq_spec, grad_spec, grad_spec),
                         check_vma=False)
```

profile of v0, /device:TPU:0, one launch (start us, length us, event | category | flops | bytes accessed | tf_op | source)
XLA Modules:
  0.0 467.8 jit_solution(7405684136504405201)
XLA Ops:
  0.6 1.3 copy.56
  1.9 0.9 collective-permute-start
  2.8 2.5 collective-permute-start.1
  5.7 3.8 dynamic-slice_bitcast_fusion
  9.6 5.8 %copy.87 = bf16[512,32,128]{2,0,1:T(8,128)(2,1)} copy(bf16[512,32,128]{2,1,0:T(8,128)(2,1)} %param.9) | data formatting | bytes 8388608 | tf_op args[3]
  15.4 7.9 %copy_bitcast_fusion = (bf16[32,512,128]{2,1,0:T(8,128)(2,1)}, bf16[32,512,128]{2,1,0:T(8,128)(2,1)}) fusion(bf16[512,32,128]{2,1,0:T(8,128)(2,1)} %param.11, bf16[512,32,128]{2,1,0:T(8,128)(2,1)} %param.10), kind=kLoop, calls=%fused_computation | loop fusion | bytes 16777216 | tf_op jit(solution)/shard_map/transpose | solution.py:311
  23.4 1.5 dynamic-slice_bitcast_fusion.2
  27.2 3.5 collective-permute-done.2
  31.5 1.5 select_dynamic-update-slice_fusion
  33.1 2.7 copy.77.c_ref
  35.9 23.4 %heads.8 = (bf16[32,512,128]{2,1,0:T(8,128)(2,1)}, bf16[16,512,128]{2,1,0:T(8,128)(2,1)S(1)}, f32[32,192,512]{2,1,0:T(8,128)}, f32[16,192,512]{2,1,0:T(8,128)}, ...) custom-call(s32[3]{0:T(128)S(1)} %get-tuple-element.140.idx_ref, ...), custom_call_target="tpu_custom_call" | custom-call | flops 7751073792 | bytes 8388608 | tf_op jit(solution)/shard_map/heads/pallas_call | solution.py:158
  59.3 23.6 %heads.9 = (bf16[32,512,128]{2,1,0:T(8,128)(2,1)}, bf16[16,512,128]{2,1,0:T(8,128)(2,1)S(1)}, f32[32,192,512]{2,1,0:T(8,128)}, f32[16,192,512]{2,1,0:T(8,128)}, ...) custom-call(s32[3]{0:T(128)S(1)} %get-tuple-element.152.idx_ref, ...), custom_call_target="tpu_custom_call", output_to_operand_aliasing={{0}: (11, {}), {1}: (12, {}), {2}: (13, {}), {3}: (14, {}),... | custom-call | flops 7751073792 | bytes 8388608 | tf_op jit(solution)/shard_map/heads/pallas_call | solution.py:158
  82.9 22.9 %heads.10 = (bf16[32,512,128]{2,1,0:T(8,128)(2,1)}, bf16[16,512,128]{2,1,0:T(8,128)(2,1)S(1)}, f32[32,192,512]{2,1,0:T(8,128)}, f32[16,192,512]{2,1,0:T(8,128)},...) custom-call(s32[3]{0:T(128)S(1)} %get-tuple-element.153.idx_ref, ...), custom_call_target="tpu_custom_call", output_to_operand_aliasing={{0}: (11, {}), {1}: (12, {}), {2}: (13, {}), {3}: (14, {}),... | custom-call | flops 7751073792 | bytes 8388608 | tf_op jit(solution)/shard_map/heads/pallas_call | solution.py:158
  105.8 1.0 copy-done.33
  106.8 23.1 %heads.11 = (bf16[32,512,128]{2,1,0:T(8,128)(2,1)}, bf16[16,512,128]{2,1,0:T(8,128)(2,1)S(1)}, f32[32,192,512]{2,1,0:T(8,128)}, f32[16,192,512]{2,1,0:T(8,128)},...) custom-call(s32[3]{0:T(128)S(1)} %get-tuple-element.154.idx_ref, ...), custom_call_target="tpu_custom_call", output_to_operand_aliasing={{0}: (11, {}), {1}: (12, {}), {2}: (13, {}), {3}: (14, {}),... | custom-call | flops 7751073792 | bytes 8388608 | tf_op jit(solution)/shard_map/heads/pallas_call | solution.py:158
  129.9 1.0 copy-done.36
  130.9 23.2 %heads.12 = (bf16[32,512,128]{2,1,0:T(8,128)(2,1)}, bf16[16,512,128]{2,1,0:T(8,128)(2,1)S(1)}, f32[32,192,512]{2,1,0:T(8,128)}, f32[16,192,512]{2,1,0:T(8,128)},...) custom-call(s32[3]{0:T(128)S(1)} %get-tuple-element.155.idx_ref, ...), custom_call_target="tpu_custom_call", output_to_operand_aliasing={{0}: (11, {}), {1}: (12, {}), {2}: (13, {}), {3}: (14, {}),... | custom-call | flops 7751073792 | bytes 8388608 | tf_op jit(solution)/shard_map/heads/pallas_call | solution.py:158
  154.1 1.0 copy-done.39
  155.2 23.0 %heads.13 = (bf16[32,512,128]{2,1,0:T(8,128)(2,1)}, bf16[16,512,128]{2,1,0:T(8,128)(2,1)S(1)}, f32[32,192,512]{2,1,0:T(8,128)}, f32[16,192,512]{2,1,0:T(8,128)},...) custom-call(s32[3]{0:T(128)S(1)} %get-tuple-element.156.idx_ref, ...), custom_call_target="tpu_custom_call", output_to_operand_aliasing={{0}: (11, {}), {1}: (12, {}), {2}: (13, {}), {3}: (14, {}),... | custom-call | flops 7751073792 | bytes 8388608 | tf_op jit(solution)/shard_map/heads/pallas_call | solution.py:158
  178.2 1.0 copy-done.40
  179.6 23.2 %heads.14 = (bf16[32,512,128]{2,1,0:T(8,128)(2,1)}, bf16[16,512,128]{2,1,0:T(8,128)(2,1)S(1)}, f32[32,192,512]{2,1,0:T(8,128)}, f32[16,192,512]{2,1,0:T(8,128)},...) custom-call(s32[3]{0:T(128)S(1)} %get-tuple-element.157.idx_ref, ...), custom_call_target="tpu_custom_call", output_to_operand_aliasing={{0}: (11, {}), {1}: (12, {}), {2}: (13, {}), {3}: (14, {}),... | custom-call | flops 7751073792 | bytes 8388608 | tf_op jit(solution)/shard_map/heads/pallas_call | solution.py:158
  202.8 1.0 copy-done.41
  203.9 23.2 %heads.15 = (bf16[32,512,128]{2,1,0:T(8,128)(2,1)}, bf16[16,512,128]{2,1,0:T(8,128)(2,1)S(1)}, f32[32,192,512]{2,1,0:T(8,128)}, f32[16,192,512]{2,1,0:T(8,128)},...) custom-call(s32[3]{0:T(128)S(1)} %get-tuple-element.158.idx_ref, ...), custom_call_target="tpu_custom_call", output_to_operand_aliasing={{0}: (11, {}), {1}: (12, {}), {2}: (13, {}), {3}: (14, {}),... | custom-call | flops 7751073792 | bytes 8388608 | tf_op jit(solution)/shard_map/heads/pallas_call | solution.py:158
  227.1 1.0 copy-done.42
  228.4 3.3 add_add_fusion.dr_ref
  231.8 1.0 copy-done.3
  232.8 2.0 collective-permute-start.22
  234.8 21.0 %dc.1 = f32[8,256,640]{2,1,0:T(8,128)} custom-call(s32[2]{0:T(128)S(1)} %pad_add_fusion.idx_ref, bf16[2048,4096]{1,0:T(8,128)(2,1)} %get-tuple-element.109.dkv_ref, bf16[32,512,128]{2,1,0:T(8,128)(2,1)S(1)} %copy-done.2, bf16[32,512,128]{2,1,0:T(8,128)(2,1)S(1)} %copy-done.1, f32[2048,64]{1,0:T(8,128)S(1)} %add_add_fusion.dr_ref), custom_call_target="tpu_custom_call" | custom-call | flops 8589934592 | bytes 31457280 | tf_op jit(solution)/shard_map/dc/pallas_call | solution.py:206
  255.8 3.4 dynamic-slice_bitcast_fusion.1
  259.2 1.0 copy-done.15
  260.3 1.0 copy-done.19
  261.8 19.6 %collective-permute-done.22.refs_6_ = f32[2,512,256]{2,1,0:T(8,128)} collective-permute-done((f32[2,512,256]{2,1,0:T(8,128)S(1)}, f32[2,512,256]{2,1,0:T(8,128)}, u32[]{:S(2)}, u32[]{:S(2)}) %collective-permute-start.22) | collective-permute-done | bytes 1048608 | tf_op jit(solution)/shard_map/ppermute | solution.py:294
  281.4 21.8 %collective-permute-done.24.refs_7_ = f32[2,512,256]{2,1,0:T(8,128)} collective-permute-done((f32[2,512,256]{2,1,0:T(8,128)S(1)}, f32[2,512,256]{2,1,0:T(8,128)}, u32[]{:S(2)}, u32[]{:S(2)}) %collective-permute-start.24) | collective-permute-done | bytes 1048608 | tf_op jit(solution)/shard_map/ppermute | solution.py:294
  303.2 1.0 copy-done.23
  304.7 1.0 copy-done.25
  306.0 1.0 copy-done.27
  307.0 1.7 collective-permute-start.32
  308.8 1.0 copy-done.29
  309.7 22.3 %collective-permute-done.30.refs_4_ = f32[2,512,256]{2,1,0:T(8,128)} collective-permute-done((f32[2,512,256]{2,1,0:T(8,128)}, f32[2,512,256]{2,1,0:T(8,128)}, u32[]{:S(2)}, u32[]{:S(2)}) %collective-permute-start.30) | collective-permute-done | bytes 1048608 | tf_op jit(solution)/shard_map/ppermute | solution.py:294
  332.4 1.7 collective-permute-start.36
  334.1 2.8 bitcast_add_fusion
  336.9 1.7 constant_dynamic-slice_fusion.1
  338.6 2.8 copy.80
  341.3 13.1 %collective-permute-done.32.refs_5_ = f32[2,512,256]{2,1,0:T(8,128)S(1)} collective-permute-done((f32[2,512,256]{2,1,0:T(8,128)}, f32[2,512,256]{2,1,0:T(8,128)S(1)}, u32[]{:S(2)}, u32[]{:S(2)}) %collective-permute-start.32) | collective-permute-done | bytes 1048608 | tf_op jit(solution)/shard_map/ppermute | solution.py:294
  354.4 1.8 collective-permute-start.11
  356.2 20.8 %collective-permute-done.34.refs_6_ = f32[2,512,256]{2,1,0:T(8,128)} collective-permute-done((f32[2,512,256]{2,1,0:T(8,128)}, f32[2,512,256]{2,1,0:T(8,128)}, u32[]{:S(2)}, u32[]{:S(2)}) %collective-permute-start.34) | collective-permute-done | bytes 1048608 | tf_op jit(solution)/shard_map/ppermute | solution.py:294
  377.0 21.5 %collective-permute-done.36.refs_7_ = f32[2,512,256]{2,1,0:T(8,128)} collective-permute-done((f32[2,512,256]{2,1,0:T(8,128)}, f32[2,512,256]{2,1,0:T(8,128)}, u32[]{:S(2)}, u32[]{:S(2)}) %collective-permute-start.36) | collective-permute-done | bytes 1048608 | tf_op jit(solution)/shard_map/ppermute | solution.py:294
  398.5 2.8 copy.79
  401.9 1.9 bitcast_add_fusion.1
  404.7 1.1 collective-permute-done.35.refs_6_
  405.8 1.0 copy-done.37
  407.2 14.0 %collective-permute-done.12 = f32[256,640]{0,1:T(8,128)} collective-permute-done((f32[256,640]{0,1:T(8,128)S(1)}, f32[256,640]{0,1:T(8,128)}, u32[]{:S(2)}, u32[]{:S(2)}) %collective-permute-start.12) | collective-permute-done | bytes 655392 | tf_op jit(solution)/shard_map/ppermute | solution.py:294
  421.2 2.2 bitcast_add_fusion.2
  423.4 1.8 collective-permute-start.13
  425.2 1.2 copy-done.32
  426.4 6.1 %join.4 = (f32[512,32,128]{2,1,0:T(8,128)}, f32[512,32,128]{2,1,0:T(8,128)}) custom-call(s32[1]{0:T(128)} %bitcast.23.idx_ref, f32[2,512,256]{2,1,0:T(8,128)} %get-tuple-element.122.refs_0_, f32[2,512,256]{2,1,0:T(8,128)} %get-tuple-element.123.refs_1_, f32[2,512,256]{2,1,0:T(8,128)S(1)} %copy-done.8, f32[2,512,256]{2,1,0:T(8,128)S(1)} %copy-done.12, ...), custom_call_target="tpu_custom_call" | custom-call | flops 1000000000 | bytes 12582912 | tf_op jit(solution)/shard_map/join/pallas_call | solution.py:259
  432.5 2.2 place.2
  434.8 4.7 %copy.81 = bf16[512,32,128]{2,1,0:T(8,128)(2,1)} copy(bf16[512,32,128]{2,0,1:T(8,128)(2,1)S(1)} %bitcast.38) | data formatting | bytes 8388608
  439.6 5.6 %join.5 = (f32[512,32,128]{2,1,0:T(8,128)}, f32[512,32,128]{2,1,0:T(8,128)}) custom-call(s32[1]{0:T(128)} %bitcast.22.idx_ref, f32[2,512,256]{2,1,0:T(8,128)S(1)} %copy-done.24, f32[2,512,256]{2,1,0:T(8,128)S(1)} %copy-done.26, f32[2,512,256]{2,1,0:T(8,128)S(1)} %copy-done.28, ...), custom_call_target="tpu_custom_call", output_to_operand_aliasing={{0}: (9, {}), {1}: (10, {})} | custom-call | flops 1000000000 | bytes 12582912 | tf_op jit(solution)/shard_map/join/pallas_call | solution.py:259
  445.2 6.0 %join.6 = (f32[512,32,128]{2,1,0:T(8,128)}, f32[512,32,128]{2,1,0:T(8,128)}) custom-call(s32[1]{0:T(128)} %bitcast.21.idx_ref, f32[2,512,256]{2,1,0:T(8,128)S(1)} %copy-done.6, f32[2,512,256]{2,1,0:T(8,128)S(1)} %copy-done.14, f32[2,512,256]{2,1,0:T(8,128)S(1)} %copy-done.18, ...), custom_call_target="tpu_custom_call", output_to_operand_aliasing={{0}: (9, {}), {1}: (10, {})} | custom-call | flops 1000000000 | bytes 12582912 | tf_op jit(solution)/shard_map/join/pallas_call | solution.py:259
  451.3 5.8 %join.7 = (f32[512,32,128]{2,1,0:T(8,128)}, f32[512,32,128]{2,1,0:T(8,128)}) custom-call(s32[1]{0:T(128)} %bitcast.20.idx_ref, f32[2,512,256]{2,1,0:T(8,128)S(1)} %copy-done.4, f32[2,512,256]{2,1,0:T(8,128)S(1)} %copy-done.10, f32[2,512,256]{2,1,0:T(8,128)S(1)} %copy-done.16, ...), custom_call_target="tpu_custom_call", output_to_operand_aliasing={{0}: (9, {}), {1}: (10, {})} | custom-call | flops 1000000000 | bytes 12582912 | tf_op jit(solution)/shard_map/join/pallas_call | solution.py:259
  457.1 1.9 maximum_select_fusion
  459.7 1.3 copy.82
  461.0 6.5 %place.3 = f32[32,192,512]{2,1,0:T(8,128)} custom-call(s32[2]{0:T(128)S(1)} %pad_add_fusion.idx_ref, f32[16,192,512]{2,1,0:T(8,128)} %collective-permute-done.9.part_ref, f32[32,192,512]{2,1,0:T(8,128)} %get-tuple-element.108.full_ref), custom_call_target="tpu_custom_call", output_to_operand_aliasing={{}: (2, {})} | custom-call | flops 1000000000 | bytes 12582912 | tf_op jit(solution)/shard_map/place/pallas_call | solution.py:227
  (169 shorter events, 9.2 us)
Async XLA Ops:
  1.9 28.8 %copy-start.46 = (bf16[512,512]{0,1:T(8,128)(2,1)}, bf16[512,512]{0,1:T(8,128)(2,1)S(1)}, u32[]{:S(2)}) copy-start(bf16[512,512]{0,1:T(8,128)(2,1)S(1)} %copy.56) | copy-start | bytes 1572868
  1.9 25.2 %collective-permute-start = (bf16[512,512]{0,1:T(8,128)(2,1)S(1)}, bf16[512,512]{0,1:T(8,128)(2,1)S(1)}, u32[]{:S(2)}, u32[]{:S(2)}) collective-permute-start(bf16[512,512]{0,1:T(8,128)(2,1)S(1)} %copy.56), channel_id=1, source_target_pairs={{0,1},{1,0},{2,3},{3,2},{4,5},{5,4},{6,7},{7,6}} | collective-permute-start | bytes 1572872 | tf_op jit(solution)/shard_map/ppermute | solution.py:295
  2.8 23.7 %collective-permute-start.1 = (bf16[512,512]{0,1:T(8,128)(2,1)S(1)}, bf16[512,512]{0,1:T(8,128)(2,1)S(1)}, u32[]{:S(2)}, u32[]{:S(2)}) collective-permute-start(bf16[512,512]{0,1:T(8,128)(2,1)S(1)} %copy.56), channel_id=1, source_target_pairs={{0,2},{1,3},{2,0},{3,1},{4,6},{5,7},{6,4},{7,5}} | collective-permute-start | bytes 1572872 | tf_op jit(solution)/shard_map/ppermute | solution.py:294
  5.3 20.3 %collective-permute-start.3 = (bf16[64,512]{1,0:T(8,128)(2,1)}, bf16[64,512]{1,0:T(8,128)(2,1)S(1)}, u32[]{:S(2)}, u32[]{:S(2)}) collective-permute-start(bf16[64,512]{1,0:T(8,128)(2,1)} %bitcast.68), channel_id=1, source_target_pairs={{0,1},{1,0},{2,3},{3,2},{4,5},{5,4},{6,7},{7,6}} | collective-permute-start | bytes 196616 | tf_op jit(solution)/shard_map/ppermute | solution.py:295
  5.5 19.5 %collective-permute-start.4 = (bf16[64,512]{1,0:T(8,128)(2,1)}, bf16[64,512]{1,0:T(8,128)(2,1)S(1)}, u32[]{:S(2)}, u32[]{:S(2)}) collective-permute-start(bf16[64,512]{1,0:T(8,128)(2,1)} %bitcast.69), channel_id=1, source_target_pairs={{0,2},{1,3},{2,0},{3,1},{4,6},{5,7},{6,4},{7,5}} | collective-permute-start | bytes 196616 | tf_op jit(solution)/shard_map/ppermute | solution.py:294
  9.6 26.3 %collective-permute-start.6 = (bf16[16,192,512]{2,1,0:T(8,128)(2,1)}, bf16[16,192,512]{2,1,0:T(8,128)(2,1)}, u32[]{:S(2)}, u32[]{:S(2)}) collective-permute-start(bf16[16,192,512]{2,1,0:T(8,128)(2,1)} %dynamic-slice_bitcast_fusion), channel_id=1, source_target_pairs={{0,1},{1,0},{2,3},{3,2},{4,5},{5,4},{6,7},{7,6}} | collective-permute-start | bytes 9437192 | tf_op jit(solution)/shard_map/ppermute | solution.py:295
  15.4 8.0 %copy-start.43 = (bf16[512,32,128]{2,0,1:T(8,128)(2,1)S(1)}, bf16[512,32,128]{2,0,1:T(8,128)(2,1)}, u32[]{:S(2)}) copy-start(bf16[512,32,128]{2,0,1:T(8,128)(2,1)} %copy.87) | copy-start | bytes 12582916
  25.0 1.4 collective-permute-start.5
  25.5 10.4 %collective-permute-start.7 = (bf16[16,512,128]{2,1,0:T(8,128)(2,1)}, bf16[16,512,128]{2,1,0:T(8,128)(2,1)}, u32[]{:S(2)}, u32[]{:S(2)}) collective-permute-start(bf16[16,512,128]{2,1,0:T(8,128)(2,1)} %dynamic-slice_bitcast_fusion.2), channel_id=1, source_target_pairs={{0,1},{1,0},{2,3},{3,2},{4,5},{5,4},{6,7},{7,6}} | collective-permute-start | bytes 6291464 | tf_op jit(solution)/shard_map/ppermute | solution.py:295
  26.5 4.2 collective-permute-start.2
  106.8 196.4 %copy-start.7 = (f32[2,512,256]{2,1,0:T(8,128)}, f32[2,512,256]{2,1,0:T(8,128)S(1)}, u32[]{:S(2)}) copy-start(f32[2,512,256]{2,1,0:T(8,128)S(1)} %get-tuple-element.124.refs_2_) | copy-start | bytes 3145732
  130.9 173.3 %copy-start.11 = (f32[2,512,256]{2,1,0:T(8,128)}, f32[2,512,256]{2,1,0:T(8,128)S(1)}, u32[]{:S(2)}) copy-start(f32[2,512,256]{2,1,0:T(8,128)S(1)} %get-tuple-element.125.refs_3_) | copy-start | bytes 3145732
  155.1 23.1 %copy-start.5 = (f32[2,512,256]{2,1,0:T(8,128)}, f32[2,512,256]{2,1,0:T(8,128)S(1)}, u32[]{:S(2)}) copy-start(f32[2,512,256]{2,1,0:T(8,128)S(1)} %get-tuple-element.118.refs_0_) | copy-start | bytes 3145732
  155.1 76.7 %collective-permute-start.14 = (f32[2,512,256]{2,1,0:T(8,128)S(1)}, f32[2,512,256]{2,1,0:T(8,128)S(1)}, u32[]{:S(2)}, u32[]{:S(2)}) collective-permute-start(f32[2,512,256]{2,1,0:T(8,128)S(1)} %get-tuple-element.118.refs_0_), channel_id=1, source_target_pairs={{0,1},{1,0},{2,3},{3,2},{4,5},{5,4},{6,7},{7,6}} | collective-permute-start | bytes 3145736 | tf_op jit(solution)/shard_map/ppermute | solution.py:295
  155.2 106.1 %collective-permute-start.18 = (f32[2,512,256]{2,1,0:T(8,128)S(1)}, f32[2,512,256]{2,1,0:T(8,128)}, u32[]{:S(2)}, u32[]{:S(2)}) collective-permute-start(f32[2,512,256]{2,1,0:T(8,128)S(1)} %get-tuple-element.118.refs_0_), channel_id=1, source_target_pairs={{0,2},{1,3},{2,0},{3,1},{4,6},{5,7},{6,4},{7,5}} | collective-permute-start | bytes 3145736 | tf_op jit(solution)/shard_map/ppermute | solution.py:294
  179.1 52.6 %copy-start.13 = (f32[2,512,256]{2,1,0:T(8,128)}, f32[2,512,256]{2,1,0:T(8,128)S(1)}, u32[]{:S(2)}) copy-start(f32[2,512,256]{2,1,0:T(8,128)S(1)} %get-tuple-element.119.refs_1_) | copy-start | bytes 3145732
  179.1 53.7 %collective-permute-start.15 = (f32[2,512,256]{2,1,0:T(8,128)S(1)}, f32[2,512,256]{2,1,0:T(8,128)S(1)}, u32[]{:S(2)}, u32[]{:S(2)}) collective-permute-start(f32[2,512,256]{2,1,0:T(8,128)S(1)} %get-tuple-element.119.refs_1_), channel_id=1, source_target_pairs={{0,1},{1,0},{2,3},{3,2},{4,5},{5,4},{6,7},{7,6}} | collective-permute-start | bytes 3145736 | tf_op jit(solution)/shard_map/ppermute | solution.py:295
  203.7 29.1 %copy-start.17 = (f32[2,512,256]{2,1,0:T(8,128)}, f32[2,512,256]{2,1,0:T(8,128)S(1)}, u32[]{:S(2)}) copy-start(f32[2,512,256]{2,1,0:T(8,128)S(1)} %get-tuple-element.120.refs_2_) | copy-start | bytes 3145732
  203.7 55.5 %collective-permute-start.16 = (f32[2,512,256]{2,1,0:T(8,128)S(1)}, f32[2,512,256]{2,1,0:T(8,128)S(1)}, u32[]{:S(2)}, u32[]{:S(2)}) collective-permute-start(f32[2,512,256]{2,1,0:T(8,128)S(1)} %get-tuple-element.120.refs_2_), channel_id=1, source_target_pairs={{0,1},{1,0},{2,3},{3,2},{4,5},{5,4},{6,7},{7,6}} | collective-permute-start | bytes 3145736 | tf_op jit(solution)/shard_map/ppermute | solution.py:295
  228.0 32.3 %copy-start.21 = (f32[2,512,256]{2,1,0:T(8,128)}, f32[2,512,256]{2,1,0:T(8,128)S(1)}, u32[]{:S(2)}) copy-start(f32[2,512,256]{2,1,0:T(8,128)S(1)} %get-tuple-element.121.refs_3_) | copy-start | bytes 3145732
  228.0 32.3 %collective-permute-start.17 = (f32[2,512,256]{2,1,0:T(8,128)S(1)}, f32[2,512,256]{2,1,0:T(8,128)S(1)}, u32[]{:S(2)}, u32[]{:S(2)}) collective-permute-start(f32[2,512,256]{2,1,0:T(8,128)S(1)} %get-tuple-element.121.refs_3_), channel_id=1, source_target_pairs={{0,1},{1,0},{2,3},{3,2},{4,5},{5,4},{6,7},{7,6}} | collective-permute-start | bytes 3145736 | tf_op jit(solution)/shard_map/ppermute | solution.py:295
  228.4 6.4 %copy-start.1 = (bf16[32,512,128]{2,1,0:T(8,128)(2,1)S(1)}, bf16[32,512,128]{2,1,0:T(8,128)(2,1)}, u32[]{:S(2)}) copy-start(bf16[32,512,128]{2,1,0:T(8,128)(2,1)} %get-tuple-element.159.wv_ref) | copy-start | bytes 12582916
  228.4 6.4 %copy-start.2 = (bf16[32,512,128]{2,1,0:T(8,128)(2,1)S(1)}, bf16[32,512,128]{2,1,0:T(8,128)(2,1)}, u32[]{:S(2)}) copy-start(bf16[32,512,128]{2,1,0:T(8,128)(2,1)} %get-tuple-element.160.wk_ref) | copy-start | bytes 12582916
  232.8 28.9 %collective-permute-start.20 = (f32[2,512,256]{2,1,0:T(8,128)S(1)}, f32[2,512,256]{2,1,0:T(8,128)}, u32[]{:S(2)}, u32[]{:S(2)}) collective-permute-start(f32[2,512,256]{2,1,0:T(8,128)S(1)} %get-tuple-element.119.refs_1_), channel_id=1, source_target_pairs={{0,2},{1,3},{2,0},{3,1},{4,6},{5,7},{6,4},{7,5}} | collective-permute-start | bytes 3145736 | tf_op jit(solution)/shard_map/ppermute | solution.py:294
  232.8 23.0 %copy-start.9 = (f32[2,512,256]{2,1,0:T(8,128)}, f32[2,512,256]{2,1,0:T(8,128)S(1)}, u32[]{:S(2)}) copy-start(f32[2,512,256]{2,1,0:T(8,128)S(1)} %collective-permute-done.15.refs_1_) | copy-start | bytes 3145732
  232.8 48.6 %collective-permute-start.22 = (f32[2,512,256]{2,1,0:T(8,128)S(1)}, f32[2,512,256]{2,1,0:T(8,128)}, u32[]{:S(2)}, u32[]{:S(2)}) collective-permute-start(f32[2,512,256]{2,1,0:T(8,128)S(1)} %get-tuple-element.120.refs_2_), channel_id=1, source_target_pairs={{0,2},{1,3},{2,0},{3,1},{4,6},{5,7},{6,4},{7,5}} | collective-permute-start | bytes 3145736 | tf_op jit(solution)/shard_map/ppermute | solution.py:294
  260.2 72.1 %collective-permute-start.10 = (f32[2,2,256,640]{3,2,1,0:T(8,128)}, f32[2,2,256,640]{3,2,1,0:T(8,128)}, u32[]{:S(2)}, u32[]{:S(2)}) collective-permute-start(f32[2,2,256,640]{3,2,1,0:T(8,128)} %dynamic-slice_bitcast_fusion.1), channel_id=1, source_target_pairs={{0,1},{1,0},{2,3},{3,2},{4,5},{5,4},{6,7},{7,6}} | collective-permute-start | bytes 7864328 | tf_op jit(solution)/shard_map/ppermute | solution.py:295
  261.3 41.9 %collective-permute-start.24 = (f32[2,512,256]{2,1,0:T(8,128)S(1)}, f32[2,512,256]{2,1,0:T(8,128)}, u32[]{:S(2)}, u32[]{:S(2)}) collective-permute-start(f32[2,512,256]{2,1,0:T(8,128)S(1)} %get-tuple-element.121.refs_3_), channel_id=1, source_target_pairs={{0,2},{1,3},{2,0},{3,1},{4,6},{5,7},{6,4},{7,5}} | collective-permute-start | bytes 3145736 | tf_op jit(solution)/shard_map/ppermute | solution.py:294
  261.3 41.9 %collective-permute-start.26 = (f32[2,512,256]{2,1,0:T(8,128)}, f32[2,512,256]{2,1,0:T(8,128)S(1)}, u32[]{:S(2)}, u32[]{:S(2)}) collective-permute-start(f32[2,512,256]{2,1,0:T(8,128)} %get-tuple-element.122.refs_0_), channel_id=1, source_target_pairs={{0,1},{1,0},{2,3},{3,2},{4,5},{5,4},{6,7},{7,6}} | collective-permute-start | bytes 3145736 | tf_op jit(solution)/shard_map/ppermute | solution.py:295
  261.7 43.0 %collective-permute-start.27 = (f32[2,512,256]{2,1,0:T(8,128)}, f32[2,512,256]{2,1,0:T(8,128)S(1)}, u32[]{:S(2)}, u32[]{:S(2)}) collective-permute-start(f32[2,512,256]{2,1,0:T(8,128)} %get-tuple-element.123.refs_1_), channel_id=1, source_target_pairs={{0,1},{1,0},{2,3},{3,2},{4,5},{5,4},{6,7},{7,6}} | collective-permute-start | bytes 3145736 | tf_op jit(solution)/shard_map/ppermute | solution.py:295
  281.4 179.7 %collective-permute-start.9 = (f32[16,192,512]{2,1,0:T(8,128)}, f32[16,192,512]{2,1,0:T(8,128)}, u32[]{:S(2)}, u32[]{:S(2)}) collective-permute-start(f32[16,192,512]{2,1,0:T(8,128)} %get-tuple-element.107), channel_id=1, source_target_pairs={{0,1},{1,0},{2,3},{3,2},{4,5},{5,4},{6,7},{7,6}} | collective-permute-start | bytes 18874376 | tf_op jit(solution)/shard_map/ppermute | solution.py:295
  303.2 2.8 collective-permute-start.28
  304.2 4.6 collective-permute-start.29
  305.7 26.3 %collective-permute-start.30 = (f32[2,512,256]{2,1,0:T(8,128)}, f32[2,512,256]{2,1,0:T(8,128)}, u32[]{:S(2)}, u32[]{:S(2)}) collective-permute-start(f32[2,512,256]{2,1,0:T(8,128)} %get-tuple-element.122.refs_0_), channel_id=1, source_target_pairs={{0,2},{1,3},{2,0},{3,1},{4,6},{5,7},{6,4},{7,5}} | collective-permute-start | bytes 3145736 | tf_op jit(solution)/shard_map/ppermute | solution.py:294
  307.0 47.4 %collective-permute-start.32 = (f32[2,512,256]{2,1,0:T(8,128)}, f32[2,512,256]{2,1,0:T(8,128)S(1)}, u32[]{:S(2)}, u32[]{:S(2)}) collective-permute-start(f32[2,512,256]{2,1,0:T(8,128)} %get-tuple-element.123.refs_1_), channel_id=1, source_target_pairs={{0,2},{1,3},{2,0},{3,1},{4,6},{5,7},{6,4},{7,5}} | collective-permute-start | bytes 3145736 | tf_op jit(solution)/shard_map/ppermute | solution.py:294
  309.7 91.6 %collective-permute-start.8 = (bf16[16,512,128]{2,1,0:T(8,128)(2,1)S(1)}, bf16[16,512,128]{2,1,0:T(8,128)(2,1)}, u32[]{:S(2)}, u32[]{:S(2)}) collective-permute-start(bf16[16,512,128]{2,1,0:T(8,128)(2,1)S(1)} %get-tuple-element.105), channel_id=1, source_target_pairs={{0,1},{1,0},{2,3},{3,2},{4,5},{5,4},{6,7},{7,6}} | collective-permute-start | bytes 6291464 | tf_op jit(solution)/shard_map/ppermute | solution.py:295
  332.1 44.9 %collective-permute-start.34 = (f32[2,512,256]{2,1,0:T(8,128)}, f32[2,512,256]{2,1,0:T(8,128)}, u32[]{:S(2)}, u32[]{:S(2)}) collective-permute-start(f32[2,512,256]{2,1,0:T(8,128)} %copy-done.7), channel_id=1, source_target_pairs={{0,2},{1,3},{2,0},{3,1},{4,6},{5,7},{6,4},{7,5}} | collective-permute-start | bytes 3145736 | tf_op jit(solution)/shard_map/ppermute | solution.py:294
  332.4 66.2 %collective-permute-start.36 = (f32[2,512,256]{2,1,0:T(8,128)}, f32[2,512,256]{2,1,0:T(8,128)}, u32[]{:S(2)}, u32[]{:S(2)}) collective-permute-start(f32[2,512,256]{2,1,0:T(8,128)} %copy-done.11), channel_id=1, source_target_pairs={{0,2},{1,3},{2,0},{3,1},{4,6},{5,7},{6,4},{7,5}} | collective-permute-start | bytes 3145736 | tf_op jit(solution)/shard_map/ppermute | solution.py:294
  354.4 44.1 %copy-start.31 = (f32[2,512,256]{2,1,0:T(8,128)}, f32[2,512,256]{2,1,0:T(8,128)S(1)}, u32[]{:S(2)}) copy-start(f32[2,512,256]{2,1,0:T(8,128)S(1)} %collective-permute-done.32.refs_5_) | copy-start | bytes 3145732
  354.4 47.4 %collective-permute-start.11 = (f32[2,256,640]{1,2,0:T(8,128)}, f32[2,256,640]{1,2,0:T(8,128)}, u32[]{:S(2)}, u32[]{:S(2)}) collective-permute-start(f32[2,256,640]{1,2,0:T(8,128)} %bitcast.67), channel_id=1, source_target_pairs={{0,4},{4,0},{1,5},{5,1},{2,6},{6,2},{3,7},{7,3}} | collective-permute-start | bytes 3932168 | tf_op jit(solution)/shard_map/ppermute | solution.py:296
  377.0 26.9 %collective-permute-start.19 = (f32[2,512,256]{2,1,0:T(8,128)}, f32[2,512,256]{2,1,0:T(8,128)}, u32[]{:S(2)}, u32[]{:S(2)}) collective-permute-start(f32[2,512,256]{2,1,0:T(8,128)} %collective-permute-done.18.refs_4_), channel_id=1, source_target_pairs={{0,1},{1,0},{2,3},{3,2},{4,5},{5,4},{6,7},{7,6}} | collective-permute-start | bytes 3145736 | tf_op jit(solution)/shard_map/ppermute | solution.py:295
  398.5 5.7 %collective-permute-start.31 = (f32[2,512,256]{2,1,0:T(8,128)}, f32[2,512,256]{2,1,0:T(8,128)}, u32[]{:S(2)}, u32[]{:S(2)}) collective-permute-start(f32[2,512,256]{2,1,0:T(8,128)} %collective-permute-done.30.refs_4_), channel_id=1, source_target_pairs={{0,1},{1,0},{2,3},{3,2},{4,5},{5,4},{6,7},{7,6}} | collective-permute-start | bytes 3145736 | tf_op jit(solution)/shard_map/ppermute | solution.py:295
  401.3 23.9 %copy-start.8 = (f32[2,512,256]{2,1,0:T(8,128)S(1)}, f32[2,512,256]{2,1,0:T(8,128)}, u32[]{:S(2)}) copy-start(f32[2,512,256]{2,1,0:T(8,128)} %copy-done.7) | copy-start | bytes 3145732
  401.3 23.9 %copy-start.12 = (f32[2,512,256]{2,1,0:T(8,128)S(1)}, f32[2,512,256]{2,1,0:T(8,128)}, u32[]{:S(2)}) copy-start(f32[2,512,256]{2,1,0:T(8,128)} %copy-done.11) | copy-start | bytes 3145732
  401.3 3.2 collective-permute-start.33
  401.8 4.0 collective-permute-start.35
  403.9 17.3 %collective-permute-start.12 = (f32[256,640]{0,1:T(8,128)S(1)}, f32[256,640]{0,1:T(8,128)}, u32[]{:S(2)}, u32[]{:S(2)}) collective-permute-start(f32[256,640]{0,1:T(8,128)S(1)} %dynamic-slice_bitcast_fusion.3), channel_id=1, source_target_pairs={{0,2},{1,3},{2,0},{3,1},{4,6},{5,7},{6,4},{7,5}} | collective-permute-start | bytes 1966088 | tf_op jit(solution)/shard_map/ppermute | solution.py:294
  404.2 19.2 %collective-permute-start.37 = (f32[2,512,256]{2,1,0:T(8,128)}, f32[2,512,256]{2,1,0:T(8,128)}, u32[]{:S(2)}, u32[]{:S(2)}) collective-permute-start(f32[2,512,256]{2,1,0:T(8,128)} %collective-permute-done.36.refs_7_), channel_id=1, source_target_pairs={{0,1},{1,0},{2,3},{3,2},{4,5},{5,4},{6,7},{7,6}} | collective-permute-start | bytes 3145736 | tf_op jit(solution)/shard_map/ppermute | solution.py:295
  404.5 20.7 %copy-start.34 = (f32[2,512,256]{2,1,0:T(8,128)}, f32[2,512,256]{2,1,0:T(8,128)S(1)}, u32[]{:S(2)}) copy-start(f32[2,512,256]{2,1,0:T(8,128)S(1)} %collective-permute-done.33.refs_5_) | copy-start | bytes 3145732
  404.5 46.7 %collective-permute-start.21 = (f32[2,512,256]{2,1,0:T(8,128)}, f32[2,512,256]{2,1,0:T(8,128)}, u32[]{:S(2)}, u32[]{:S(2)}) collective-permute-start(f32[2,512,256]{2,1,0:T(8,128)} %collective-permute-done.20.refs_5_), channel_id=1, source_target_pairs={{0,1},{1,0},{2,3},{3,2},{4,5},{5,4},{6,7},{7,6}} | collective-permute-start | bytes 3145736 | tf_op jit(solution)/shard_map/ppermute | solution.py:295
  406.8 44.4 %collective-permute-start.23 = (f32[2,512,256]{2,1,0:T(8,128)}, f32[2,512,256]{2,1,0:T(8,128)}, u32[]{:S(2)}, u32[]{:S(2)}) collective-permute-start(f32[2,512,256]{2,1,0:T(8,128)} %collective-permute-done.22.refs_6_), channel_id=1, source_target_pairs={{0,1},{1,0},{2,3},{3,2},{4,5},{5,4},{6,7},{7,6}} | collective-permute-start | bytes 3145736 | tf_op jit(solution)/shard_map/ppermute | solution.py:295
  421.2 30.0 %collective-permute-start.25 = (f32[2,512,256]{2,1,0:T(8,128)}, f32[2,512,256]{2,1,0:T(8,128)}, u32[]{:S(2)}, u32[]{:S(2)}) collective-permute-start(f32[2,512,256]{2,1,0:T(8,128)} %collective-permute-done.24.refs_7_), channel_id=1, source_target_pairs={{0,1},{1,0},{2,3},{3,2},{4,5},{5,4},{6,7},{7,6}} | collective-permute-start | bytes 3145736 | tf_op jit(solution)/shard_map/ppermute | solution.py:295
  423.4 33.7 %collective-permute-start.13 = (f32[256,640]{0,1:T(8,128)}, f32[256,640]{0,1:T(8,128)}, u32[]{:S(2)}, u32[]{:S(2)}) collective-permute-start(f32[256,640]{0,1:T(8,128)} %bitcast_add_fusion.2), channel_id=1, source_target_pairs={{0,4},{4,0},{1,5},{5,1},{2,6},{6,2},{3,7},{7,3}} | collective-permute-start | bytes 1966088 | tf_op jit(solution)/shard_map/ppermute | solution.py:296
  426.4 6.1 %copy-start = (bf16[32,512,128]{2,1,0:T(8,128)(2,1)S(1)}, bf16[32,512,128]{2,1,0:T(8,128)(2,1)}, u32[]{:S(2)}) copy-start(bf16[32,512,128]{2,1,0:T(8,128)(2,1)} %get-tuple-element.106.full_ref) | copy-start | bytes 12582916
  434.7 4.8 %copy-start.24 = (f32[2,512,256]{2,1,0:T(8,128)S(1)}, f32[2,512,256]{2,1,0:T(8,128)}, u32[]{:S(2)}) copy-start(f32[2,512,256]{2,1,0:T(8,128)} %copy-done.23) | copy-start | bytes 3145732
  434.7 4.8 %copy-start.26 = (f32[2,512,256]{2,1,0:T(8,128)S(1)}, f32[2,512,256]{2,1,0:T(8,128)}, u32[]{:S(2)}) copy-start(f32[2,512,256]{2,1,0:T(8,128)} %copy-done.25) | copy-start | bytes 3145732
  439.5 5.7 %copy-start.6 = (f32[2,512,256]{2,1,0:T(8,128)S(1)}, f32[2,512,256]{2,1,0:T(8,128)}, u32[]{:S(2)}) copy-start(f32[2,512,256]{2,1,0:T(8,128)} %copy-done.5) | copy-start | bytes 3145732
  439.5 5.7 %copy-start.14 = (f32[2,512,256]{2,1,0:T(8,128)S(1)}, f32[2,512,256]{2,1,0:T(8,128)}, u32[]{:S(2)}) copy-start(f32[2,512,256]{2,1,0:T(8,128)} %copy-done.13) | copy-start | bytes 3145732
  439.5 5.7 %copy-start.18 = (f32[2,512,256]{2,1,0:T(8,128)S(1)}, f32[2,512,256]{2,1,0:T(8,128)}, u32[]{:S(2)}) copy-start(f32[2,512,256]{2,1,0:T(8,128)} %copy-done.17) | copy-start | bytes 3145732
  439.6 5.7 %copy-start.22 = (f32[2,512,256]{2,1,0:T(8,128)S(1)}, f32[2,512,256]{2,1,0:T(8,128)}, u32[]{:S(2)}) copy-start(f32[2,512,256]{2,1,0:T(8,128)} %copy-done.21) | copy-start | bytes 3145732
  445.2 6.0 %copy-start.4 = (f32[2,512,256]{2,1,0:T(8,128)S(1)}, f32[2,512,256]{2,1,0:T(8,128)}, u32[]{:S(2)}) copy-start(f32[2,512,256]{2,1,0:T(8,128)} %copy-done.3) | copy-start | bytes 3145732
  445.2 6.0 %copy-start.10 = (f32[2,512,256]{2,1,0:T(8,128)S(1)}, f32[2,512,256]{2,1,0:T(8,128)}, u32[]{:S(2)}) copy-start(f32[2,512,256]{2,1,0:T(8,128)} %copy-done.9) | copy-start | bytes 3145732
  445.2 6.0 %copy-start.16 = (f32[2,512,256]{2,1,0:T(8,128)S(1)}, f32[2,512,256]{2,1,0:T(8,128)}, u32[]{:S(2)}) copy-start(f32[2,512,256]{2,1,0:T(8,128)} %copy-done.15) | copy-start | bytes 3145732
  445.2 6.0 %copy-start.20 = (f32[2,512,256]{2,1,0:T(8,128)S(1)}, f32[2,512,256]{2,1,0:T(8,128)}, u32[]{:S(2)}) copy-start(f32[2,512,256]{2,1,0:T(8,128)} %copy-done.19) | copy-start | bytes 3145732
  (25 other events, 50.7 us)
where the time goes:
time: 473 us; the launch traced here: 468 us
  Pallas kernels  239 us (51%)
  waiting for transfers between devices  139 us (29%)
  local copies, waits for them, and re-layouts  56.7 us (12%)
  starting transfers between devices  18.3 us (4%)
  other arithmetic  14.1 us (3%)
    pallas_call x8, Pallas kernels, group_call(): pl.pallas_call(functools.partial(group_kernel, cp_half, scale, len(carrie...  186 us
    ppermute x11, waiting for transfers between devices, device_fn(): swap_x = lambda a: lax.ppermute(a, 'cp', x_perm)  133 us
    unnamed x116, local copies, waits for them, and re-layouts  29.1 us
    pallas_call x4, Pallas kernels, join_call(): pl.pallas_call(functools.partial(join_kernel, n_parts), grid_spec=pltpu.P...  23.5 us
    pallas_call x1, Pallas kernels, dc_call(): pl.pallas_call(functools.partial(dc_kernel, order), grid_spec=pltpu.Prefe...  21 us
  transfers between devices with their start and end apart: 38, of which 10 were waited for; matrix products, arithmetic and copies ran while one was open for 11% of the time, Pallas kernels for 25%

commit v1 on v0

--- a/solution.py
+++ b/solution.py
@@ -33,7 +33,7 @@
     return pltpu.CompilerParams(dimension_semantics=("arbitrary",), vmem_limit_bytes=mib * 2 ** 20)
 
 
-def head_body(lens, scale, c_ref, ct_ref, w_s, wt_s, k_s, kt_s, v_s, vt_s, qt_s, do_s, s_s, p_s, ds_s,
+def head_body(lens, scale, c_ref, ct_ref, w_s, k_s, kt_s, v_s, vt_s, qt_s, do_s, s_s, p_s, ds_s,
               o_s, dqt_s, dw_ref, dkv_ref, dr_ref):
     n_max = max(lens)
     n_rows = n_max * PIECE
@@ -43,12 +43,12 @@
         kv = dot(c_ref[rows(j, 2), :], w_s[...]).astype(BF16)
         k_s[rows(j, 2), 0:d_n] = kv[:, :d_n]
         v_s[rows(j, 2), :] = kv[:, d_n:]
-        kv_t = dot(wt_s[...], ct_ref[:, rows(j, 2)]).astype(BF16)
-        kt_s[0:d_n, rows(j, 2)] = kv_t[:d_n]
-        vt_s[:, rows(j, 2)] = kv_t[d_n:]
+        kt_s[0:d_n, rows(j, 2)] = kv[:, :d_n].T
+        vt_s[:, rows(j, 2)] = kv[:, d_n:].T
     key_i = lax.broadcasted_iota(jnp.int32, (PIECE, PIECE), 0)
     qry_i = lax.broadcasted_iota(jnp.int32, (PIECE, PIECE), 1)
     for b, n in enumerate(lens):
+        base = sum(lens[:b])
         qt_b = qt_s[:, rows(b)]
         do_t = do_s[rows(b), :].T
         top8 = jnp.full((8, PIECE), NEG_BIG, F32)
@@ -56,14 +56,14 @@
             s = dot(k_s[rows(j), :], qt_b)
             if j == n - 1:
                 s = jnp.where(key_i <= qry_i, s, NEG_BIG)
-            s_s[rows(j), :] = s
+            s_s[rows(base + j), :] = s
             top8 = jnp.maximum(top8, jnp.max(s.reshape(PIECE // 8, 8, PIECE), axis=0))
         top = jnp.max(top8, axis=0, keepdims=True) * to_log2
         sum8 = jnp.zeros((8, PIECE), F32)
         for j in range(n):
-            p = jnp.exp2(s_s[rows(j), :] * to_log2 - top)
+            p = jnp.exp2(s_s[rows(base + j), :] * to_log2 - top)
             sum8 = sum8 + jnp.sum(p.reshape(PIECE // 8, 8, PIECE), axis=0)
-            s_s[rows(j), :] = p
+            s_s[rows(base + j), :] = p
             p_s[rows(j), rows(b)] = p.astype(BF16)
         inv = 1.0 / jnp.sum(sum8, axis=0, keepdims=True)
         o_t = dot(vt_s[:, 0:n * PIECE], p_s[0:n * PIECE, rows(b)]) * inv
@@ -71,7 +71,7 @@
         d_dot = jnp.sum(o_t * do_t.astype(F32), axis=0, keepdims=True)
         for j in range(n):
             dp = dot(v_s[rows(j), :], do_t)
-            p = s_s[rows(j), :] * inv
+            p = s_s[rows(base + j), :] * inv
             p_s[rows(j), rows(b)] = p.astype(BF16)
             ds_s[rows(j), rows(b)] = (p * (dp - d_dot)).astype(BF16)
         dqt_s[:, rows(b)] = dot(kt_s[:, 0:n * PIECE], ds_s[0:n * PIECE, rows(b)]) * scale
@@ -89,7 +89,7 @@
 
 def group_kernel(cp_half, scale, n_alias, idx_ref, c_ref, ct_ref, r_ref, rt_ref, wk_ref, wv_ref, q_own, q_oth, do_own, do_oth, *rest):
     (o_own, o_oth, dq_own, dq_oth, dkv_ref, dw_ref, dr_ref,
-     w_s, wt_s, k_s, kt_s, v_s, vt_s, qt_s, do_s, s_s, p_s, ds_s, o_s, dqt_s) = rest[n_alias:]
+     w_s, k_s, kt_s, v_s, vt_s, qt_s, do_s, s_s, p_s, ds_s, o_s, dqt_s) = rest[n_alias:]
     d_n = v_s.shape[1]
     core = idx_ref[1]
 
@@ -101,8 +101,6 @@
 
     w_s[:, 0:d_n] = wk_ref[0]
     w_s[:, d_n:] = wv_ref[0]
-    wt_s[0:d_n, :] = wk_ref[0].T
-    wt_s[d_n:, :] = wv_ref[0].T
 
     def at(i):
         return pl.ds(pl.multiple_of(i * PIECE, PIECE), PIECE)
@@ -118,7 +116,7 @@
         dev_a, dev_b = 2 * chip, 2 * chip + 1
         lens = (n_pieces - dev_a, n_pieces - dev_b, dev_b + 1, dev_a + 1)
         pl.when(idx_ref[0] == chip)(functools.partial(
-            head_body, lens, scale, c_ref, ct_ref, w_s, wt_s, k_s, kt_s, v_s, vt_s, qt_s, do_s, s_s, p_s, ds_s,
+            head_body, lens, scale, c_ref, ct_ref, w_s, k_s, kt_s, v_s, vt_s, qt_s, do_s, s_s, p_s, ds_s,
             o_s, dqt_s, dw_ref, dkv_ref, dr_ref))
     for pos, half, o_ref, dq_ref in ((own_lo, lo, o_own, dq_own), (own_hi, hi, o_own, dq_own),
                                      (oth_lo, lo, o_oth, dq_oth), (oth_hi, hi, o_oth, dq_oth)):
@@ -135,7 +133,7 @@
     half_heads, d_qk, tok = q_oth.shape
     d_v = do_oth.shape[2]
     kv = w_k.shape[2] + w_v.shape[2]
-    whole = lambda *shape: pl.BlockSpec(shape, lambda h, idx: (0,) * len(shape))
+    whole = lambda *shape: pl.BlockSpec(shape, lambda h, idx: (0,) * len(shape), pipeline_mode=pl.Buffered(1))
     mine = lambda *shape: pl.BlockSpec((1,) + shape, lambda h, idx: (idx[1] * half_heads + idx[2] + h, 0, 0))
     part = lambda *shape: pl.BlockSpec((1,) + shape, lambda h, idx: (idx[2] + h, 0, 0))
     in_specs = [whole(seq, rank), whole(rank, seq), whole(seq, d_r), whole(d_r, seq),
@@ -143,7 +141,7 @@
     out_specs = [mine(tok, d_v), part(tok, d_v), mine(d_qk, tok), part(d_qk, tok),
                  pl.BlockSpec((seq, kv), lambda h, idx: (0, idx[2] + h)),
                  pl.BlockSpec((1, rank, kv), lambda h, idx: (h, 0, 0)),
-                 whole(seq, d_r)]
+                 pl.BlockSpec((seq, d_r), lambda h, idx: (0, 0))]
     out_shape = [sds((2 * half_heads, tok, d_v), BF16), sds((half_heads, tok, d_v), BF16),
                  sds((2 * half_heads, d_qk, tok), F32), sds((half_heads, d_qk, tok), F32),
                  sds((seq, half_heads * kv), BF16), sds((count, rank, kv), F32), sds((seq, d_r), F32)]
@@ -160,62 +158,67 @@
         grid_spec=pltpu.PrefetchScalarGridSpec(
             num_scalar_prefetch=1, grid=(count,), in_specs=in_specs, out_specs=out_specs,
             scratch_shapes=[
-                pltpu.VMEM((rank, kv), BF16), pltpu.VMEM((kv, rank), BF16),
+                pltpu.VMEM((rank, kv), BF16),
                 pltpu.VMEM((seq, d_qk), BF16), pltpu.VMEM((d_qk, seq), BF16),
                 pltpu.VMEM((seq, d_v), BF16), pltpu.VMEM((d_v, seq), BF16),
                 pltpu.VMEM((d_qk, 2 * tok), BF16), pltpu.VMEM((2 * tok, d_v), BF16),
-                pltpu.VMEM((seq, PIECE), F32),
+                pltpu.VMEM((seq * 2 + 2 * PIECE, PIECE), F32),
                 pltpu.VMEM((seq, 2 * tok), BF16), pltpu.VMEM((seq, 2 * tok), BF16),
                 pltpu.VMEM((2 * tok, d_v), BF16), pltpu.VMEM((d_qk, 2 * tok), F32)]),
         out_shape=out_shape,
         input_output_aliases=aliases,
-        compiler_params=params(48),
+        compiler_params=params(60),
         cost_estimate=pl.CostEstimate(flops=int(flops), bytes_accessed=count * 4 * 2 ** 20, transcendentals=count * pairs),
         name="heads",
     )(*args)
 
 
-def dc_kernel(order, idx_ref, dkv_ref, wk_ref, wv_ref, dr_ref, out_ref, acc_s, w_s):
-    rank, d_n = wk_ref.shape[1:]
-    w_s[:, 0:d_n] = wk_ref[0]
-    w_s[:, d_n:] = wv_ref[0]
+def dc_kernel(order, idx_ref, dkv_ref, wk_ref, wv_ref, *rest):
+    out_ref, acc_s, w_s = rest[-3:]
+    heads, cols, d_n = wk_ref.shape
+    for g in range(heads):
+        w_s[:, 2 * g * d_n:(2 * g + 1) * d_n] = wk_ref[g]
+        w_s[:, (2 * g + 1) * d_n:(2 * g + 2) * d_n] = wv_ref[g]
     h = pl.program_id(0)
 
     @pl.when(h == 0)
     def _():
         acc_s[...] = jnp.zeros(acc_s.shape, F32)
 
-    for j in range(len(order)):
-        acc_s[rows(j), :] += dot_t(dkv_ref[rows(j), :], w_s[...])
+    for j in range(0, len(order), 2):
+        acc_s[rows(j, 2), :] += dot_t(dkv_ref[rows(j, 2), :], w_s[...])
 
     @pl.when(h == pl.num_programs(0) - 1)
     def _():
         for slot, piece in enumerate(order):
-            out_ref[slot, :, 0:rank] = acc_s[rows(piece), :]
-            dr = dr_ref[rows(piece), :]
-            out_ref[slot, :, rank:] = jnp.concatenate([dr, jnp.zeros_like(dr)], axis=1)
-
-
-def dc_call(idx, dkv, w_k, w_v, dr, order):
-    seq, d_r = dr.shape
+            out_ref[slot, :, 0:cols] = acc_s[rows(piece), :]
+            if len(rest) == 4:
+                dr = rest[0][rows(piece), :]
+                out_ref[slot, :, cols:] = jnp.concatenate([dr, jnp.zeros_like(dr)], axis=1)
+
+
+def dc_call(half, idx, dkv, w_k, w_v, extra, order):
+    seq = dkv.shape[0]
     half_heads = w_k.shape[0] // 2
     rank, d_n = w_k.shape[1:]
     kv = d_n + w_v.shape[2]
-    mine = lambda *shape: pl.BlockSpec((1,) + shape, lambda h, idx: (idx[1] * half_heads + h, 0, 0))
-    shape = (len(order), PIECE, rank + 2 * d_r)
+    step = 2
+    n_steps = half_heads // step
+    w_spec = pl.BlockSpec((step, rank // 2, d_n), lambda h, idx: (idx[1] * n_steps + h, half, 0))
+    shape = (len(order), PIECE, rank // 2 + sum(2 * e.shape[1] for e in extra))
     return pl.pallas_call(
         functools.partial(dc_kernel, order),
         grid_spec=pltpu.PrefetchScalarGridSpec(
-            num_scalar_prefetch=1, grid=(half_heads,),
-            in_specs=[pl.BlockSpec((seq, kv), lambda h, idx: (0, h)), mine(rank, d_n), mine(rank, d_n),
-                      pl.BlockSpec((seq, d_r), lambda h, idx: (0, 0))],
+            num_scalar_prefetch=1, grid=(n_steps,),
+            in_specs=[pl.BlockSpec((seq, step * kv), lambda h, idx: (0, h)), w_spec, w_spec]
+            + [pl.BlockSpec(e.shape, lambda h, idx: (0, 0)) for e in extra],
             out_specs=pl.BlockSpec(shape, lambda h, idx: (0, 0, 0)),
-            scratch_shapes=[pltpu.VMEM((seq, rank), F32), pltpu.VMEM((rank, kv), BF16)]),
+            scratch_shapes=[pltpu.VMEM((seq, rank // 2), F32), pltpu.VMEM((rank // 2, step * kv), BF16)]),
         out_shape=sds(shape, F32),
-        compiler_params=params(40),
-        cost_estimate=pl.CostEstimate(flops=2 * seq * rank * kv * half_heads, bytes_accessed=30 * 2 ** 20, transcendentals=0),
+        compiler_params=params(60),
+        cost_estimate=pl.CostEstimate(flops=seq * rank * kv * half_heads, bytes_accessed=25 * 2 ** 20, transcendentals=0),
         name="dc",
-    )(idx, dkv, w_k, w_v, dr)
+    )(idx, dkv, w_k, w_v, *extra)
 
 
 def place_kernel(idx_ref, part_ref, full_ref, out_ref):
@@ -332,30 +335,34 @@
 
         order = [piece for c in range(2) for x in range(cp_half)
                  for piece in (2 * x + c, 2 * n_cp - 1 - 2 * x - c)]
-        by_dev = dc_call(idx, dkv, w_k, w_v, dr, order).reshape(2, cp_half, 2, PIECE, -1)
-        dq = place_call(idx, swap_core(dq_oth), dq_full, 4).transpose(2, 0, 1)
-        out = place_call(idx, swap_core(o_oth), o_full, 8).transpose(1, 0, 2)
 
         def fold(arr, axis, pos, swap):
             keep = lax.dynamic_index_in_dim(arr, pos, axis, keepdims=False)
             send = lax.dynamic_index_in_dim(arr, 1 - pos, axis, keepdims=False)
             return keep + swap(send)
 
-        part = fold(by_dev, 0, core, swap_core)
-        part = fold(part, 1, my_tp, swap_tp)
-        part = fold(part, 0, chip, swap_x)
-        mate = swap_tp(part)
-        full = jnp.where(my_tp == 0, jnp.concatenate([part, mate], axis=0), jnp.concatenate([mate, part], axis=0))
+        full = []
+        for half, extra in ((0, ()), (1, (dr,))):
+            part = dc_call(half, idx, dkv, w_k, w_v, extra, order).reshape(2, cp_half, 2, PIECE, -1)
+            part = fold(part, 0, core, swap_core)
+            part = fold(part, 1, my_tp, swap_tp)
+            part = fold(part, 0, chip, swap_x)
+            mate = swap_tp(part)
+            full.append(jnp.where(my_tp == 0, jnp.concatenate([part, mate], axis=0), jnp.concatenate([mate, part], axis=0)))
+        dc = jnp.concatenate([full[0], full[1][:, :rank // 2]], axis=1)
+        dr_out = full[1][:, rank // 2:rank // 2 + d_r]
 
         n_batch = half_heads // BATCH
         per = BATCH // GROUP
         dws = ()
         for i in range(n_batch):
             sel = slice(i * per, (i + 1) * per)
-            for side, (a, b) in ((core, (own, far)), (1 - core, (near, far_near))):
+            for side, a, b in ((core, own, far), (1 - core, near, far_near)):
                 block = (side * n_batch + i).reshape(1).astype(jnp.int32)
                 dws = join_call(block, a[sel], b[sel], dws, n_heads)
-        return (out, dq, full[:, :rank], full[:, rank:rank + d_r], *dws)
+        dq = place_call(idx, swap_core(dq_oth), dq_full, 4).transpose(2, 0, 1)
+        out = place_call(idx, swap_core(o_oth), o_full, 8).transpose(1, 0, 2)
+        return (out, dq, dc, dr_out, *dws)
 
     return jax.shard_map(device_fn, mesh=mesh,
                          in_specs=(seq_spec, seq_spec, head_spec, head_spec, weight_spec, weight_spec),

time: 473 us -> 514 us (1.087)
  waiting for transfers between devices: 139 us -> 174 us
    ppermute x11 -> x12, waiting for transfers between devices: 133 us -> 165 us  [device_fn(): swap_x = lambda a: lax.ppermute(a, 'cp', x_perm)]
    pallas_call x1 -> x2, Pallas kernels: 21 us -> 27.5 us  [dc_call(): pl.pallas_call(functools.partial(dc_kernel, order), grid_spec=pltpu.Prefe...]
    unnamed x116 -> x94, local copies, waits for them, and re-layouts: 29.1 us -> 23.4 us
  transfers between devices with their start and end apart: 38 -> 42, of which waited for: 10 -> 15; matrix products, arithmetic and copies ran while one was open for 11% -> 11% of each run, Pallas kernels for 25% -> 8%
where the time goes in v1:
time: 514 us; the launch traced here: 508 us
  Pallas kernels  242 us (47%)
  waiting for transfers between devices  174 us (34%)
  local copies, waits for them, and re-layouts  55.9 us (11%)
  starting transfers between devices  19.1 us (4%)
  other arithmetic  15.2 us (3%)
    pallas_call x8, Pallas kernels, group_call(): pl.pallas_call(functools.partial(group_kernel, cp_half, scale, len(carrie...  183 us
    ppermute x12, waiting for transfers between devices, device_fn(): swap_x = lambda a: lax.ppermute(a, 'cp', x_perm)  165 us
    pallas_call x2, Pallas kernels, dc_call(): pl.pallas_call(functools.partial(dc_kernel, order), grid_spec=pltpu.Prefe...  27.5 us
    pallas_call x4, Pallas kernels, join_call(): pl.pallas_call(functools.partial(join_kernel, n_parts), grid_spec=pltpu.P...  24.3 us
    unnamed x94, local copies, waits for them, and re-layouts  23.4 us
  transfers between devices with their start and end apart: 42, of which 15 were waited for; matrix products, arithmetic and copies ran while one was open for 11% of the time, Pallas kernels for 8%

profile of v1, /device:TPU:0, one launch (start us, length us, event | category | flops | bytes accessed | tf_op | source)
XLA Modules:
  0.0 508.2 jit_solution(9541530096620417797)
XLA Ops:
  0.6 1.3 copy.56
  2.7 2.5 collective-permute-start.1
  5.7 3.8 dynamic-slice_bitcast_fusion
  9.6 5.8 %copy.89 = bf16[512,32,128]{2,0,1:T(8,128)(2,1)} copy(bf16[512,32,128]{2,1,0:T(8,128)(2,1)} %param.9) | data formatting | bytes 8388608 | tf_op args[3]
  15.4 7.9 %copy_bitcast_fusion = (bf16[32,512,128]{2,1,0:T(8,128)(2,1)}, bf16[32,512,128]{2,1,0:T(8,128)(2,1)}) fusion(bf16[512,32,128]{2,1,0:T(8,128)(2,1)} %param.11, bf16[512,32,128]{2,1,0:T(8,128)(2,1)} %param.10), kind=kLoop, calls=%fused_computation | loop fusion | bytes 16777216 | tf_op jit(solution)/shard_map/transpose | solution.py:314
  24.6 1.5 dynamic-slice_bitcast_fusion.1
  28.0 1.0 copy.78.r_ref
  29.1 3.3 collective-permute-done.2
  33.3 1.5 select_dynamic-update-slice_fusion
  34.9 2.6 copy.77.c_ref
  37.6 23.1 %heads.8 = (bf16[32,512,128]{2,1,0:T(8,128)(2,1)}, bf16[16,512,128]{2,1,0:T(8,128)(2,1)}, f32[32,192,512]{2,1,0:T(8,128)}, f32[16,192,512]{2,1,0:T(8,128)}, bf16...) custom-call(s32[3]{0:T(128)} %get-tuple-element.140.idx_ref, bf16[2048,512]{1,0:T(8,128)(2,1)} %copy.77.c_ref, ...), custom_call_target="tpu_custom_call" | custom-call | flops 7751073792 | bytes 8388608 | tf_op jit(solution)/shard_map/heads/pallas_call | solution.py:156
  60.7 22.8 %heads.9 = (bf16[32,512,128]{2,1,0:T(8,128)(2,1)}, bf16[16,512,128]{2,1,0:T(8,128)(2,1)}, f32[32,192,512]{2,1,0:T(8,128)}, f32[16,192,512]{2,1,0:T(8,128)}, bf16...) custom-call(s32[3]{0:T(128)} %get-tuple-element.154.idx_ref, ...), custom_call_target="tpu_custom_call", output_to_operand_aliasing={{0}: (11, {}), {1}: (12, {}), {2}: (13, {}), {3}: (14, {}),... | custom-call | flops 7751073792 | bytes 8388608 | tf_op jit(solution)/shard_map/heads/pallas_call | solution.py:156
  83.5 23.0 %heads.10 = (bf16[32,512,128]{2,1,0:T(8,128)(2,1)}, bf16[16,512,128]{2,1,0:T(8,128)(2,1)}, f32[32,192,512]{2,1,0:T(8,128)}, f32[16,192,512]{2,1,0:T(8,128)}, bf1...) custom-call(s32[3]{0:T(128)} %get-tuple-element.155.idx_ref, ...), custom_call_target="tpu_custom_call", output_to_operand_aliasing={{0}: (11, {}), {1}: (12, {}), {2}: (13, {}), {3}: (14, {}),... | custom-call | flops 7751073792 | bytes 8388608 | tf_op jit(solution)/shard_map/heads/pallas_call | solution.py:156
  106.5 22.8 %heads.11 = (bf16[32,512,128]{2,1,0:T(8,128)(2,1)}, bf16[16,512,128]{2,1,0:T(8,128)(2,1)}, f32[32,192,512]{2,1,0:T(8,128)}, f32[16,192,512]{2,1,0:T(8,128)}, bf1...) custom-call(s32[3]{0:T(128)} %get-tuple-element.156.idx_ref, ...), custom_call_target="tpu_custom_call", output_to_operand_aliasing={{0}: (11, {}), {1}: (12, {}), {2}: (13, {}), {3}: (14, {}),... | custom-call | flops 7751073792 | bytes 8388608 | tf_op jit(solution)/shard_map/heads/pallas_call | solution.py:156
  129.3 23.0 %heads.12 = (bf16[32,512,128]{2,1,0:T(8,128)(2,1)}, bf16[16,512,128]{2,1,0:T(8,128)(2,1)}, f32[32,192,512]{2,1,0:T(8,128)}, f32[16,192,512]{2,1,0:T(8,128)}, bf1...) custom-call(s32[3]{0:T(128)} %get-tuple-element.157.idx_ref, ...), custom_call_target="tpu_custom_call", output_to_operand_aliasing={{0}: (11, {}), {1}: (12, {}), {2}: (13, {}), {3}: (14, {}),... | custom-call | flops 7751073792 | bytes 8388608 | tf_op jit(solution)/shard_map/heads/pallas_call | solution.py:156
  152.3 22.8 %heads.13 = (bf16[32,512,128]{2,1,0:T(8,128)(2,1)}, bf16[16,512,128]{2,1,0:T(8,128)(2,1)}, f32[32,192,512]{2,1,0:T(8,128)}, f32[16,192,512]{2,1,0:T(8,128)}, bf1...) custom-call(s32[3]{0:T(128)} %get-tuple-element.158.idx_ref, ...), custom_call_target="tpu_custom_call", output_to_operand_aliasing={{0}: (11, {}), {1}: (12, {}), {2}: (13, {}), {3}: (14, {}),... | custom-call | flops 7751073792 | bytes 8388608 | tf_op jit(solution)/shard_map/heads/pallas_call | solution.py:156
  175.1 23.0 %heads.14 = (bf16[32,512,128]{2,1,0:T(8,128)(2,1)}, bf16[16,512,128]{2,1,0:T(8,128)(2,1)}, f32[32,192,512]{2,1,0:T(8,128)}, f32[16,192,512]{2,1,0:T(8,128)}, bf1...) custom-call(s32[3]{0:T(128)} %get-tuple-element.159.idx_ref, ...), custom_call_target="tpu_custom_call", output_to_operand_aliasing={{0}: (11, {}), {1}: (12, {}), {2}: (13, {}), {3}: (14, {}),... | custom-call | flops 7751073792 | bytes 8388608 | tf_op jit(solution)/shard_map/heads/pallas_call | solution.py:156
  198.1 23.0 %heads.15 = (bf16[32,512,128]{2,1,0:T(8,128)(2,1)}, bf16[16,512,128]{2,1,0:T(8,128)(2,1)}, f32[32,192,512]{2,1,0:T(8,128)}, f32[16,192,512]{2,1,0:T(8,128)}, bf1...) custom-call(s32[3]{0:T(128)} %get-tuple-element.160.idx_ref, ...), custom_call_target="tpu_custom_call", output_to_operand_aliasing={{0}: (11, {}), {1}: (12, {}), {2}: (13, {}), {3}: (14, {}),... | custom-call | flops 7751073792 | bytes 8388608 | tf_op jit(solution)/shard_map/heads/pallas_call | solution.py:156
  221.1 13.5 %dc.2 = f32[8,256,256]{2,1,0:T(8,128)} custom-call(s32[2]{0:T(128)} %pad_add_fusion.idx_ref, bf16[2048,4096]{1,0:T(8,128)(2,1)} %get-tuple-element.109.dkv_ref, bf16[32,512,128]{2,1,0:T(8,128)(2,1)} %get-tuple-element.162.wk_ref, bf16[32,512,128]{2,1,0:T(8,128)(2,1)} %get-tuple-element.161.wv_ref), custom_call_target="tpu_custom_call" | custom-call | flops 4294967296 | bytes 26214400 | tf_op jit(solution)/shard_map/dc/pallas_call | solution.py:209
  234.6 1.3 dynamic-slice_bitcast_fusion.3
  237.0 1.7 collective-permute-done.10
  238.7 1.4 collective-permute-done.18.refs_0_
  241.7 1.0 copy-done.12
  242.7 1.4 collective-permute-start.26
  244.0 1.0 copy-done.14
  246.7 18.1 %collective-permute-done.22.refs_4_ = f32[2,512,256]{2,1,0:T(8,128)S(1)} collective-permute-done((f32[2,512,256]{2,1,0:T(8,128)S(1)}, f32[2,512,256]{2,1,0:T(8,128)S(1)}, u32[]{:S(2)}, u32[]{:S(2)}) %collective-permute-start.22) | collective-permute-done | bytes 1048608 | tf_op jit(solution)/shard_map/ppermute | solution.py:297
  264.7 22.5 %collective-permute-done.24.refs_5_ = f32[2,512,256]{2,1,0:T(8,128)S(1)} collective-permute-done((f32[2,512,256]{2,1,0:T(8,128)S(1)}, f32[2,512,256]{2,1,0:T(8,128)S(1)}, u32[]{:S(2)}, u32[]{:S(2)}) %collective-permute-start.24) | collective-permute-done | bytes 1048608 | tf_op jit(solution)/shard_map/ppermute | solution.py:297
  287.2 22.5 %collective-permute-done.26.refs_6_ = f32[2,512,256]{2,1,0:T(8,128)S(1)} collective-permute-done((f32[2,512,256]{2,1,0:T(8,128)}, f32[2,512,256]{2,1,0:T(8,128)S(1)}, u32[]{:S(2)}, u32[]{:S(2)}) %collective-permute-start.26) | collective-permute-done | bytes 1048608 | tf_op jit(solution)/shard_map/ppermute | solution.py:297
  309.7 1.0 copy-done.22
  310.6 4.8 add_add_fusion.rest_0_
  315.5 15.8 %collective-permute-done.28.refs_7_ = f32[2,512,256]{2,1,0:T(8,128)S(1)} collective-permute-done((f32[2,512,256]{2,1,0:T(8,128)}, f32[2,512,256]{2,1,0:T(8,128)S(1)}, u32[]{:S(2)}, u32[]{:S(2)}) %collective-permute-start.28) | collective-permute-done | bytes 1048608 | tf_op jit(solution)/shard_map/ppermute | solution.py:297
  331.3 1.0 copy-done.24
  332.3 14.0 %dc.3 = f32[8,256,384]{2,1,0:T(8,128)} custom-call(s32[2]{0:T(128)} %pad_add_fusion.idx_ref, bf16[2048,4096]{1,0:T(8,128)(2,1)} %get-tuple-element.109.dkv_ref, bf16[32,512,128]{2,1,0:T(8,128)(2,1)} %get-tuple-element.162.wk_ref, bf16[32,512,128]{2,1,0:T(8,128)(2,1)} %get-tuple-element.161.wv_ref, f32[2048,64]{1,0:T(8,128)} %add_add_fusion.rest_0_), custom_call_target="tpu_custom_call" | custom-call | flops 4294967296 | bytes 26214400 | tf_op jit(solution)/shard_map/dc/pallas_call | solution.py:209
  346.3 2.7 dynamic-slice_bitcast_fusion.2
  349.7 1.7 collective-permute-start.36
  351.5 24.3 %collective-permute-done.34.refs_4_ = f32[2,512,256]{2,1,0:T(8,128)} collective-permute-done((f32[2,512,256]{2,1,0:T(8,128)}, f32[2,512,256]{2,1,0:T(8,128)}, u32[]{:S(2)}, u32[]{:S(2)}) %collective-permute-start.34) | collective-permute-done | bytes 1048608 | tf_op jit(solution)/shard_map/ppermute | solution.py:297
  376.1 1.7 bitcast_add_fusion.1
  377.8 20.5 %collective-permute-done.36.refs_5_ = f32[2,512,256]{2,1,0:T(8,128)} collective-permute-done((f32[2,512,256]{2,1,0:T(8,128)}, f32[2,512,256]{2,1,0:T(8,128)}, u32[]{:S(2)}, u32[]{:S(2)}) %collective-permute-start.36) | collective-permute-done | bytes 1048608 | tf_op jit(solution)/shard_map/ppermute | solution.py:297
  398.6 1.1 constant_dynamic-slice_fusion.3
  399.6 2.0 copy.80
  401.6 1.8 collective-permute-start.11
  403.4 2.0 copy.79
  405.5 2.0 bitcast_add_fusion
  407.5 1.3 constant_dynamic-slice_fusion.1
  408.8 2.3 copy.82
  411.0 2.7 collective-permute-done.11
  413.8 1.7 collective-permute-start.15
  415.5 1.3 bitcast_add_fusion.3
  416.8 3.9 collective-permute-done.38.refs_6_
  421.0 22.2 %collective-permute-done.40.refs_7_ = f32[2,512,256]{2,1,0:T(8,128)} collective-permute-done((f32[2,512,256]{2,1,0:T(8,128)}, f32[2,512,256]{2,1,0:T(8,128)}, u32[]{:S(2)}, u32[]{:S(2)}) %collective-permute-start.40) | collective-permute-done | bytes 1048608 | tf_op jit(solution)/shard_map/ppermute | solution.py:297
  443.2 4.6 collective-permute-done.12
  448.5 2.3 copy.81
  450.8 1.5 bitcast_add_fusion.2
  454.3 10.5 %collective-permute-done.16 = f32[256,384]{0,1:T(8,128)S(1)} collective-permute-done((f32[256,384]{0,1:T(8,128)S(1)}, f32[256,384]{0,1:T(8,128)S(1)}, u32[]{:S(2)}, u32[]{:S(2)}) %collective-permute-start.16) | collective-permute-done | bytes 393248 | tf_op jit(solution)/shard_map/ppermute | solution.py:297
  464.8 1.2 copy-done.5
  466.0 1.2 copy-done.8
  467.2 6.7 %join.4 = (f32[512,32,128]{2,1,0:T(8,128)}, f32[512,32,128]{2,1,0:T(8,128)}) custom-call(s32[1]{0:T(128)} %bitcast.30.idx_ref, f32[2,512,256]{2,1,0:T(8,128)} %get-tuple-element.122.refs_0_, f32[2,512,256]{2,1,0:T(8,128)} %get-tuple-element.123.refs_1_, f32[2,512,256]{2,1,0:T(8,128)S(1)} %copy-done.5, f32[2,512,256]{2,1,0:T(8,128)S(1)} %copy-done.8, ...), custom_call_target="tpu_custom_call" | custom-call | flops 1000000000 | bytes 12582912 | tf_op jit(solution)/shard_map/join/pallas_call | solution.py:262
  474.8 4.7 copy.83
  479.5 1.8 collective-permute-start.13
  481.6 7.5 %join.5 = (f32[512,32,128]{2,1,0:T(8,128)}, f32[512,32,128]{2,1,0:T(8,128)}) custom-call(s32[1]{0:T(128)} %bitcast.29.idx_ref, f32[2,512,256]{2,1,0:T(8,128)} %collective-permute-done.30.refs_0_, f32[2,512,256]{2,1,0:T(8,128)} %collective-permute-done.31.refs_1_, ...), custom_call_target="tpu_custom_call", output_to_operand_aliasing={{0}: (9, {}), {1}: (10, {})} | custom-call | flops 1000000000 | bytes 12582912 | tf_op jit(solution)/shard_map/join/pallas_call | solution.py:262
  489.3 4.2 join.6
  493.5 5.8 %join.7 = (f32[512,32,128]{2,1,0:T(8,128)}, f32[512,32,128]{2,1,0:T(8,128)}) custom-call(s32[1]{0:T(128)} %bitcast.27.idx_ref, f32[2,512,256]{2,1,0:T(8,128)S(1)} %copy-done.11, f32[2,512,256]{2,1,0:T(8,128)S(1)} %copy-done.13, f32[2,512,256]{2,1,0:T(8,128)S(1)} %copy-done.15, ...), custom_call_target="tpu_custom_call", output_to_operand_aliasing={{0}: (9, {}), {1}: (10, {})} | custom-call | flops 1000000000 | bytes 12582912 | tf_op jit(solution)/shard_map/join/pallas_call | solution.py:262
  500.2 1.3 copy.84
  501.5 6.5 %place.3 = f32[32,192,512]{2,1,0:T(8,128)} custom-call(s32[2]{0:T(128)S(1)} %copy-done.26, f32[16,192,512]{2,1,0:T(8,128)} %collective-permute-done.9.part_ref, f32[32,192,512]{2,1,0:T(8,128)} %get-tuple-element.108.full_ref), custom_call_target="tpu_custom_call", output_to_operand_aliasing={{}: (2, {})} | custom-call | flops 1000000000 | bytes 12582912 | tf_op jit(solution)/shard_map/place/pallas_call | solution.py:230
  (166 shorter events, 16.4 us)
Async XLA Ops:
  1.9 27.2 %collective-permute-start = (bf16[512,512]{0,1:T(8,128)(2,1)S(1)}, bf16[512,512]{0,1:T(8,128)(2,1)S(1)}, u32[]{:S(2)}, u32[]{:S(2)}) collective-permute-start(bf16[512,512]{0,1:T(8,128)(2,1)S(1)} %copy.56), channel_id=1, source_target_pairs={{0,1},{1,0},{2,3},{3,2},{4,5},{5,4},{6,7},{7,6}} | collective-permute-start | bytes 1572872 | tf_op jit(solution)/shard_map/ppermute | solution.py:298
  2.7 24.9 %collective-permute-start.1 = (bf16[512,512]{0,1:T(8,128)(2,1)S(1)}, bf16[512,512]{0,1:T(8,128)(2,1)S(1)}, u32[]{:S(2)}, u32[]{:S(2)}) collective-permute-start(bf16[512,512]{0,1:T(8,128)(2,1)S(1)} %copy.56), channel_id=1, source_target_pairs={{0,2},{1,3},{2,0},{3,1},{4,6},{5,7},{6,4},{7,5}} | collective-permute-start | bytes 1572872 | tf_op jit(solution)/shard_map/ppermute | solution.py:297
  5.3 22.0 %collective-permute-start.3 = (bf16[64,512]{1,0:T(8,128)(2,1)}, bf16[64,512]{1,0:T(8,128)(2,1)S(1)}, u32[]{:S(2)}, u32[]{:S(2)}) collective-permute-start(bf16[64,512]{1,0:T(8,128)(2,1)} %bitcast.83), channel_id=1, source_target_pairs={{0,1},{1,0},{2,3},{3,2},{4,5},{5,4},{6,7},{7,6}} | collective-permute-start | bytes 196616 | tf_op jit(solution)/shard_map/ppermute | solution.py:298
  5.4 20.7 %collective-permute-start.4 = (bf16[64,512]{1,0:T(8,128)(2,1)}, bf16[64,512]{1,0:T(8,128)(2,1)S(1)}, u32[]{:S(2)}, u32[]{:S(2)}) collective-permute-start(bf16[64,512]{1,0:T(8,128)(2,1)} %bitcast.84), channel_id=1, source_target_pairs={{0,2},{1,3},{2,0},{3,1},{4,6},{5,7},{6,4},{7,5}} | collective-permute-start | bytes 196616 | tf_op jit(solution)/shard_map/ppermute | solution.py:297
  9.6 28.0 %collective-permute-start.6 = (bf16[16,192,512]{2,1,0:T(8,128)(2,1)}, bf16[16,192,512]{2,1,0:T(8,128)(2,1)}, u32[]{:S(2)}, u32[]{:S(2)}) collective-permute-start(bf16[16,192,512]{2,1,0:T(8,128)(2,1)} %dynamic-slice_bitcast_fusion), channel_id=1, source_target_pairs={{0,1},{1,0},{2,3},{3,2},{4,5},{5,4},{6,7},{7,6}} | collective-permute-start | bytes 9437192 | tf_op jit(solution)/shard_map/ppermute | solution.py:298
  15.4 9.2 %copy-start.27 = (bf16[512,32,128]{2,0,1:T(8,128)(2,1)S(1)}, bf16[512,32,128]{2,0,1:T(8,128)(2,1)}, u32[]{:S(2)}) copy-start(bf16[512,32,128]{2,0,1:T(8,128)(2,1)} %copy.89) | copy-start | bytes 12582916
  26.1 1.4 collective-permute-start.5
  27.3 10.3 %collective-permute-start.7 = (bf16[16,512,128]{2,1,0:T(8,128)(2,1)}, bf16[16,512,128]{2,1,0:T(8,128)(2,1)}, u32[]{:S(2)}, u32[]{:S(2)}) collective-permute-start(bf16[16,512,128]{2,1,0:T(8,128)(2,1)} %dynamic-slice_bitcast_fusion.1), channel_id=1, source_target_pairs={{0,1},{1,0},{2,3},{3,2},{4,5},{5,4},{6,7},{7,6}} | collective-permute-start | bytes 6291464 | tf_op jit(solution)/shard_map/ppermute | solution.py:298
  27.6 4.9 copy-start.35
  27.6 4.8 collective-permute-start.2
  28.0 6.8 %copy-start.29 = (bf16[64,2048]{1,0:T(8,128)(2,1)}, bf16[64,2048]{1,0:T(8,128)(2,1)S(1)}, u32[]{:S(2)}) copy-start(bf16[64,2048]{1,0:T(8,128)(2,1)S(1)} %slice_dynamic-update-slice_fusion.6.rt_ref) | copy-start | bytes 786436
  221.0 14.9 %copy-start.1 = (f32[2,512,256]{2,1,0:T(8,128)S(1)}, f32[2,512,256]{2,1,0:T(8,128)}, u32[]{:S(2)}) copy-start(f32[2,512,256]{2,1,0:T(8,128)} %get-tuple-element.118.refs_0_) | copy-start | bytes 3145732
  221.1 15.3 %copy-start.2 = (f32[2,512,256]{2,1,0:T(8,128)S(1)}, f32[2,512,256]{2,1,0:T(8,128)}, u32[]{:S(2)}) copy-start(f32[2,512,256]{2,1,0:T(8,128)} %get-tuple-element.119.refs_1_) | copy-start | bytes 3145732
  221.1 88.6 %copy-start.4 = (f32[2,512,256]{2,1,0:T(8,128)S(1)}, f32[2,512,256]{2,1,0:T(8,128)}, u32[]{:S(2)}) copy-start(f32[2,512,256]{2,1,0:T(8,128)} %get-tuple-element.124.refs_2_) | copy-start | bytes 3145732
  235.9 2.8 collective-permute-start.10
  235.9 4.1 collective-permute-start.18
  236.4 5.3 %collective-permute-start.19 = (f32[2,512,256]{2,1,0:T(8,128)S(1)}, f32[2,512,256]{2,1,0:T(8,128)S(1)}, u32[]{:S(2)}, u32[]{:S(2)}) collective-permute-start(f32[2,512,256]{2,1,0:T(8,128)S(1)} %copy-done.2), channel_id=1, source_target_pairs={{0,1},{1,0},{2,3},{3,2},{4,5},{5,4},{6,7},{7,6}} | collective-permute-start | bytes 3145736 | tf_op jit(solution)/shard_map/ppermute | solution.py:298
  236.4 7.6 %collective-permute-start.20 = (f32[2,512,256]{2,1,0:T(8,128)}, f32[2,512,256]{2,1,0:T(8,128)S(1)}, u32[]{:S(2)}, u32[]{:S(2)}) collective-permute-start(f32[2,512,256]{2,1,0:T(8,128)} %get-tuple-element.120.refs_2_), channel_id=1, source_target_pairs={{0,1},{1,0},{2,3},{3,2},{4,5},{5,4},{6,7},{7,6}} | collective-permute-start | bytes 3145736 | tf_op jit(solution)/shard_map/ppermute | solution.py:298
  236.9 8.8 %collective-permute-start.21 = (f32[2,512,256]{2,1,0:T(8,128)}, f32[2,512,256]{2,1,0:T(8,128)S(1)}, u32[]{:S(2)}, u32[]{:S(2)}) collective-permute-start(f32[2,512,256]{2,1,0:T(8,128)} %get-tuple-element.121.refs_3_), channel_id=1, source_target_pairs={{0,1},{1,0},{2,3},{3,2},{4,5},{5,4},{6,7},{7,6}} | collective-permute-start | bytes 3145736 | tf_op jit(solution)/shard_map/ppermute | solution.py:298
  238.7 26.0 %collective-permute-start.22 = (f32[2,512,256]{2,1,0:T(8,128)S(1)}, f32[2,512,256]{2,1,0:T(8,128)S(1)}, u32[]{:S(2)}, u32[]{:S(2)}) collective-permute-start(f32[2,512,256]{2,1,0:T(8,128)S(1)} %copy-done.1), channel_id=1, source_target_pairs={{0,2},{1,3},{2,0},{3,1},{4,6},{5,7},{6,4},{7,5}} | collective-permute-start | bytes 3145736 | tf_op jit(solution)/shard_map/ppermute | solution.py:297
  241.0 46.2 %collective-permute-start.24 = (f32[2,512,256]{2,1,0:T(8,128)S(1)}, f32[2,512,256]{2,1,0:T(8,128)S(1)}, u32[]{:S(2)}, u32[]{:S(2)}) collective-permute-start(f32[2,512,256]{2,1,0:T(8,128)S(1)} %copy-done.2), channel_id=1, source_target_pairs={{0,2},{1,3},{2,0},{3,1},{4,6},{5,7},{6,4},{7,5}} | collective-permute-start | bytes 3145736 | tf_op jit(solution)/shard_map/ppermute | solution.py:297
  242.7 67.0 %collective-permute-start.26 = (f32[2,512,256]{2,1,0:T(8,128)}, f32[2,512,256]{2,1,0:T(8,128)S(1)}, u32[]{:S(2)}, u32[]{:S(2)}) collective-permute-start(f32[2,512,256]{2,1,0:T(8,128)} %get-tuple-element.120.refs_2_), channel_id=1, source_target_pairs={{0,2},{1,3},{2,0},{3,1},{4,6},{5,7},{6,4},{7,5}} | collective-permute-start | bytes 3145736 | tf_op jit(solution)/shard_map/ppermute | solution.py:297
  245.0 86.3 %collective-permute-start.28 = (f32[2,512,256]{2,1,0:T(8,128)}, f32[2,512,256]{2,1,0:T(8,128)S(1)}, u32[]{:S(2)}, u32[]{:S(2)}) collective-permute-start(f32[2,512,256]{2,1,0:T(8,128)} %get-tuple-element.121.refs_3_), channel_id=1, source_target_pairs={{0,2},{1,3},{2,0},{3,1},{4,6},{5,7},{6,4},{7,5}} | collective-permute-start | bytes 3145736 | tf_op jit(solution)/shard_map/ppermute | solution.py:297
  246.6 254.9 %collective-permute-start.9 = (f32[16,192,512]{2,1,0:T(8,128)}, f32[16,192,512]{2,1,0:T(8,128)}, u32[]{:S(2)}, u32[]{:S(2)}) collective-permute-start(f32[16,192,512]{2,1,0:T(8,128)} %get-tuple-element.107), channel_id=1, source_target_pairs={{0,1},{1,0},{2,3},{3,2},{4,5},{5,4},{6,7},{7,6}} | collective-permute-start | bytes 18874376 | tf_op jit(solution)/shard_map/ppermute | solution.py:298
  264.7 45.0 %copy-start.18 = (f32[2,512,256]{2,1,0:T(8,128)}, f32[2,512,256]{2,1,0:T(8,128)S(1)}, u32[]{:S(2)}) copy-start(f32[2,512,256]{2,1,0:T(8,128)S(1)} %collective-permute-done.22.refs_4_) | copy-start | bytes 3145732
  264.7 84.2 %collective-permute-start.30 = (f32[2,512,256]{2,1,0:T(8,128)}, f32[2,512,256]{2,1,0:T(8,128)}, u32[]{:S(2)}, u32[]{:S(2)}) collective-permute-start(f32[2,512,256]{2,1,0:T(8,128)} %get-tuple-element.122.refs_0_), channel_id=1, source_target_pairs={{0,1},{1,0},{2,3},{3,2},{4,5},{5,4},{6,7},{7,6}} | collective-permute-start | bytes 3145736 | tf_op jit(solution)/shard_map/ppermute | solution.py:298
  287.2 22.5 %copy-start.20 = (f32[2,512,256]{2,1,0:T(8,128)}, f32[2,512,256]{2,1,0:T(8,128)S(1)}, u32[]{:S(2)}) copy-start(f32[2,512,256]{2,1,0:T(8,128)S(1)} %collective-permute-done.24.refs_5_) | copy-start | bytes 3145732
  287.2 62.3 %collective-permute-start.31 = (f32[2,512,256]{2,1,0:T(8,128)}, f32[2,512,256]{2,1,0:T(8,128)}, u32[]{:S(2)}, u32[]{:S(2)}) collective-permute-start(f32[2,512,256]{2,1,0:T(8,128)} %get-tuple-element.123.refs_1_), channel_id=1, source_target_pairs={{0,1},{1,0},{2,3},{3,2},{4,5},{5,4},{6,7},{7,6}} | collective-permute-start | bytes 3145736 | tf_op jit(solution)/shard_map/ppermute | solution.py:298
  309.7 40.1 %collective-permute-start.32 = (f32[2,512,256]{2,1,0:T(8,128)S(1)}, f32[2,512,256]{2,1,0:T(8,128)}, u32[]{:S(2)}, u32[]{:S(2)}) collective-permute-start(f32[2,512,256]{2,1,0:T(8,128)S(1)} %copy-done.4), channel_id=1, source_target_pairs={{0,1},{1,0},{2,3},{3,2},{4,5},{5,4},{6,7},{7,6}} | collective-permute-start | bytes 3145736 | tf_op jit(solution)/shard_map/ppermute | solution.py:298
  310.6 21.6 %copy-start.7 = (f32[2,512,256]{2,1,0:T(8,128)S(1)}, f32[2,512,256]{2,1,0:T(8,128)}, u32[]{:S(2)}) copy-start(f32[2,512,256]{2,1,0:T(8,128)} %get-tuple-element.125.refs_3_) | copy-start | bytes 3145732
  332.3 19.2 %collective-permute-start.33 = (f32[2,512,256]{2,1,0:T(8,128)S(1)}, f32[2,512,256]{2,1,0:T(8,128)}, u32[]{:S(2)}, u32[]{:S(2)}) collective-permute-start(f32[2,512,256]{2,1,0:T(8,128)S(1)} %copy-done.7), channel_id=1, source_target_pairs={{0,1},{1,0},{2,3},{3,2},{4,5},{5,4},{6,7},{7,6}} | collective-permute-start | bytes 3145736 | tf_op jit(solution)/shard_map/ppermute | solution.py:298
  348.9 52.7 %collective-permute-start.14 = (f32[2,2,256,384]{3,2,1,0:T(8,128)}, f32[2,2,256,384]{3,2,1,0:T(8,128)}, u32[]{:S(2)}, u32[]{:S(2)}) collective-permute-start(f32[2,2,256,384]{3,2,1,0:T(8,128)} %dynamic-slice_bitcast_fusion.2), channel_id=1, source_target_pairs={{0,1},{1,0},{2,3},{3,2},{4,5},{5,4},{6,7},{7,6}} | collective-permute-start | bytes 4718600 | tf_op jit(solution)/shard_map/ppermute | solution.py:298
  349.4 26.3 %collective-permute-start.34 = (f32[2,512,256]{2,1,0:T(8,128)}, f32[2,512,256]{2,1,0:T(8,128)}, u32[]{:S(2)}, u32[]{:S(2)}) collective-permute-start(f32[2,512,256]{2,1,0:T(8,128)} %get-tuple-element.122.refs_0_), channel_id=1, source_target_pairs={{0,2},{1,3},{2,0},{3,1},{4,6},{5,7},{6,4},{7,5}} | collective-permute-start | bytes 3145736 | tf_op jit(solution)/shard_map/ppermute | solution.py:297
  349.7 48.5 %collective-permute-start.36 = (f32[2,512,256]{2,1,0:T(8,128)}, f32[2,512,256]{2,1,0:T(8,128)}, u32[]{:S(2)}, u32[]{:S(2)}) collective-permute-start(f32[2,512,256]{2,1,0:T(8,128)} %get-tuple-element.123.refs_1_), channel_id=1, source_target_pairs={{0,2},{1,3},{2,0},{3,1},{4,6},{5,7},{6,4},{7,5}} | collective-permute-start | bytes 3145736 | tf_op jit(solution)/shard_map/ppermute | solution.py:297
  351.5 96.3 %collective-permute-start.8 = (bf16[16,512,128]{2,1,0:T(8,128)(2,1)}, bf16[16,512,128]{2,1,0:T(8,128)(2,1)S(1)}, u32[]{:S(2)}, u32[]{:S(2)}) collective-permute-start(bf16[16,512,128]{2,1,0:T(8,128)(2,1)} %get-tuple-element.105), channel_id=1, source_target_pairs={{0,1},{1,0},{2,3},{3,2},{4,5},{5,4},{6,7},{7,6}} | collective-permute-start | bytes 6291464 | tf_op jit(solution)/shard_map/ppermute | solution.py:298
  375.8 44.9 %collective-permute-start.38 = (f32[2,512,256]{2,1,0:T(8,128)}, f32[2,512,256]{2,1,0:T(8,128)}, u32[]{:S(2)}, u32[]{:S(2)}) collective-permute-start(f32[2,512,256]{2,1,0:T(8,128)} %get-tuple-element.124.refs_2_), channel_id=1, source_target_pairs={{0,2},{1,3},{2,0},{3,1},{4,6},{5,7},{6,4},{7,5}} | collective-permute-start | bytes 3145736 | tf_op jit(solution)/shard_map/ppermute | solution.py:297
  398.3 44.9 %collective-permute-start.40 = (f32[2,512,256]{2,1,0:T(8,128)}, f32[2,512,256]{2,1,0:T(8,128)}, u32[]{:S(2)}, u32[]{:S(2)}) collective-permute-start(f32[2,512,256]{2,1,0:T(8,128)} %get-tuple-element.125.refs_3_), channel_id=1, source_target_pairs={{0,2},{1,3},{2,0},{3,1},{4,6},{5,7},{6,4},{7,5}} | collective-permute-start | bytes 3145736 | tf_op jit(solution)/shard_map/ppermute | solution.py:297
  401.6 12.1 %collective-permute-start.11 = (f32[2,256,256]{1,2,0:T(8,128)}, f32[2,256,256]{1,2,0:T(8,128)}, u32[]{:S(2)}, u32[]{:S(2)}) collective-permute-start(f32[2,256,256]{1,2,0:T(8,128)} %bitcast.82), channel_id=1, source_target_pairs={{0,4},{4,0},{1,5},{5,1},{2,6},{6,2},{3,7},{7,3}} | collective-permute-start | bytes 1572872 | tf_op jit(solution)/shard_map/ppermute | solution.py:299
  413.8 34.7 %collective-permute-start.15 = (f32[2,256,384]{1,2,0:T(8,128)}, f32[2,256,384]{1,2,0:T(8,128)}, u32[]{:S(2)}, u32[]{:S(2)}) collective-permute-start(f32[2,256,384]{1,2,0:T(8,128)} %bitcast.81), channel_id=1, source_target_pairs={{0,4},{4,0},{1,5},{5,1},{2,6},{6,2},{3,7},{7,3}} | collective-permute-start | bytes 2359304 | tf_op jit(solution)/shard_map/ppermute | solution.py:299
  416.8 31.0 %copy-start.32 = (f32[2,256,256]{1,2,0:T(8,128)}, f32[2,256,256]{1,2,0:T(8,128)S(1)}, u32[]{:S(2)}) copy-start(f32[2,256,256]{1,2,0:T(8,128)S(1)} %bitcast_add_fusion.3) | copy-start | bytes 1572868
  420.7 27.0 %collective-permute-start.12 = (f32[256,256]{0,1:T(8,128)S(1)}, f32[256,256]{0,1:T(8,128)S(1)}, u32[]{:S(2)}, u32[]{:S(2)}) collective-permute-start(f32[256,256]{0,1:T(8,128)S(1)} %dynamic-slice_bitcast_fusion.5), channel_id=1, source_target_pairs={{0,2},{1,3},{2,0},{3,1},{4,6},{5,7},{6,4},{7,5}} | collective-permute-start | bytes 786440 | tf_op jit(solution)/shard_map/ppermute | solution.py:297
  443.2 10.0 %collective-permute-start.23 = (f32[2,512,256]{2,1,0:T(8,128)}, f32[2,512,256]{2,1,0:T(8,128)}, u32[]{:S(2)}, u32[]{:S(2)}) collective-permute-start(f32[2,512,256]{2,1,0:T(8,128)} %copy-done.18), channel_id=1, source_target_pairs={{0,1},{1,0},{2,3},{3,2},{4,5},{5,4},{6,7},{7,6}} | collective-permute-start | bytes 3145736 | tf_op jit(solution)/shard_map/ppermute | solution.py:298
  447.8 5.7 %collective-permute-start.25 = (f32[2,512,256]{2,1,0:T(8,128)}, f32[2,512,256]{2,1,0:T(8,128)}, u32[]{:S(2)}, u32[]{:S(2)}) collective-permute-start(f32[2,512,256]{2,1,0:T(8,128)} %copy-done.20), channel_id=1, source_target_pairs={{0,1},{1,0},{2,3},{3,2},{4,5},{5,4},{6,7},{7,6}} | collective-permute-start | bytes 3145736 | tf_op jit(solution)/shard_map/ppermute | solution.py:298
  447.8 6.0 %collective-permute-start.35 = (f32[2,512,256]{2,1,0:T(8,128)}, f32[2,512,256]{2,1,0:T(8,128)}, u32[]{:S(2)}, u32[]{:S(2)}) collective-permute-start(f32[2,512,256]{2,1,0:T(8,128)} %collective-permute-done.34.refs_4_), channel_id=1, source_target_pairs={{0,1},{1,0},{2,3},{3,2},{4,5},{5,4},{6,7},{7,6}} | collective-permute-start | bytes 3145736 | tf_op jit(solution)/shard_map/ppermute | solution.py:298
  448.5 5.6 %collective-permute-start.37 = (f32[2,512,256]{2,1,0:T(8,128)}, f32[2,512,256]{2,1,0:T(8,128)}, u32[]{:S(2)}, u32[]{:S(2)}) collective-permute-start(f32[2,512,256]{2,1,0:T(8,128)} %collective-permute-done.36.refs_5_), channel_id=1, source_target_pairs={{0,1},{1,0},{2,3},{3,2},{4,5},{5,4},{6,7},{7,6}} | collective-permute-start | bytes 3145736 | tf_op jit(solution)/shard_map/ppermute | solution.py:298
  453.2 11.5 %collective-permute-start.16 = (f32[256,384]{0,1:T(8,128)S(1)}, f32[256,384]{0,1:T(8,128)S(1)}, u32[]{:S(2)}, u32[]{:S(2)}) collective-permute-start(f32[256,384]{0,1:T(8,128)S(1)} %dynamic-slice_bitcast_fusion.4), channel_id=1, source_target_pairs={{0,2},{1,3},{2,0},{3,1},{4,6},{5,7},{6,4},{7,5}} | collective-permute-start | bytes 1179656 | tf_op jit(solution)/shard_map/ppermute | solution.py:297
  453.5 26.0 %collective-permute-start.39 = (f32[2,512,256]{2,1,0:T(8,128)}, f32[2,512,256]{2,1,0:T(8,128)}, u32[]{:S(2)}, u32[]{:S(2)}) collective-permute-start(f32[2,512,256]{2,1,0:T(8,128)} %collective-permute-done.38.refs_6_), channel_id=1, source_target_pairs={{0,1},{1,0},{2,3},{3,2},{4,5},{5,4},{6,7},{7,6}} | collective-permute-start | bytes 3145736 | tf_op jit(solution)/shard_map/ppermute | solution.py:298
  453.8 27.6 %collective-permute-start.41 = (f32[2,512,256]{2,1,0:T(8,128)}, f32[2,512,256]{2,1,0:T(8,128)}, u32[]{:S(2)}, u32[]{:S(2)}) collective-permute-start(f32[2,512,256]{2,1,0:T(8,128)} %collective-permute-done.40.refs_7_), channel_id=1, source_target_pairs={{0,1},{1,0},{2,3},{3,2},{4,5},{5,4},{6,7},{7,6}} | collective-permute-start | bytes 3145736 | tf_op jit(solution)/shard_map/ppermute | solution.py:298
  454.0 39.4 %collective-permute-start.27 = (f32[2,512,256]{2,1,0:T(8,128)}, f32[2,512,256]{2,1,0:T(8,128)}, u32[]{:S(2)}, u32[]{:S(2)}) collective-permute-start(f32[2,512,256]{2,1,0:T(8,128)} %copy-done.22), channel_id=1, source_target_pairs={{0,1},{1,0},{2,3},{3,2},{4,5},{5,4},{6,7},{7,6}} | collective-permute-start | bytes 3145736 | tf_op jit(solution)/shard_map/ppermute | solution.py:298
  464.7 28.7 %collective-permute-start.29 = (f32[2,512,256]{2,1,0:T(8,128)}, f32[2,512,256]{2,1,0:T(8,128)}, u32[]{:S(2)}, u32[]{:S(2)}) collective-permute-start(f32[2,512,256]{2,1,0:T(8,128)} %copy-done.24), channel_id=1, source_target_pairs={{0,1},{1,0},{2,3},{3,2},{4,5},{5,4},{6,7},{7,6}} | collective-permute-start | bytes 3145736 | tf_op jit(solution)/shard_map/ppermute | solution.py:298
  467.2 6.7 %copy-start.33 = (f32[2,256,256]{1,2,0:T(8,128)S(1)}, f32[2,256,256]{1,2,0:T(8,128)}, u32[]{:S(2)}) copy-start(f32[2,256,256]{1,2,0:T(8,128)} %copy-done.32) | copy-start | bytes 1572868
  467.2 6.7 %copy-start.39 = (f32[256,256]{0,1:T(8,128)S(1)}, f32[256,256]{0,1:T(8,128)}, u32[]{:S(2)}) copy-start(f32[256,256]{0,1:T(8,128)} %copy-done.38) | copy-start | bytes 786436
  467.2 6.8 %copy-start = (bf16[32,512,128]{2,1,0:T(8,128)(2,1)S(1)}, bf16[32,512,128]{2,1,0:T(8,128)(2,1)}, u32[]{:S(2)}) copy-start(bf16[32,512,128]{2,1,0:T(8,128)(2,1)} %get-tuple-element.106.full_ref) | copy-start | bytes 12582916
  467.2 6.8 %copy-start.26 = (s32[2]{0:T(128)S(1)}, s32[2]{0:T(128)}, u32[]{:S(2)}) copy-start(s32[2]{0:T(128)} %pad_add_fusion.idx_ref) | copy-start | bytes 28
  474.7 4.7 copy-start.31
  479.5 19.8 %collective-permute-start.13 = (f32[256,256]{0,1:T(8,128)S(1)}, f32[256,256]{0,1:T(8,128)S(1)}, u32[]{:S(2)}, u32[]{:S(2)}) collective-permute-start(f32[256,256]{0,1:T(8,128)S(1)} %bitcast_add_fusion.5), channel_id=1, source_target_pairs={{0,4},{4,0},{1,5},{5,1},{2,6},{6,2},{3,7},{7,3}} | collective-permute-start | bytes 786440 | tf_op jit(solution)/shard_map/ppermute | solution.py:299
  481.3 18.0 %collective-permute-start.17 = (f32[256,384]{0,1:T(8,128)S(1)}, f32[256,384]{0,1:T(8,128)S(1)}, u32[]{:S(2)}, u32[]{:S(2)}) collective-permute-start(f32[256,384]{0,1:T(8,128)S(1)} %bitcast_add_fusion.4), channel_id=1, source_target_pairs={{0,4},{4,0},{1,5},{5,1},{2,6},{6,2},{3,7},{7,3}} | collective-permute-start | bytes 1179656 | tf_op jit(solution)/shard_map/ppermute | solution.py:299
  481.6 7.6 %copy-start.3 = (f32[2,512,256]{2,1,0:T(8,128)S(1)}, f32[2,512,256]{2,1,0:T(8,128)}, u32[]{:S(2)}) copy-start(f32[2,512,256]{2,1,0:T(8,128)} %get-tuple-element.119.refs_1_) | copy-start | bytes 3145732
  481.6 7.6 %copy-start.6 = (f32[2,512,256]{2,1,0:T(8,128)S(1)}, f32[2,512,256]{2,1,0:T(8,128)}, u32[]{:S(2)}) copy-start(f32[2,512,256]{2,1,0:T(8,128)} %get-tuple-element.120.refs_2_) | copy-start | bytes 3145732
  481.6 7.6 %copy-start.9 = (f32[2,512,256]{2,1,0:T(8,128)S(1)}, f32[2,512,256]{2,1,0:T(8,128)}, u32[]{:S(2)}) copy-start(f32[2,512,256]{2,1,0:T(8,128)} %get-tuple-element.121.refs_3_) | copy-start | bytes 3145732
  481.6 7.6 %copy-start.19 = (f32[2,512,256]{2,1,0:T(8,128)S(1)}, f32[2,512,256]{2,1,0:T(8,128)}, u32[]{:S(2)}) copy-start(f32[2,512,256]{2,1,0:T(8,128)} %copy-done.18) | copy-start | bytes 3145732
  481.6 7.6 %copy-start.21 = (f32[2,512,256]{2,1,0:T(8,128)S(1)}, f32[2,512,256]{2,1,0:T(8,128)}, u32[]{:S(2)}) copy-start(f32[2,512,256]{2,1,0:T(8,128)} %copy-done.20) | copy-start | bytes 3145732
  481.6 7.6 %copy-start.23 = (f32[2,512,256]{2,1,0:T(8,128)S(1)}, f32[2,512,256]{2,1,0:T(8,128)}, u32[]{:S(2)}) copy-start(f32[2,512,256]{2,1,0:T(8,128)} %copy-done.22) | copy-start | bytes 3145732
  481.6 7.6 %copy-start.25 = (f32[2,512,256]{2,1,0:T(8,128)S(1)}, f32[2,512,256]{2,1,0:T(8,128)}, u32[]{:S(2)}) copy-start(f32[2,512,256]{2,1,0:T(8,128)} %copy-done.24) | copy-start | bytes 3145732
  (18 other events, 38.2 us)

commit v2 on v1

--- a/solution.py
+++ b/solution.py
@@ -11,8 +11,7 @@
 
 NEG_BIG = -1.0e30
 PIECE = 256
-GROUP = 2
-BATCH = 8
+GROUPS = ((2, 3, 3), (4, 4))
 F32 = jnp.float32
 BF16 = jnp.bfloat16
 
@@ -88,7 +87,7 @@
 
 
 def group_kernel(cp_half, scale, n_alias, idx_ref, c_ref, ct_ref, r_ref, rt_ref, wk_ref, wv_ref, q_own, q_oth, do_own, do_oth, *rest):
-    (o_own, o_oth, dq_own, dq_oth, dkv_ref, dw_ref, dr_ref,
+    (o_own, o_oth, dq_own, dq_oth, dkv_ref, dr_ref, dw_ref,
      w_s, k_s, kt_s, v_s, vt_s, qt_s, do_s, s_s, p_s, ds_s, o_s, dqt_s) = rest[n_alias:]
     d_n = v_s.shape[1]
     core = idx_ref[1]
@@ -97,7 +96,7 @@
     def _():
         k_s[:, d_n:] = r_ref[...]
         kt_s[d_n:, :] = rt_ref[...]
-        dr_ref[...] = jnp.zeros(dr_ref.shape, F32)
+        dr_ref[...] = rest[n_alias - 1][...] if n_alias else jnp.zeros(dr_ref.shape, F32)
 
     w_s[:, 0:d_n] = wk_ref[0]
     w_s[:, d_n:] = wv_ref[0]
@@ -137,20 +136,22 @@
     mine = lambda *shape: pl.BlockSpec((1,) + shape, lambda h, idx: (idx[1] * half_heads + idx[2] + h, 0, 0))
     part = lambda *shape: pl.BlockSpec((1,) + shape, lambda h, idx: (idx[2] + h, 0, 0))
     in_specs = [whole(seq, rank), whole(rank, seq), whole(seq, d_r), whole(d_r, seq),
-                mine(rank, w_k.shape[2]), mine(rank, d_v), mine(d_qk, tok), part(d_qk, tok), mine(tok, d_v), part(tok, d_v)]
-    out_specs = [mine(tok, d_v), part(tok, d_v), mine(d_qk, tok), part(d_qk, tok),
+                part(rank, w_k.shape[2]), part(rank, d_v), mine(d_qk, tok), part(d_qk, tok), part(tok, d_v), part(tok, d_v)]
+    out_specs = [part(tok, d_v), part(tok, d_v), mine(d_qk, tok), part(d_qk, tok),
                  pl.BlockSpec((seq, kv), lambda h, idx: (0, idx[2] + h)),
-                 pl.BlockSpec((1, rank, kv), lambda h, idx: (h, 0, 0)),
-                 pl.BlockSpec((seq, d_r), lambda h, idx: (0, 0))]
-    out_shape = [sds((2 * half_heads, tok, d_v), BF16), sds((half_heads, tok, d_v), BF16),
+                 pl.BlockSpec((seq, d_r), lambda h, idx: (0, 0)),
+                 pl.BlockSpec((1, rank, kv), lambda h, idx: (h, 0, 0))]
+    out_shape = [sds((half_heads, tok, d_v), BF16), sds((half_heads, tok, d_v), BF16),
                  sds((2 * half_heads, d_qk, tok), F32), sds((half_heads, d_qk, tok), F32),
-                 sds((seq, half_heads * kv), BF16), sds((count, rank, kv), F32), sds((seq, d_r), F32)]
+                 sds((seq, half_heads * kv), BF16), sds((seq, d_r), F32), sds((count, rank, kv), F32)]
     args = [idx, c_all, ct_all, r_all, rt_all, w_k, w_v, q_all, q_oth, do_all, do_oth]
     aliases = {}
     for i, arr in enumerate(carried):
         aliases[len(args)] = i
         args.append(arr)
         in_specs.append(pl.BlockSpec(memory_space=pl.ANY))
+    if carried:
+        in_specs[-1] = whole(seq, d_r)
     pairs = 2 * tok * (seq // 2 + PIECE // 2)
     flops = count * (2 * pairs * (3 * d_qk + 3 * d_v) + 6 * seq * rank * kv)
     return pl.pallas_call(
@@ -173,52 +174,136 @@
     )(*args)
 
 
-def dc_kernel(order, idx_ref, dkv_ref, wk_ref, wv_ref, *rest):
-    out_ref, acc_s, w_s = rest[-3:]
-    heads, cols, d_n = wk_ref.shape
-    for g in range(heads):
-        w_s[:, 2 * g * d_n:(2 * g + 1) * d_n] = wk_ref[g]
-        w_s[:, (2 * g + 1) * d_n:(2 * g + 2) * d_n] = wv_ref[g]
-    h = pl.program_id(0)
-
-    @pl.when(h == 0)
+def dc_kernel(idx_ref, lo_ref, hi_ref, wk_ref, wv_ref, dr_lo, dr_hi, a_ref, b_ref, w_s):
+    heads, _, d_n = wk_ref.shape
+    cols = a_ref.shape[3]
+
+    @pl.when(pl.program_id(0) == 0)
     def _():
-        acc_s[...] = jnp.zeros(acc_s.shape, F32)
-
-    for j in range(0, len(order), 2):
-        acc_s[rows(j, 2), :] += dot_t(dkv_ref[rows(j, 2), :], w_s[...])
-
-    @pl.when(h == pl.num_programs(0) - 1)
-    def _():
-        for slot, piece in enumerate(order):
-            out_ref[slot, :, 0:cols] = acc_s[rows(piece), :]
-            if len(rest) == 4:
-                dr = rest[0][rows(piece), :]
-                out_ref[slot, :, cols:] = jnp.concatenate([dr, jnp.zeros_like(dr)], axis=1)
-
-
-def dc_call(half, idx, dkv, w_k, w_v, extra, order):
-    seq = dkv.shape[0]
-    half_heads = w_k.shape[0] // 2
-    rank, d_n = w_k.shape[1:]
+        for g in range(heads):
+            w_s[:, 2 * g * d_n:(2 * g + 1) * d_n] = wk_ref[g]
+            w_s[:, (2 * g + 1) * d_n:(2 * g + 2) * d_n] = wv_ref[g]
+
+    for j in range(2):
+        for k, dkv_ref in enumerate((lo_ref, hi_ref)):
+            (a_ref, b_ref)[j][0, k, :, 0:cols] = dot_t(dkv_ref[...], w_s[rows(j), :])
+    for k, dr_ref in enumerate((dr_lo, dr_hi)):
+        dr = dr_ref[...]
+        b_ref[0, k, :, cols:] = jnp.concatenate([dr, jnp.zeros_like(dr)], axis=1)
+
+
+def dc_call(idx, dkv, w_k, w_v, dr):
+    seq, d_r = dr.shape
+    half_heads, rank, d_n = w_k.shape
     kv = d_n + w_v.shape[2]
-    step = 2
-    n_steps = half_heads // step
-    w_spec = pl.BlockSpec((step, rank // 2, d_n), lambda h, idx: (idx[1] * n_steps + h, half, 0))
-    shape = (len(order), PIECE, rank // 2 + sum(2 * e.shape[1] for e in extra))
-    return pl.pallas_call(
-        functools.partial(dc_kernel, order),
-        grid_spec=pltpu.PrefetchScalarGridSpec(
-            num_scalar_prefetch=1, grid=(n_steps,),
-            in_specs=[pl.BlockSpec((seq, step * kv), lambda h, idx: (0, h)), w_spec, w_spec]
-            + [pl.BlockSpec(e.shape, lambda h, idx: (0, 0)) for e in extra],
-            out_specs=pl.BlockSpec(shape, lambda h, idx: (0, 0, 0)),
-            scratch_shapes=[pltpu.VMEM((seq, rank // 2), F32), pltpu.VMEM((rank // 2, step * kv), BF16)]),
-        out_shape=sds(shape, F32),
-        compiler_params=params(60),
-        cost_estimate=pl.CostEstimate(flops=seq * rank * kv * half_heads, bytes_accessed=25 * 2 ** 20, transcendentals=0),
+    n = seq // (2 * PIECE)
+    dev = lambda i: 2 * (i % (n // 2)) + i // (n // 2)
+    lo = lambda w: pl.BlockSpec((PIECE, w), lambda i, idx: (dev(i), 0))
+    hi = lambda w: pl.BlockSpec((PIECE, w), lambda i, idx: (2 * n - 1 - dev(i), 0))
+    w_spec = pl.BlockSpec((half_heads, rank, d_n), lambda i, idx: (0, 0, 0), pipeline_mode=pl.Buffered(1))
+    shapes = [(n, 2, PIECE, rank // 2), (n, 2, PIECE, rank // 2 + 2 * d_r)]
+    return pl.pallas_call(
+        dc_kernel,
+        grid_spec=pltpu.PrefetchScalarGridSpec(
+            num_scalar_prefetch=1, grid=(n,),
+            in_specs=[lo(half_heads * kv), hi(half_heads * kv), w_spec, w_spec, lo(d_r), hi(d_r)],
+            out_specs=[pl.BlockSpec((1,) + s[1:], lambda i, idx: (i, 0, 0, 0)) for s in shapes],
+            scratch_shapes=[pltpu.VMEM((rank, half_heads * kv), BF16)]),
+        out_shape=[sds(s, F32) for s in shapes],
+        compiler_params=params(60),
+        cost_estimate=pl.CostEstimate(flops=2 * seq * rank * kv * half_heads, bytes_accessed=30 * 2 ** 20, transcendentals=0),
         name="dc",
-    )(idx, dkv, w_k, w_v, *extra)
+    )(idx, dkv, dkv, w_k, w_v, dr, dr)
+
+
+def gather_kernel(n_dev, idx_ref, *refs):
+    c_refs, r_refs = refs[0:4], refs[4:8]
+    c_all, ct_all, r_all, rt_all = refs[8:]
+    chip, core = idx_ref[0], idx_ref[1]
+    devs = (2 * chip + core, 2 * chip + 1 - core, 2 - 2 * chip + core, 3 - 2 * chip - core)
+    for dev, c_ref, r_ref in zip(devs, c_refs, r_refs):
+        for piece, half in ((dev, rows(0)), (2 * n_dev - 1 - dev, rows(1))):
+            at = pl.ds(pl.multiple_of(piece * PIECE, PIECE), PIECE)
+            c = c_ref[half, :]
+            c_all[at, :] = c
+            ct_all[:, at] = c.T
+            r = r_ref[:, half]
+            rt_all[:, at] = r
+            r_all[at, :] = r.T
+
+
+def gather_call(idx, n_dev, c_parts, r_parts):
+    tok, rank = c_parts[0].shape
+    d_r = r_parts[0].shape[0]
+    seq = n_dev * tok
+    whole = lambda shape: pl.BlockSpec(shape, lambda i, idx: (0, 0))
+    shapes = [(seq, rank), (rank, seq), (seq, d_r), (d_r, seq)]
+    return pl.pallas_call(
+        functools.partial(gather_kernel, n_dev),
+        grid_spec=pltpu.PrefetchScalarGridSpec(
+            num_scalar_prefetch=1, grid=(1,),
+            in_specs=[whole((tok, rank))] * 4 + [whole((d_r, tok))] * 4,
+            out_specs=[whole(s) for s in shapes]),
+        out_shape=[sds(s, BF16) for s in shapes],
+        compiler_params=params(60),
+        cost_estimate=pl.CostEstimate(flops=10 ** 9, bytes_accessed=8 * 2 ** 20, transcendentals=0),
+        name="gather",
+    )(idx, *c_parts, *r_parts)
+
+
+def relay_kernel(idx_ref, *refs):
+    wide_s = refs[-1]
+    n = len(refs) // 2
+    for in_ref, out_ref in zip(refs[:n], refs[n:-1]):
+        heads, rows_n, d = out_ref.shape
+        wide_s[...] = in_ref[...].astype(F32).reshape(rows_n * heads, d)
+        for h in range(heads):
+            out_ref[h] = wide_s[pl.ds(h, rows_n, stride=heads), :].astype(BF16)
+
+
+def relay_call(idx, w_uk, w_uv, d_out):
+    tok, n_heads, d = d_out.shape
+    heads = n_heads // 2
+    n = 128
+    near = pl.BlockSpec((n, heads, d), lambda i, idx: (i, idx[1], 0))
+    away = pl.BlockSpec((n, heads, d), lambda i, idx: (i, 1 - idx[1], 0))
+    return pl.pallas_call(
+        relay_kernel,
+        grid_spec=pltpu.PrefetchScalarGridSpec(
+            num_scalar_prefetch=1, grid=(tok // n,), in_specs=[away, near, near, near],
+            out_specs=[pl.BlockSpec((heads, n, d), lambda i, idx: (0, i, 0))] * 4,
+            scratch_shapes=[pltpu.VMEM((n * heads, d), F32)]),
+        out_shape=[sds((heads, tok, d), BF16)] * 4,
+        compiler_params=params(60),
+        cost_estimate=pl.CostEstimate(flops=10 ** 9, bytes_accessed=16 * d_out.size, transcendentals=0),
+        name="relay",
+    )(idx, d_out, d_out, w_uk, w_uv)
+
+
+def out_kernel(idx_ref, own_ref, oth_ref, out_ref, wide_s):
+    core = idx_ref[1]
+    heads, n, d = own_ref.shape
+    for side, ref in ((core, own_ref), (1 - core, oth_ref)):
+        for h in range(heads):
+            wide_s[pl.ds(h, n, stride=heads), :] = ref[h].astype(F32)
+        out_ref[:, pl.ds(pl.multiple_of(side * heads, heads), heads), :] = wide_s[...].reshape(n, heads, d).astype(BF16)
+
+
+def out_call(idx, own, oth):
+    heads, tok, d = own.shape
+    n = 128
+    part = pl.BlockSpec((heads, n, d), lambda i, idx: (0, i, 0))
+    return pl.pallas_call(
+        out_kernel,
+        grid_spec=pltpu.PrefetchScalarGridSpec(
+            num_scalar_prefetch=1, grid=(tok // n,), in_specs=[part, part],
+            out_specs=pl.BlockSpec((n, 2 * heads, d), lambda i, idx: (i, 0, 0)),
+            scratch_shapes=[pltpu.VMEM((n * heads, d), F32)]),
+        out_shape=sds((tok, 2 * heads, d), BF16),
+        compiler_params=params(60),
+        cost_estimate=pl.CostEstimate(flops=10 ** 9, bytes_accessed=4 * own.size * 2, transcendentals=0),
+        name="out",
+    )(idx, own, oth)
 
 
 def place_kernel(idx_ref, part_ref, full_ref, out_ref):
@@ -235,7 +320,7 @@
             out_specs=pl.BlockSpec((step, a, b), lambda h, idx: ((1 - idx[1]) * (n // step) + h, 0, 0))),
         out_shape=sds(full.shape, full.dtype),
         input_output_aliases={2: 0},
-        compiler_params=params(24),
+        compiler_params=params(60),
         cost_estimate=pl.CostEstimate(flops=10 ** 9, bytes_accessed=2 * part.size * part.dtype.itemsize, transcendentals=0),
         name="place",
     )(idx, part, full)
@@ -245,30 +330,33 @@
     a_refs, b_refs = refs[:n_parts], refs[n_parts:2 * n_parts]
     k_ref, v_ref = refs[-2:]
     d_n = k_ref.shape[2]
-    for i, (a_ref, b_ref) in enumerate(zip(a_refs, b_refs)):
+    h = 0
+    for a_ref, b_ref in zip(a_refs, b_refs):
         for g in range(a_ref.shape[0]):
             s = a_ref[g] + b_ref[g]
-            k_ref[:, i * a_ref.shape[0] + g, :] = s[:, :d_n]
-            v_ref[:, i * a_ref.shape[0] + g, :] = s[:, d_n:]
+            k_ref[:, h, :] = s[:, :d_n]
+            v_ref[:, h, :] = s[:, d_n:]
+            h += 1
 
 
 def join_call(block, parts_a, parts_b, carried, n_heads):
-    g, rank, kv = parts_a[0].shape
+    rank, kv = parts_a[0].shape[1:]
     n_parts = len(parts_a)
+    heads = sum(p.shape[0] for p in parts_a)
     r_blk = 128
-    part = pl.BlockSpec((g, r_blk, kv), lambda i, idx: (0, i, 0))
-    out = pl.BlockSpec((r_blk, g * n_parts, kv // 2), lambda i, idx: (i, idx[0], 0))
+    parts = [pl.BlockSpec((p.shape[0], r_blk, kv), lambda i, idx: (0, i, 0)) for p in parts_a]
+    out = pl.BlockSpec((r_blk, heads, kv // 2), lambda i, idx: (i, idx[0], 0))
     args = [block, *parts_a, *parts_b, *carried]
     return pl.pallas_call(
         functools.partial(join_kernel, n_parts),
         grid_spec=pltpu.PrefetchScalarGridSpec(
             num_scalar_prefetch=1, grid=(rank // r_blk,),
-            in_specs=[part] * (2 * n_parts) + [pl.BlockSpec(memory_space=pl.ANY)] * len(carried),
+            in_specs=parts + parts + [pl.BlockSpec(memory_space=pl.ANY)] * len(carried),
             out_specs=[out, out]),
         out_shape=[sds((rank, n_heads, kv // 2), F32)] * 2,
         input_output_aliases={1 + 2 * n_parts + i: i for i in range(len(carried))},
-        compiler_params=params(24),
-        cost_estimate=pl.CostEstimate(flops=10 ** 9, bytes_accessed=3 * n_parts * g * rank * kv * 4, transcendentals=0),
+        compiler_params=params(60),
+        cost_estimate=pl.CostEstimate(flops=10 ** 9, bytes_accessed=3 * heads * rank * kv * 4, transcendentals=0),
         name="join",
     )(*args)
 
@@ -298,43 +386,31 @@
         swap_core = lambda a: lax.ppermute(a, 'cp', core_perm)
         swap_tp = lambda a: lax.ppermute(a, 'tp', tp_perm)
 
-        def gather(own, axis):
+        def parts(own):
             far = swap_x(own)
-            near, far_near = swap_core(own), swap_core(far)
-            pick = lambda cond, a, b: jnp.where(cond, a, b)
-            here = (pick(core == 0, own, near), pick(core == 0, near, own))
-            there = (pick(core == 0, far, far_near), pick(core == 0, far_near, far))
-            dev = [pick(chip == 0, here[0], there[0]), pick(chip == 0, here[1], there[1]),
-                   pick(chip == 0, there[0], here[0]), pick(chip == 0, there[1], here[1])]
-            cut = lambda a, i: lax.slice_in_dim(a, i * PIECE, (i + 1) * PIECE, axis=axis)
-            return jnp.concatenate([cut(d, 0) for d in dev] + [cut(d, 1) for d in dev[::-1]], axis=axis)
-
-        c_all, rt_all = gather(c_latent, 0), gather(k_rope.T, 1)
-        ct_all, r_all = c_all.T, rt_all.T
-        w_k, w_v = w_uk.transpose(1, 0, 2), w_uv.transpose(1, 0, 2)
+            return own, swap_core(own), far, swap_core(far)
+
+        idx = jnp.stack([chip, core]).astype(jnp.int32)
+        c_all, ct_all, r_all, rt_all = gather_call(idx, n_cp, parts(c_latent), parts(k_rope.T))
+        do_send, do_all, w_k, w_v = relay_call(idx, w_uk, w_uv, d_out)
         q_all = q_heads.transpose(1, 2, 0)
-        do_all = d_out.transpose(1, 0, 2)
         away = (1 - core) * half_heads
         q_oth = swap_core(lax.dynamic_slice_in_dim(q_all, away, half_heads, 0))
-        do_oth = swap_core(lax.dynamic_slice_in_dim(do_all, away, half_heads, 0))
-
-        n_groups = half_heads // GROUP
-        carried, own, far, near, far_near, dr = (), [], [], [], [], 0.0
-        for g in range(n_groups):
-            idx = jnp.stack([chip, core, jnp.int32(g * GROUP)]).astype(jnp.int32)
-            outs = group_call(GROUP, cp_half, scale, idx, c_all, ct_all, r_all, rt_all, w_k, w_v,
+        do_oth = swap_core(do_send)
+
+        carried, own, far, near, far_near = (), [], [], [], []
+        first = 0
+        for count in sum(GROUPS, ()):
+            idx_g = jnp.stack([chip, core, jnp.int32(first)]).astype(jnp.int32)
+            outs = group_call(count, cp_half, scale, idx_g, c_all, ct_all, r_all, rt_all, w_k, w_v,
                       q_all, q_oth, do_all, do_oth, carried)
-            carried = outs[:5]
-            own.append(outs[5])
-            far.append(swap_x(outs[5]))
-            near.append(swap_core(outs[5]))
+            carried = outs[:6]
+            own.append(outs[6])
+            far.append(swap_x(outs[6]))
+            near.append(swap_core(outs[6]))
             far_near.append(swap_core(far[-1]))
-            dr = dr + outs[6]
-        o_full, o_oth, dq_full, dq_oth, dkv = carried
-        idx = jnp.stack([chip, core]).astype(jnp.int32)
-
-        order = [piece for c in range(2) for x in range(cp_half)
-                 for piece in (2 * x + c, 2 * n_cp - 1 - 2 * x - c)]
+            first += count
+        o_own, o_oth, dq_full, dq_oth, dkv, dr = carried
 
         def fold(arr, axis, pos, swap):
             keep = lax.dynamic_index_in_dim(arr, pos, axis, keepdims=False)
@@ -342,8 +418,8 @@
             return keep + swap(send)
 
         full = []
-        for half, extra in ((0, ()), (1, (dr,))):
-            part = dc_call(half, idx, dkv, w_k, w_v, extra, order).reshape(2, cp_half, 2, PIECE, -1)
+        for part in dc_call(idx, dkv, w_k, w_v, dr):
+            part = part.reshape(2, cp_half, 2, PIECE, -1)
             part = fold(part, 0, core, swap_core)
             part = fold(part, 1, my_tp, swap_tp)
             part = fold(part, 0, chip, swap_x)
@@ -352,16 +428,15 @@
         dc = jnp.concatenate([full[0], full[1][:, :rank // 2]], axis=1)
         dr_out = full[1][:, rank // 2:rank // 2 + d_r]
 
-        n_batch = half_heads // BATCH
-        per = BATCH // GROUP
-        dws = ()
-        for i in range(n_batch):
-            sel = slice(i * per, (i + 1) * per)
+        dws, g0 = (), 0
+        for i, groups in enumerate(GROUPS):
+            sel = slice(g0, g0 + len(groups))
+            g0 += len(groups)
             for side, a, b in ((core, own, far), (1 - core, near, far_near)):
-                block = (side * n_batch + i).reshape(1).astype(jnp.int32)
+                block = (side * len(GROUPS) + i).reshape(1).astype(jnp.int32)
                 dws = join_call(block, a[sel], b[sel], dws, n_heads)
-        dq = place_call(idx, swap_core(dq_oth), dq_full, 4).transpose(2, 0, 1)
-        out = place_call(idx, swap_core(o_oth), o_full, 8).transpose(1, 0, 2)
+        dq = place_call(idx, swap_core(dq_oth), dq_full, 2).transpose(2, 0, 1)
+        out = out_call(idx, o_own, swap_core(o_oth))
         return (out, dq, dc, dr_out, *dws)
 
     return jax.shard_map(device_fn, mesh=mesh,

time: 514 us -> 499 us (0.971)
  local copies, waits for them, and re-layouts: 55.9 us -> 18.5 us
  waiting for transfers between devices: 174 us -> 202 us
    ppermute x12 -> x9, waiting for transfers between devices: 165 us -> 186 us  [device_fn(): swap_x = lambda a: lax.ppermute(a, 'cp', x_perm)]
    unnamed x94 -> x25, local copies, waits for them, and re-layouts: 23.4 us -> 4.37 us
    pallas_call x8 -> x5, Pallas kernels: 183 us -> 167 us  [group_call(): pl.pallas_call(functools.partial(group_kernel, cp_half, scale, len(carrie...]
    pallas_call x2 -> x4, Pallas kernels: 27.5 us -> 40.4 us  [the longest x1 16.7 us: dc_call(): pl.pallas_call(dc_kernel, grid_spec=pltpu.PrefetchScalarGridSpec(num_scal...]
    ppermute x4, waiting for transfers between devices: 2.74 us -> 12.9 us  [device_fn(): swap_tp = lambda a: lax.ppermute(a, 'tp', tp_perm)]
    transpose x2 -> x0, local copies, waits for them, and re-layouts: 8.87 us -> none  [the longest x1 7.85 us: device_fn(): w_k, w_v = (w_uk.transpose(1, 0, 2), w_uv.transpose(1, 0, 2))]
  transfers between devices with their start and end apart: 42 -> 33, of which waited for: 15 -> 12; matrix products, arithmetic and copies ran while one was open for 11% -> 4% of each run, Pallas kernels for 8% -> 10%
where the time goes in v2:
time: 499 us; the launch traced here: 495 us
  Pallas kernels  243 us (49%)
  waiting for transfers between devices  202 us (40%)
  starting transfers between devices  19.9 us (4%)
  local copies, waits for them, and re-layouts  18.5 us (4%)
  other arithmetic  10.6 us (2%)
    ppermute x9, waiting for transfers between devices, device_fn(): swap_x = lambda a: lax.ppermute(a, 'cp', x_perm)  186 us
    pallas_call x5, Pallas kernels, group_call(): pl.pallas_call(functools.partial(group_kernel, cp_half, scale, len(carrie...  167 us
    pallas_call x4, Pallas kernels, join_call(): pl.pallas_call(functools.partial(join_kernel, n_parts), grid_spec=pltpu.P...  26.6 us
    pallas_call x1, Pallas kernels, dc_call(): pl.pallas_call(dc_kernel, grid_spec=pltpu.PrefetchScalarGridSpec(num_scal...  16.7 us
    ppermute x4, waiting for transfers between devices, device_fn(): swap_tp = lambda a: lax.ppermute(a, 'tp', tp_perm)  12.9 us
    pallas_call x1, Pallas kernels, relay_call(): pl.pallas_call(relay_kernel, grid_spec=pltpu.PrefetchScalarGridSpec(num_s...  10.6 us
  transfers between devices with their start and end apart: 33, of which 12 were waited for; matrix products, arithmetic and copies ran while one was open for 4% of the time, Pallas kernels for 10%

profile of v2, /device:TPU:0, one launch (start us, length us, event | category | flops | bytes accessed | tf_op | source)
XLA Modules:
  0.0 494.6 jit_solution(7329637244696480833)
XLA Ops:
  0.7 3.8 dynamic-slice_bitcast_fusion
  4.5 0.8 collective-permute-start.6
  5.3 0.6 pad_add_fusion.idx_ref
  5.9 10.6 %relay.1 = (bf16[16,512,128]{2,1,0:T(8,128)(2,1)}, bf16[16,512,128]{2,1,0:T(8,128)(2,1)}, bf16[16,512,128]{2,1,0:T(8,128)(2,1)}, bf16[16,512,128]{2,1,0:T(8,128)(2,1)}) custom-call(s32[2]{0:T(128)} %pad_add_fusion.idx_ref, bf16[512,32,128]{2,1,0:T(8,128)(2,1)} %refs_1_.1, bf16[512,32,128]{2,1,0:T(8,128)(2,1)} %refs_1_.1, bf16[512,32,128]{2,1,0:T(8,128)(2,1)} %refs_2_.1, ...), custom_call_target="tpu_custom_call" | custom-call | flops 1000000000 | bytes 33554432 | tf_op jit(solution)/shard_map/relay/pallas_call | solution.py:270
  16.5 3.0 collective-permute-start.1
  19.5 12.4 %collective-permute-done.1.refs_2_ = bf16[512,512]{1,0:T(8,128)(2,1)} collective-permute-done((bf16[512,512]{1,0:T(8,128)(2,1)}, bf16[512,512]{1,0:T(8,128)(2,1)}, u32[]{:S(2)}, u32[]{:S(2)}) %collective-permute-start.1) | collective-permute-done | bytes 524320 | tf_op jit(solution)/shard_map/ppermute | solution.py:385
  31.9 0.5 collective-permute-start.3
  32.4 1.7 collective-permute-done.3.refs_5_
  34.2 1.7 collective-permute-start.4
  35.9 0.6 pad_add_fusion.6
  36.6 1.9 collective-permute-done.4.refs_6_
  38.5 0.7 pad_add_fusion.5
  39.1 0.6 collective-permute-done.5.refs_7_
  39.7 0.6 copy-done.11
  40.3 5.1 %gather.1 = (bf16[2048,512]{1,0:T(8,128)(2,1)}, bf16[512,2048]{1,0:T(8,128)(2,1)}, bf16[2048,64]{1,0:T(8,128)(2,1)}, bf16[64,2048]{1,0:T(8,128)(2,1)}) custom-call(s32[2]{0:T(128)} %pad_add_fusion.idx_ref, bf16[512,512]{1,0:T(8,128)(2,1)} %refs_0_.2, bf16[512,512]{1,0:T(8,128)(2,1)} %collective-permute-done.refs_1_, ...), custom_call_target="tpu_custom_call" | custom-call | flops 1000000000 | bytes 8388608 | tf_op jit(solution)/shard_map/gather/pallas_call | solution.py:241
  45.5 1.7 copy-done
  47.1 22.7 %heads.5 = (bf16[16,512,128]{2,1,0:T(8,128)(2,1)}, bf16[16,512,128]{2,1,0:T(8,128)(2,1)}, f32[32,192,512]{2,1,0:T(8,128)}, f32[16,192,512]{2,1,0:T(8,128)}, bf16...) custom-call(s32[3]{0:T(128)} %get-tuple-element.118.idx_ref, ...), custom_call_target="tpu_custom_call" | custom-call | flops 7751073792 | bytes 8388608 | tf_op jit(solution)/shard_map/heads/pallas_call | solution.py:157
  69.8 31.8 %heads.6 = (bf16[16,512,128]{2,1,0:T(8,128)(2,1)}, bf16[16,512,128]{2,1,0:T(8,128)(2,1)}, f32[32,192,512]{2,1,0:T(8,128)}, f32[16,192,512]{2,1,0:T(8,128)}, bf16...) custom-call(s32[3]{0:T(128)} %get-tuple-element.124.idx_ref, ...), custom_call_target="tpu_custom_call", output_to_operand_aliasing={{0}: (11, {}), {1}: (12, {}), {2}: (13, {}), {3}: (14, {}),... | custom-call | flops 11626610688 | bytes 12582912 | tf_op jit(solution)/shard_map/heads/pallas_call | solution.py:157
  101.7 31.6 %heads.7 = (bf16[16,512,128]{2,1,0:T(8,128)(2,1)}, bf16[16,512,128]{2,1,0:T(8,128)(2,1)}, f32[32,192,512]{2,1,0:T(8,128)}, f32[16,192,512]{2,1,0:T(8,128)}, bf16...) custom-call(s32[3]{0:T(128)} %get-tuple-element.125.idx_ref, ...), custom_call_target="tpu_custom_call", output_to_operand_aliasing={{0}: (11, {}), {1}: (12, {}), {2}: (13, {}), {3}: (14, {}),... | custom-call | flops 11626610688 | bytes 12582912 | tf_op jit(solution)/shard_map/heads/pallas_call | solution.py:157
  133.3 40.4 %heads.8 = (bf16[16,512,128]{2,1,0:T(8,128)(2,1)}, bf16[16,512,128]{2,1,0:T(8,128)(2,1)}, f32[32,192,512]{2,1,0:T(8,128)}, f32[16,192,512]{2,1,0:T(8,128)}, bf16...) custom-call(s32[3]{0:T(128)} %get-tuple-element.126.idx_ref, ...), custom_call_target="tpu_custom_call", output_to_operand_aliasing={{0}: (11, {}), {1}: (12, {}), {2}: (13, {}), {3}: (14, {}),... | custom-call | flops 15502147584 | bytes 16777216 | tf_op jit(solution)/shard_map/heads/pallas_call | solution.py:157
  173.7 40.4 %heads.9 = (bf16[16,512,128]{2,1,0:T(8,128)(2,1)}, bf16[16,512,128]{2,1,0:T(8,128)(2,1)}, f32[32,192,512]{2,1,0:T(8,128)}, f32[16,192,512]{2,1,0:T(8,128)}, bf16...) custom-call(s32[3]{0:T(128)} %get-tuple-element.127.idx_ref, ...), custom_call_target="tpu_custom_call", output_to_operand_aliasing={{0}: (11, {}), {1}: (12, {}), {2}: (13, {}), {3}: (14, {}),... | custom-call | flops 15502147584 | bytes 16777216 | tf_op jit(solution)/shard_map/heads/pallas_call | solution.py:157
  214.2 16.7 %dc.1 = (f32[4,2,256,256]{3,2,1,0:T(8,128)}, f32[4,2,256,384]{3,2,1,0:T(8,128)}) custom-call(s32[2]{0:T(128)} %pad_add_fusion.idx_ref, bf16[2048,4096]{1,0:T(8,128)(2,1)} %get-tuple-element.95.lo_ref.hi_ref, bf16[2048,4096]{1,0:T(8,128)(2,1)} %get-tuple-element.95.lo_ref.hi_ref, bf16[16,512,128]{2,1,0:T(8,128)(2,1)} %get-tuple-element.63.wk_ref, ...), custom_call_target="tpu_custom_call" | custom-call | flops 8589934592 | bytes 31457280 | tf_op jit(solution)/shard_map/dc/pallas_call | solution.py:205
  230.8 1.3 dynamic-slice_bitcast_fusion.2
  232.3 0.4 collective-permute-start.24
  232.7 2.7 dynamic-slice_bitcast_fusion.1
  235.6 0.4 collective-permute-start.25
  236.1 1.4 bitcast_add_fusion.1
  237.6 1.0 copy.44
  238.6 1.8 collective-permute-start.11
  240.3 21.1 %collective-permute-done.27.refs_3_ = f32[2,512,256]{2,1,0:T(8,128)} collective-permute-done((f32[2,512,256]{2,1,0:T(8,128)}, f32[2,512,256]{2,1,0:T(8,128)}, u32[]{:S(2)}, u32[]{:S(2)}) %collective-permute-start.27) | collective-permute-done | bytes 1048608 | tf_op jit(solution)/shard_map/ppermute | solution.py:385
  261.5 0.3 collective-permute-start.29
  261.8 0.8 copy-done.7
  262.6 1.7 collective-permute-start.31
  264.3 0.3 collective-permute-start.20
  264.8 1.1 bitcast_add_fusion.3
  265.9 0.7 dynamic-slice_bitcast_fusion.4
  266.7 2.0 bitcast_add_fusion
  268.7 30.4 %collective-permute-done.29.refs_4_ = f32[3,512,256]{2,1,0:T(8,128)} collective-permute-done((f32[3,512,256]{2,1,0:T(8,128)}, f32[3,512,256]{2,1,0:T(8,128)}, u32[]{:S(2)}, u32[]{:S(2)}) %collective-permute-start.29) | collective-permute-done | bytes 1572896 | tf_op jit(solution)/shard_map/ppermute | solution.py:385
  299.3 1.0 constant_dynamic-slice_fusion.1
  300.3 2.3 copy.46
  302.6 30.2 %collective-permute-done.31.refs_5_ = f32[3,512,256]{2,1,0:T(8,128)} collective-permute-done((f32[3,512,256]{2,1,0:T(8,128)}, f32[3,512,256]{2,1,0:T(8,128)}, u32[]{:S(2)}, u32[]{:S(2)}) %collective-permute-start.31) | collective-permute-done | bytes 1572896 | tf_op jit(solution)/shard_map/ppermute | solution.py:385
  332.8 1.8 collective-permute-start.15
  334.5 47.1 %collective-permute-done.12 = f32[256,256]{0,1:T(8,128)} collective-permute-done((f32[256,256]{0,1:T(8,128)}, f32[256,256]{0,1:T(8,128)}, u32[]{:S(2)}, u32[]{:S(2)}) %collective-permute-start.12) | collective-permute-done | bytes 262176 | tf_op jit(solution)/shard_map/ppermute | solution.py:385
  381.6 0.6 collective-permute-start.22
  382.2 1.7 bitcast_add_fusion.5
  383.9 1.7 collective-permute-start.13
  385.9 4.8 collective-permute-done.13
  390.8 0.5 collective-permute-start.32
  391.3 1.2 bitcast_add_fusion.2
  392.5 1.2 collective-permute-start.16
  393.8 42.5 %collective-permute-done.16 = f32[256,384]{0,1:T(8,128)S(1)} collective-permute-done((f32[256,384]{0,1:T(8,128)S(1)}, f32[256,384]{0,1:T(8,128)S(1)}, u32[]{:S(2)}, u32[]{:S(2)}) %collective-permute-start.16) | collective-permute-done | bytes 393248 | tf_op jit(solution)/shard_map/ppermute | solution.py:385
  436.3 1.7 collective-permute-start.17
  438.1 1.1 collective-permute-done.28.refs_3_
  439.3 0.4 collective-permute-start.19
  439.8 8.1 %collective-permute-done.17 = f32[256,384]{0,1:T(8,128)S(1)} collective-permute-done((f32[256,384]{0,1:T(8,128)S(1)}, f32[256,384]{0,1:T(8,128)S(1)}, u32[]{:S(2)}, u32[]{:S(2)}) %collective-permute-start.17) | collective-permute-done | bytes 393248 | tf_op jit(solution)/shard_map/ppermute | solution.py:387
  447.9 6.6 %join.4 = (f32[512,32,128]{2,1,0:T(8,128)}, f32[512,32,128]{2,1,0:T(8,128)}) custom-call(s32[1]{0:T(128)} %bitcast.23.idx_ref, f32[2,512,256]{2,1,0:T(8,128)} %get-tuple-element.101.refs_0_, f32[3,512,256]{2,1,0:T(8,128)} %get-tuple-element.102.refs_1_, f32[3,512,256]{2,1,0:T(8,128)} %get-tuple-element.103.refs_2_, ...), custom_call_target="tpu_custom_call" | custom-call | flops 1000000000 | bytes 12582912 | tf_op jit(solution)/shard_map/join/pallas_call | solution.py:350
  454.6 8.0 %out.1 = bf16[512,32,128]{2,1,0:T(8,128)(2,1)} custom-call(s32[2]{0:T(128)} %pad_add_fusion.idx_ref, bf16[16,512,128]{2,1,0:T(8,128)(2,1)} %get-tuple-element.91.own_ref, bf16[16,512,128]{2,1,0:T(8,128)(2,1)} %collective-permute-done.8.oth_ref), custom_call_target="tpu_custom_call" | custom-call | flops 1000000000 | bytes 8388608 | tf_op jit(solution)/shard_map/out/pallas_call | solution.py:296
  462.6 1.1 maximum_select_fusion.1
  463.7 6.7 %join.5 = (f32[512,32,128]{2,1,0:T(8,128)}, f32[512,32,128]{2,1,0:T(8,128)}) custom-call(s32[1]{0:T(128)} %bitcast.22.idx_ref, f32[2,512,256]{2,1,0:T(8,128)} %collective-permute-done.24.refs_0_, f32[3,512,256]{2,1,0:T(8,128)} %collective-permute-done.25.refs_1_, ...), custom_call_target="tpu_custom_call", output_to_operand_aliasing={{0}: (7, {}), {1}: (8, {})} | custom-call | flops 1000000000 | bytes 12582912 | tf_op jit(solution)/shard_map/join/pallas_call | solution.py:350
  470.4 6.6 %join.6 = (f32[512,32,128]{2,1,0:T(8,128)}, f32[512,32,128]{2,1,0:T(8,128)}) custom-call(s32[1]{0:T(128)} %bitcast.21.idx_ref, f32[4,512,256]{2,1,0:T(8,128)} %get-tuple-element.99.refs_0_, f32[4,512,256]{2,1,0:T(8,128)} %get-tuple-element.100.refs_1_, f32[4,512,256]{2,1,0:T(8,128)} %collective-permute-done.20.refs_2_, ...), custom_call_target="tpu_custom_call", output_to_operand_aliasing={{0}: (5, {}), {1}: (6, {})} | custom-call | flops 1000000000 | bytes 12582912 | tf_op jit(solution)/shard_map/join/pallas_call | solution.py:350
  477.1 0.7 slice.9
  477.9 1.3 copy.47
  479.2 6.7 %join.7 = (f32[512,32,128]{2,1,0:T(8,128)}, f32[512,32,128]{2,1,0:T(8,128)}) custom-call(s32[1]{0:T(128)} %bitcast.20.idx_ref, f32[4,512,256]{2,1,0:T(8,128)} %collective-permute-done.18.refs_0_, f32[4,512,256]{2,1,0:T(8,128)} %collective-permute-done.19.refs_1_, ...), custom_call_target="tpu_custom_call", output_to_operand_aliasing={{0}: (5, {}), {1}: (6, {})} | custom-call | flops 1000000000 | bytes 12582912 | tf_op jit(solution)/shard_map/join/pallas_call | solution.py:350
  485.8 8.5 %place.1 = f32[32,192,512]{2,1,0:T(8,128)} custom-call(s32[2]{0:T(128)} %pad_add_fusion.idx_ref, f32[16,192,512]{2,1,0:T(8,128)} %collective-permute-done.9.part_ref, f32[32,192,512]{2,1,0:T(8,128)} %get-tuple-element.94.full_ref), custom_call_target="tpu_custom_call", output_to_operand_aliasing={{}: (2, {})} | custom-call | flops 1000000000 | bytes 12582912 | tf_op jit(solution)/shard_map/place/pallas_call | solution.py:315
  (66 shorter events, 2.0 us)
Async XLA Ops:
  4.5 41.0 %collective-permute-start.6 = (bf16[16,192,512]{2,1,0:T(8,128)(2,1)}, bf16[16,192,512]{2,1,0:T(8,128)(2,1)S(1)}, u32[]{:S(2)}, u32[]{:S(2)}) collective-permute-start(bf16[16,192,512]{2,1,0:T(8,128)(2,1)} %dynamic-slice_bitcast_fusion), channel_id=1, source_target_pairs={{0,1},{1,0},{2,3},{3,2},{4,5},{5,4},{6,7},{7,6}} | collective-permute-start | bytes 9437192 | tf_op jit(solution)/shard_map/ppermute | solution.py:386
  5.9 26.1 %copy-start.8 = (bf16[512,64]{0,1:T(8,128)(2,1)S(1)}, bf16[512,64]{0,1:T(8,128)(2,1)}, u32[]{:S(2)}) copy-start(bf16[512,64]{0,1:T(8,128)(2,1)} %param.7) | copy-start | bytes 196612
  16.5 29.0 %collective-permute-start.7 = (bf16[16,512,128]{2,1,0:T(8,128)(2,1)}, bf16[16,512,128]{2,1,0:T(8,128)(2,1)}, u32[]{:S(2)}, u32[]{:S(2)}) collective-permute-start(bf16[16,512,128]{2,1,0:T(8,128)(2,1)} %get-tuple-element.66), channel_id=1, source_target_pairs={{0,1},{1,0},{2,3},{3,2},{4,5},{5,4},{6,7},{7,6}} | collective-permute-start | bytes 6291464 | tf_op jit(solution)/shard_map/ppermute | solution.py:386
  16.5 15.4 %collective-permute-start.1 = (bf16[512,512]{1,0:T(8,128)(2,1)}, bf16[512,512]{1,0:T(8,128)(2,1)}, u32[]{:S(2)}, u32[]{:S(2)}) collective-permute-start(bf16[512,512]{1,0:T(8,128)(2,1)} %refs_0_.2), channel_id=1, source_target_pairs={{0,2},{1,3},{2,0},{3,1},{4,6},{5,7},{6,4},{7,5}} | collective-permute-start | bytes 1572872 | tf_op jit(solution)/shard_map/ppermute | solution.py:385
  19.5 20.2 %collective-permute-start = (bf16[512,512]{1,0:T(8,128)(2,1)}, bf16[512,512]{1,0:T(8,128)(2,1)}, u32[]{:S(2)}, u32[]{:S(2)}) collective-permute-start(bf16[512,512]{1,0:T(8,128)(2,1)} %refs_0_.2), channel_id=1, source_target_pairs={{0,1},{1,0},{2,3},{3,2},{4,5},{5,4},{6,7},{7,6}} | collective-permute-start | bytes 1572872 | tf_op jit(solution)/shard_map/ppermute | solution.py:386
  31.9 7.8 %collective-permute-start.2 = (bf16[512,512]{1,0:T(8,128)(2,1)}, bf16[512,512]{1,0:T(8,128)(2,1)}, u32[]{:S(2)}, u32[]{:S(2)}) collective-permute-start(bf16[512,512]{1,0:T(8,128)(2,1)} %collective-permute-done.1.refs_2_), channel_id=1, source_target_pairs={{0,1},{1,0},{2,3},{3,2},{4,5},{5,4},{6,7},{7,6}} | collective-permute-start | bytes 1572872 | tf_op jit(solution)/shard_map/ppermute | solution.py:386
  31.9 2.2 collective-permute-start.3
  34.2 5.5 %copy-start.9 = (bf16[64,512]{1,0:T(8,128)(2,1)}, bf16[64,512]{1,0:T(8,128)(2,1)S(1)}, u32[]{:S(2)}) copy-start(bf16[64,512]{1,0:T(8,128)(2,1)S(1)} %collective-permute-done.3.refs_5_) | copy-start | bytes 196612
  34.2 4.3 collective-permute-start.4
  38.4 1.3 copy-start.10
  38.4 1.3 collective-permute-start.5
  39.7 0.6 copy-start.11
  45.5 1.7 copy-start
  232.1 4.0 copy-start.2
  232.2 3.8 collective-permute-start.10
  232.3 6.2 %collective-permute-start.24 = (f32[2,512,256]{2,1,0:T(8,128)}, f32[2,512,256]{2,1,0:T(8,128)}, u32[]{:S(2)}, u32[]{:S(2)}) collective-permute-start(f32[2,512,256]{2,1,0:T(8,128)} %get-tuple-element.101.refs_0_), channel_id=1, source_target_pairs={{0,1},{1,0},{2,3},{3,2},{4,5},{5,4},{6,7},{7,6}} | collective-permute-start | bytes 3145736 | tf_op jit(solution)/shard_map/ppermute | solution.py:386
  235.4 27.1 %collective-permute-start.14 = (f32[2,2,256,384]{3,2,1,0:T(8,128)}, f32[2,2,256,384]{3,2,1,0:T(8,128)}, u32[]{:S(2)}, u32[]{:S(2)}) collective-permute-start(f32[2,2,256,384]{3,2,1,0:T(8,128)} %dynamic-slice_bitcast_fusion.1), channel_id=1, source_target_pairs={{0,1},{1,0},{2,3},{3,2},{4,5},{5,4},{6,7},{7,6}} | collective-permute-start | bytes 4718600 | tf_op jit(solution)/shard_map/ppermute | solution.py:386
  235.6 28.7 %collective-permute-start.25 = (f32[3,512,256]{2,1,0:T(8,128)}, f32[3,512,256]{2,1,0:T(8,128)}, u32[]{:S(2)}, u32[]{:S(2)}) collective-permute-start(f32[3,512,256]{2,1,0:T(8,128)} %get-tuple-element.102.refs_1_), channel_id=1, source_target_pairs={{0,1},{1,0},{2,3},{3,2},{4,5},{5,4},{6,7},{7,6}} | collective-permute-start | bytes 4718600 | tf_op jit(solution)/shard_map/ppermute | solution.py:386
  235.9 25.5 %collective-permute-start.27 = (f32[2,512,256]{2,1,0:T(8,128)}, f32[2,512,256]{2,1,0:T(8,128)}, u32[]{:S(2)}, u32[]{:S(2)}) collective-permute-start(f32[2,512,256]{2,1,0:T(8,128)} %get-tuple-element.101.refs_0_), channel_id=1, source_target_pairs={{0,2},{1,3},{2,0},{3,1},{4,6},{5,7},{6,4},{7,5}} | collective-permute-start | bytes 3145736 | tf_op jit(solution)/shard_map/ppermute | solution.py:385
  235.9 28.4 %collective-permute-start.26 = (f32[3,512,256]{2,1,0:T(8,128)}, f32[3,512,256]{2,1,0:T(8,128)}, u32[]{:S(2)}, u32[]{:S(2)}) collective-permute-start(f32[3,512,256]{2,1,0:T(8,128)} %get-tuple-element.103.refs_2_), channel_id=1, source_target_pairs={{0,1},{1,0},{2,3},{3,2},{4,5},{5,4},{6,7},{7,6}} | collective-permute-start | bytes 4718600 | tf_op jit(solution)/shard_map/ppermute | solution.py:386
  237.5 24.3 %copy-start.1 = (bf16[16,512,128]{2,1,0:T(8,128)(2,1)S(1)}, bf16[16,512,128]{2,1,0:T(8,128)(2,1)}, u32[]{:S(2)}) copy-start(bf16[16,512,128]{2,1,0:T(8,128)(2,1)} %get-tuple-element.92) | copy-start | bytes 6291460
  238.6 23.2 %collective-permute-start.11 = (f32[2,256,256]{1,2,0:T(8,128)}, f32[2,256,256]{1,2,0:T(8,128)S(1)}, u32[]{:S(2)}, u32[]{:S(2)}) collective-permute-start(f32[2,256,256]{1,2,0:T(8,128)} %bitcast.46), channel_id=1, source_target_pairs={{0,4},{4,0},{1,5},{5,1},{2,6},{6,2},{3,7},{7,3}} | collective-permute-start | bytes 1572872 | tf_op jit(solution)/shard_map/ppermute | solution.py:387
  261.5 37.6 %collective-permute-start.29 = (f32[3,512,256]{2,1,0:T(8,128)}, f32[3,512,256]{2,1,0:T(8,128)}, u32[]{:S(2)}, u32[]{:S(2)}) collective-permute-start(f32[3,512,256]{2,1,0:T(8,128)} %get-tuple-element.102.refs_1_), channel_id=1, source_target_pairs={{0,2},{1,3},{2,0},{3,1},{4,6},{5,7},{6,4},{7,5}} | collective-permute-start | bytes 4718600 | tf_op jit(solution)/shard_map/ppermute | solution.py:385
  261.8 0.8 copy-start.7
  261.8 122.1 %collective-permute-start.8 = (bf16[16,512,128]{2,1,0:T(8,128)(2,1)S(1)}, bf16[16,512,128]{2,1,0:T(8,128)(2,1)}, u32[]{:S(2)}, u32[]{:S(2)}) collective-permute-start(bf16[16,512,128]{2,1,0:T(8,128)(2,1)S(1)} %copy-done.1), channel_id=1, source_target_pairs={{0,1},{1,0},{2,3},{3,2},{4,5},{5,4},{6,7},{7,6}} | collective-permute-start | bytes 6291464 | tf_op jit(solution)/shard_map/ppermute | solution.py:386
  262.6 70.2 %collective-permute-start.31 = (f32[3,512,256]{2,1,0:T(8,128)}, f32[3,512,256]{2,1,0:T(8,128)}, u32[]{:S(2)}, u32[]{:S(2)}) collective-permute-start(f32[3,512,256]{2,1,0:T(8,128)} %get-tuple-element.103.refs_2_), channel_id=1, source_target_pairs={{0,2},{1,3},{2,0},{3,1},{4,6},{5,7},{6,4},{7,5}} | collective-permute-start | bytes 4718600 | tf_op jit(solution)/shard_map/ppermute | solution.py:385
  264.3 221.5 %collective-permute-start.9 = (f32[16,192,512]{2,1,0:T(8,128)}, f32[16,192,512]{2,1,0:T(8,128)}, u32[]{:S(2)}, u32[]{:S(2)}) collective-permute-start(f32[16,192,512]{2,1,0:T(8,128)} %get-tuple-element.93), channel_id=1, source_target_pairs={{0,1},{1,0},{2,3},{3,2},{4,5},{5,4},{6,7},{7,6}} | collective-permute-start | bytes 18874376 | tf_op jit(solution)/shard_map/ppermute | solution.py:386
  264.3 128.2 %collective-permute-start.20 = (f32[4,512,256]{2,1,0:T(8,128)}, f32[4,512,256]{2,1,0:T(8,128)}, u32[]{:S(2)}, u32[]{:S(2)}) collective-permute-start(f32[4,512,256]{2,1,0:T(8,128)} %get-tuple-element.99.refs_0_), channel_id=1, source_target_pairs={{0,2},{1,3},{2,0},{3,1},{4,6},{5,7},{6,4},{7,5}} | collective-permute-start | bytes 6291464 | tf_op jit(solution)/shard_map/ppermute | solution.py:385
  299.1 82.6 %collective-permute-start.12 = (f32[256,256]{0,1:T(8,128)}, f32[256,256]{0,1:T(8,128)}, u32[]{:S(2)}, u32[]{:S(2)}) collective-permute-start(f32[256,256]{0,1:T(8,128)} %dynamic-slice_bitcast_fusion.4), channel_id=1, source_target_pairs={{0,2},{1,3},{2,0},{3,1},{4,6},{5,7},{6,4},{7,5}} | collective-permute-start | bytes 786440 | tf_op jit(solution)/shard_map/ppermute | solution.py:385
  332.8 58.0 %collective-permute-start.15 = (f32[2,256,384]{1,2,0:T(8,128)}, f32[2,256,384]{1,2,0:T(8,128)}, u32[]{:S(2)}, u32[]{:S(2)}) collective-permute-start(f32[2,256,384]{1,2,0:T(8,128)} %bitcast.45), channel_id=1, source_target_pairs={{0,4},{4,0},{1,5},{5,1},{2,6},{6,2},{3,7},{7,3}} | collective-permute-start | bytes 2359304 | tf_op jit(solution)/shard_map/ppermute | solution.py:387
  381.6 54.7 %collective-permute-start.22 = (f32[4,512,256]{2,1,0:T(8,128)}, f32[4,512,256]{2,1,0:T(8,128)}, u32[]{:S(2)}, u32[]{:S(2)}) collective-permute-start(f32[4,512,256]{2,1,0:T(8,128)} %get-tuple-element.100.refs_1_), channel_id=1, source_target_pairs={{0,2},{1,3},{2,0},{3,1},{4,6},{5,7},{6,4},{7,5}} | collective-permute-start | bytes 6291464 | tf_op jit(solution)/shard_map/ppermute | solution.py:385
  383.9 6.9 %collective-permute-start.13 = (f32[256,256]{0,1:T(8,128)}, f32[256,256]{0,1:T(8,128)S(1)}, u32[]{:S(2)}, u32[]{:S(2)}) collective-permute-start(f32[256,256]{0,1:T(8,128)} %bitcast_add_fusion.5), channel_id=1, source_target_pairs={{0,4},{4,0},{1,5},{5,1},{2,6},{6,2},{3,7},{7,3}} | collective-permute-start | bytes 786440 | tf_op jit(solution)/shard_map/ppermute | solution.py:387
  385.9 53.2 %copy-start.3 = (f32[4,512,256]{2,1,0:T(8,128)S(1)}, f32[4,512,256]{2,1,0:T(8,128)}, u32[]{:S(2)}) copy-start(f32[4,512,256]{2,1,0:T(8,128)} %get-tuple-element.99.refs_0_) | copy-start | bytes 6291460
  390.7 48.5 %collective-permute-start.30 = (f32[3,512,256]{2,1,0:T(8,128)}, f32[3,512,256]{2,1,0:T(8,128)S(1)}, u32[]{:S(2)}, u32[]{:S(2)}) collective-permute-start(f32[3,512,256]{2,1,0:T(8,128)} %collective-permute-done.29.refs_4_), channel_id=1, source_target_pairs={{0,1},{1,0},{2,3},{3,2},{4,5},{5,4},{6,7},{7,6}} | collective-permute-start | bytes 4718600 | tf_op jit(solution)/shard_map/ppermute | solution.py:386
  390.8 48.9 %collective-permute-start.32 = (f32[3,512,256]{2,1,0:T(8,128)}, f32[3,512,256]{2,1,0:T(8,128)S(1)}, u32[]{:S(2)}, u32[]{:S(2)}) collective-permute-start(f32[3,512,256]{2,1,0:T(8,128)} %collective-permute-done.31.refs_5_), channel_id=1, source_target_pairs={{0,1},{1,0},{2,3},{3,2},{4,5},{5,4},{6,7},{7,6}} | collective-permute-start | bytes 4718600 | tf_op jit(solution)/shard_map/ppermute | solution.py:386
  392.5 43.7 %collective-permute-start.16 = (f32[256,384]{0,1:T(8,128)S(1)}, f32[256,384]{0,1:T(8,128)S(1)}, u32[]{:S(2)}, u32[]{:S(2)}) collective-permute-start(f32[256,384]{0,1:T(8,128)S(1)} %dynamic-slice_bitcast_fusion.3), channel_id=1, source_target_pairs={{0,2},{1,3},{2,0},{3,1},{4,6},{5,7},{6,4},{7,5}} | collective-permute-start | bytes 1179656 | tf_op jit(solution)/shard_map/ppermute | solution.py:385
  436.2 2.9 collective-permute-start.28
  436.3 11.5 %collective-permute-start.17 = (f32[256,384]{0,1:T(8,128)S(1)}, f32[256,384]{0,1:T(8,128)S(1)}, u32[]{:S(2)}, u32[]{:S(2)}) collective-permute-start(f32[256,384]{0,1:T(8,128)S(1)} %bitcast_add_fusion.4), channel_id=1, source_target_pairs={{0,4},{4,0},{1,5},{5,1},{2,6},{6,2},{3,7},{7,3}} | collective-permute-start | bytes 1179656 | tf_op jit(solution)/shard_map/ppermute | solution.py:387
  439.1 8.7 %copy-start.6 = (f32[2,512,256]{2,1,0:T(8,128)}, f32[2,512,256]{2,1,0:T(8,128)S(1)}, u32[]{:S(2)}) copy-start(f32[2,512,256]{2,1,0:T(8,128)S(1)} %collective-permute-done.28.refs_3_) | copy-start | bytes 3145732
  439.1 40.0 %collective-permute-start.18 = (f32[4,512,256]{2,1,0:T(8,128)S(1)}, f32[4,512,256]{2,1,0:T(8,128)}, u32[]{:S(2)}, u32[]{:S(2)}) collective-permute-start(f32[4,512,256]{2,1,0:T(8,128)S(1)} %copy-done.3), channel_id=1, source_target_pairs={{0,1},{1,0},{2,3},{3,2},{4,5},{5,4},{6,7},{7,6}} | collective-permute-start | bytes 6291464 | tf_op jit(solution)/shard_map/ppermute | solution.py:386
  439.3 8.6 %copy-start.4 = (f32[3,512,256]{2,1,0:T(8,128)}, f32[3,512,256]{2,1,0:T(8,128)S(1)}, u32[]{:S(2)}) copy-start(f32[3,512,256]{2,1,0:T(8,128)S(1)} %collective-permute-done.30.refs_4_) | copy-start | bytes 4718596
  439.3 39.9 %collective-permute-start.19 = (f32[4,512,256]{2,1,0:T(8,128)}, f32[4,512,256]{2,1,0:T(8,128)}, u32[]{:S(2)}, u32[]{:S(2)}) collective-permute-start(f32[4,512,256]{2,1,0:T(8,128)} %get-tuple-element.100.refs_1_), channel_id=1, source_target_pairs={{0,1},{1,0},{2,3},{3,2},{4,5},{5,4},{6,7},{7,6}} | collective-permute-start | bytes 6291464 | tf_op jit(solution)/shard_map/ppermute | solution.py:386
  439.6 8.2 %copy-start.5 = (f32[3,512,256]{2,1,0:T(8,128)}, f32[3,512,256]{2,1,0:T(8,128)S(1)}, u32[]{:S(2)}) copy-start(f32[3,512,256]{2,1,0:T(8,128)S(1)} %collective-permute-done.32.refs_5_) | copy-start | bytes 4718596
  439.6 39.5 %collective-permute-start.21 = (f32[4,512,256]{2,1,0:T(8,128)}, f32[4,512,256]{2,1,0:T(8,128)}, u32[]{:S(2)}, u32[]{:S(2)}) collective-permute-start(f32[4,512,256]{2,1,0:T(8,128)} %collective-permute-done.20.refs_2_), channel_id=1, source_target_pairs={{0,1},{1,0},{2,3},{3,2},{4,5},{5,4},{6,7},{7,6}} | collective-permute-start | bytes 6291464 | tf_op jit(solution)/shard_map/ppermute | solution.py:386
  447.9 31.3 %collective-permute-start.23 = (f32[4,512,256]{2,1,0:T(8,128)}, f32[4,512,256]{2,1,0:T(8,128)}, u32[]{:S(2)}, u32[]{:S(2)}) collective-permute-start(f32[4,512,256]{2,1,0:T(8,128)} %collective-permute-done.22.refs_3_), channel_id=1, source_target_pairs={{0,1},{1,0},{2,3},{3,2},{4,5},{5,4},{6,7},{7,6}} | collective-permute-start | bytes 6291464 | tf_op jit(solution)/shard_map/ppermute | solution.py:386

commit v3 on v2

--- a/solution.py
+++ b/solution.py
@@ -46,10 +46,11 @@
         vt_s[:, rows(j, 2)] = kv[:, d_n:].T
     key_i = lax.broadcasted_iota(jnp.int32, (PIECE, PIECE), 0)
     qry_i = lax.broadcasted_iota(jnp.int32, (PIECE, PIECE), 1)
-    for b, n in enumerate(lens):
-        base = sum(lens[:b])
+    tops = {}
+
+    def score(b):
+        n, base = lens[b], sum(lens[:b])
         qt_b = qt_s[:, rows(b)]
-        do_t = do_s[rows(b), :].T
         top8 = jnp.full((8, PIECE), NEG_BIG, F32)
         for j in range(n):
             s = dot(k_s[rows(j), :], qt_b)
@@ -57,14 +58,23 @@
                 s = jnp.where(key_i <= qry_i, s, NEG_BIG)
             s_s[rows(base + j), :] = s
             top8 = jnp.maximum(top8, jnp.max(s.reshape(PIECE // 8, 8, PIECE), axis=0))
-        top = jnp.max(top8, axis=0, keepdims=True) * to_log2
+        tops[b] = jnp.max(top8, axis=0, keepdims=True) * to_log2
+
+    invs = {}
+
+    def soft(b):
+        n, base = lens[b], sum(lens[:b])
         sum8 = jnp.zeros((8, PIECE), F32)
         for j in range(n):
-            p = jnp.exp2(s_s[rows(base + j), :] * to_log2 - top)
+            p = jnp.exp2(s_s[rows(base + j), :] * to_log2 - tops[b])
             sum8 = sum8 + jnp.sum(p.reshape(PIECE // 8, 8, PIECE), axis=0)
             s_s[rows(base + j), :] = p
             p_s[rows(j), rows(b)] = p.astype(BF16)
-        inv = 1.0 / jnp.sum(sum8, axis=0, keepdims=True)
+        invs[b] = 1.0 / jnp.sum(sum8, axis=0, keepdims=True)
+
+    def back(b):
+        n, base, inv = lens[b], sum(lens[:b]), invs[b]
+        do_t = do_s[rows(b), :].T
         o_t = dot(vt_s[:, 0:n * PIECE], p_s[0:n * PIECE, rows(b)]) * inv
         o_s[rows(b), :] = o_t.T.astype(BF16)
         d_dot = jnp.sum(o_t * do_t.astype(F32), axis=0, keepdims=True)
@@ -74,16 +84,26 @@
             p_s[rows(j), rows(b)] = p.astype(BF16)
             ds_s[rows(j), rows(b)] = (p * (dp - d_dot)).astype(BF16)
         dqt_s[:, rows(b)] = dot(kt_s[:, 0:n * PIECE], ds_s[0:n * PIECE, rows(b)]) * scale
-    for j in range(n_max):
+
+    score(0)
+    for b in range(4):
+        soft(b)
+        if b < 3:
+            score(b + 1)
+        back(b)
+    edges = sorted({0, *lens})
+    for j, j_end in zip(edges[:-1], edges[1:]):
         w = PIECE * sum(1 for n in lens if n > j)
-        dv = dot(p_s[rows(j), 0:w], do_s[0:w, :])
-        dk = dot_t(ds_s[rows(j), 0:w], qt_s[:, 0:w]) * scale
-        dkv_ref[rows(j), 0:d_n] = dk[:, :d_n].astype(BF16)
-        dkv_ref[rows(j), d_n:] = dv.astype(BF16)
-        dr_ref[rows(j), :] += dk[:, d_n:]
+        at = rows(j, j_end - j)
+        dv = dot(p_s[at, 0:w], do_s[0:w, :])
+        dk = dot_t(ds_s[at, 0:w], qt_s[:, 0:w]) * scale
+        dkv_ref[at, 0:d_n] = dk[:, :d_n].astype(BF16)
+        dkv_ref[at, d_n:] = dv.astype(BF16)
+        dr_ref[at, :] += dk[:, d_n:]
     if n_rows < dkv_ref.shape[0]:
         dkv_ref[n_rows:, :] = jnp.zeros((dkv_ref.shape[0] - n_rows, dkv_ref.shape[1]), BF16)
-    dw_ref[0] = dot(ct_ref[:, 0:n_rows], dkv_ref[0:n_rows, :])
+    for i in range(2):
+        dw_ref[0, rows(i), :] = dot(ct_ref[rows(i), 0:n_rows], dkv_ref[0:n_rows, :])
 
 
 def group_kernel(cp_half, scale, n_alias, idx_ref, c_ref, ct_ref, r_ref, rt_ref, wk_ref, wv_ref, q_own, q_oth, do_own, do_oth, *rest):
@@ -174,22 +194,27 @@
     )(*args)
 
 
-def dc_kernel(idx_ref, lo_ref, hi_ref, wk_ref, wv_ref, dr_lo, dr_hi, a_ref, b_ref, w_s):
+def dc_kernel(idx_ref, lo_ref, hi_ref, wk_ref, wv_ref, dr_lo, dr_hi, *refs):
+    sends, keeps, w_s = refs[0:2], refs[2:4], refs[4]
     heads, _, d_n = wk_ref.shape
-    cols = a_ref.shape[3]
-
-    @pl.when(pl.program_id(0) == 0)
+    i = pl.program_id(0)
+
+    @pl.when(i == 0)
     def _():
         for g in range(heads):
             w_s[:, 2 * g * d_n:(2 * g + 1) * d_n] = wk_ref[g]
             w_s[:, (2 * g + 1) * d_n:(2 * g + 2) * d_n] = wv_ref[g]
 
-    for j in range(2):
-        for k, dkv_ref in enumerate((lo_ref, hi_ref)):
-            (a_ref, b_ref)[j][0, k, :, 0:cols] = dot_t(dkv_ref[...], w_s[rows(j), :])
-    for k, dr_ref in enumerate((dr_lo, dr_hi)):
-        dr = dr_ref[...]
-        b_ref[0, k, :, cols:] = jnp.concatenate([dr, jnp.zeros_like(dr)], axis=1)
+    def fill(outs):
+        for j, ref in enumerate(outs):
+            for k, (dkv_ref, dr_ref) in enumerate(((lo_ref, dr_lo), (hi_ref, dr_hi))):
+                ref[0, k, :, 0:PIECE] = dot_t(dkv_ref[...], w_s[rows(j), :])
+                if j == 1:
+                    dr = dr_ref[...]
+                    ref[0, k, :, PIECE:] = jnp.concatenate([dr, jnp.zeros_like(dr)], axis=1)
+
+    pl.when(i < 2)(functools.partial(fill, sends))
+    pl.when(i >= 2)(functools.partial(fill, keeps))
 
 
 def dc_call(idx, dkv, w_k, w_v, dr):
@@ -197,17 +222,18 @@
     half_heads, rank, d_n = w_k.shape
     kv = d_n + w_v.shape[2]
     n = seq // (2 * PIECE)
-    dev = lambda i: 2 * (i % (n // 2)) + i // (n // 2)
-    lo = lambda w: pl.BlockSpec((PIECE, w), lambda i, idx: (dev(i), 0))
-    hi = lambda w: pl.BlockSpec((PIECE, w), lambda i, idx: (2 * n - 1 - dev(i), 0))
+    dev = lambda i, idx: 2 * (i % 2) + jnp.where(i < 2, 1 - idx[1], idx[1])
+    lo = lambda w: pl.BlockSpec((PIECE, w), lambda i, idx: (dev(i, idx), 0))
+    hi = lambda w: pl.BlockSpec((PIECE, w), lambda i, idx: (2 * n - 1 - dev(i, idx), 0))
     w_spec = pl.BlockSpec((half_heads, rank, d_n), lambda i, idx: (0, 0, 0), pipeline_mode=pl.Buffered(1))
-    shapes = [(n, 2, PIECE, rank // 2), (n, 2, PIECE, rank // 2 + 2 * d_r)]
+    shapes = [(n // 2, 2, PIECE, rank // 2), (n // 2, 2, PIECE, rank // 2 + 2 * d_r)] * 2
+    maps = [lambda i, idx: (jnp.minimum(i, 1), 0, 0, 0)] * 2 + [lambda i, idx: (jnp.maximum(i - 2, 0), 0, 0, 0)] * 2
     return pl.pallas_call(
         dc_kernel,
         grid_spec=pltpu.PrefetchScalarGridSpec(
             num_scalar_prefetch=1, grid=(n,),
             in_specs=[lo(half_heads * kv), hi(half_heads * kv), w_spec, w_spec, lo(d_r), hi(d_r)],
-            out_specs=[pl.BlockSpec((1,) + s[1:], lambda i, idx: (i, 0, 0, 0)) for s in shapes],
+            out_specs=[pl.BlockSpec((1,) + s[1:], m) for s, m in zip(shapes, maps)],
             scratch_shapes=[pltpu.VMEM((rank, half_heads * kv), BF16)]),
         out_shape=[sds(s, F32) for s in shapes],
         compiler_params=params(60),
@@ -412,17 +438,16 @@
             first += count
         o_own, o_oth, dq_full, dq_oth, dkv, dr = carried
 
-        def fold(arr, axis, pos, swap):
-            keep = lax.dynamic_index_in_dim(arr, pos, axis, keepdims=False)
-            send = lax.dynamic_index_in_dim(arr, 1 - pos, axis, keepdims=False)
-            return keep + swap(send)
+        def fold(arrs, axis, pos, swap):
+            cut = lambda p: [lax.dynamic_index_in_dim(a, p, axis, keepdims=False) for a in arrs]
+            return cut(pos) + [swap(functools.reduce(jnp.add, cut(1 - pos)))]
 
         full = []
-        for part in dc_call(idx, dkv, w_k, w_v, dr):
-            part = part.reshape(2, cp_half, 2, PIECE, -1)
-            part = fold(part, 0, core, swap_core)
-            part = fold(part, 1, my_tp, swap_tp)
-            part = fold(part, 0, chip, swap_x)
+        dc_out = dc_call(idx, dkv, w_k, w_v, dr)
+        for half in range(2):
+            arrs = [dc_out[2 + half], swap_core(dc_out[half])]
+            arrs = fold(arrs, 1, my_tp, swap_tp)
+            part = functools.reduce(jnp.add, fold(arrs, 0, chip, swap_x))
             mate = swap_tp(part)
             full.append(jnp.where(my_tp == 0, jnp.concatenate([part, mate], axis=0), jnp.concatenate([mate, part], axis=0)))
         dc = jnp.concatenate([full[0], full[1][:, :rank // 2]], axis=1)

time: 499 us -> 464 us (0.930)
  Pallas kernels: 243 us -> 211 us
  local copies, waits for them, and re-layouts: 18.5 us -> 8.69 us
    pallas_call x5, Pallas kernels: 167 us -> 134 us  [group_call(): pl.pallas_call(functools.partial(group_kernel, cp_half, scale, len(carrie...]
    ppermute x4, waiting for transfers between devices: 12.9 us -> 28.4 us  [device_fn(): swap_tp = lambda a: lax.ppermute(a, 'tp', tp_perm)]
    ppermute x9, waiting for transfers between devices: 186 us -> 173 us  [device_fn(): swap_x = lambda a: lax.ppermute(a, 'cp', x_perm)]
    ppermute x9, starting transfers between devices: 9.11 us -> 15.8 us  [device_fn(): swap_x = lambda a: lax.ppermute(a, 'cp', x_perm)]
  transfers between devices with their start and end apart: 33 -> 33, of which waited for: 12 -> 11; matrix products, arithmetic and copies ran while one was open for 4% -> 3% of each run, Pallas kernels for 10% -> 11%
where the time goes in v3:
time: 464 us; the launch traced here: 460 us
  Pallas kernels  211 us (45%)
  waiting for transfers between devices  204 us (44%)
  starting transfers between devices  24.8 us (5%)
  other arithmetic  10.7 us (2%)
  local copies, waits for them, and re-layouts  8.69 us (2%)
    ppermute x9, waiting for transfers between devices, device_fn(): swap_x = lambda a: lax.ppermute(a, 'cp', x_perm)  173 us
    pallas_call x5, Pallas kernels, group_call(): pl.pallas_call(functools.partial(group_kernel, cp_half, scale, len(carrie...  134 us
    ppermute x4, waiting for transfers between devices, device_fn(): swap_tp = lambda a: lax.ppermute(a, 'tp', tp_perm)  28.4 us
    pallas_call x4, Pallas kernels, join_call(): pl.pallas_call(functools.partial(join_kernel, n_parts), grid_spec=pltpu.P...  26.7 us
    pallas_call x1, Pallas kernels, dc_call(): pl.pallas_call(dc_kernel, grid_spec=pltpu.PrefetchScalarGridSpec(num_scal...  17.8 us
    ppermute x9, starting transfers between devices, device_fn(): swap_x = lambda a: lax.ppermute(a, 'cp', x_perm)  15.8 us
    pallas_call x1, Pallas kernels, relay_call(): pl.pallas_call(relay_kernel, grid_spec=pltpu.PrefetchScalarGridSpec(num_s...  10.6 us
  transfers between devices with their start and end apart: 33, of which 11 were waited for; matrix products, arithmetic and copies ran while one was open for 3% of the time, Pallas kernels for 11%

profile of v3, /device:TPU:0, one launch (start us, length us, event | category | flops | bytes accessed | tf_op | source)
XLA Modules:
  0.0 460.0 jit_solution(17054389058797256249)
XLA Ops:
  0.7 3.8 dynamic-slice_bitcast_fusion
  4.5 0.8 collective-permute-start.6
  5.3 0.6 pad_add_fusion.idx_ref
  5.9 10.6 %relay.1 = (bf16[16,512,128]{2,1,0:T(8,128)(2,1)}, bf16[16,512,128]{2,1,0:T(8,128)(2,1)}, bf16[16,512,128]{2,1,0:T(8,128)(2,1)}, bf16[16,512,128]{2,1,0:T(8,128)(2,1)}) custom-call(s32[2]{0:T(128)} %pad_add_fusion.idx_ref, bf16[512,32,128]{2,1,0:T(8,128)(2,1)} %refs_1_.1, bf16[512,32,128]{2,1,0:T(8,128)(2,1)} %refs_1_.1, bf16[512,32,128]{2,1,0:T(8,128)(2,1)} %refs_2_.1, ...), custom_call_target="tpu_custom_call" | custom-call | flops 1000000000 | bytes 33554432 | tf_op jit(solution)/shard_map/relay/pallas_call | solution.py:296
  16.6 3.0 collective-permute-start.1
  19.6 12.1 %collective-permute-done.1.refs_2_ = bf16[512,512]{1,0:T(8,128)(2,1)S(1)} collective-permute-done((bf16[512,512]{1,0:T(8,128)(2,1)S(1)}, bf16[512,512]{1,0:T(8,128)(2,1)S(1)}, u32[]{:S(2)}, u32[]{:S(2)}) %collective-permute-start.1) | collective-permute-done | bytes 524320 | tf_op jit(solution)/shard_map/ppermute | solution.py:411
  31.7 0.5 collective-permute-start.3
  32.2 1.5 collective-permute-done.3.refs_5_
  33.7 1.7 collective-permute-start.4
  35.5 0.6 pad_add_fusion.6
  36.1 1.9 collective-permute-done.4.refs_6_
  38.0 0.6 pad_add_fusion.5
  38.6 0.6 collective-permute-done.5.refs_7_
  39.3 0.8 copy-done.14
  40.1 5.1 %gather.1 = (bf16[2048,512]{1,0:T(8,128)(2,1)}, bf16[512,2048]{1,0:T(8,128)(2,1)}, bf16[2048,64]{1,0:T(8,128)(2,1)}, bf16[64,2048]{1,0:T(8,128)(2,1)}) custom-call(s32[2]{0:T(128)} %pad_add_fusion.idx_ref, bf16[512,512]{1,0:T(8,128)(2,1)} %refs_0_.2, bf16[512,512]{1,0:T(8,128)(2,1)} %copy-done.14, bf16[512,512]{1,0:T(8,128)(2,1)} %copy-done.13, ...), custom_call_target="tpu_custom_call" | custom-call | flops 1000000000 | bytes 8388608 | tf_op jit(solution)/shard_map/gather/pallas_call | solution.py:267
  45.2 1.7 copy-done
  46.9 18.9 %heads.5 = (bf16[16,512,128]{2,1,0:T(8,128)(2,1)}, bf16[16,512,128]{2,1,0:T(8,128)(2,1)}, f32[32,192,512]{2,1,0:T(8,128)}, f32[16,192,512]{2,1,0:T(8,128)}, bf16...) custom-call(s32[3]{0:T(128)} %get-tuple-element.122.idx_ref, ...), custom_call_target="tpu_custom_call" | custom-call | flops 7751073792 | bytes 8388608 | tf_op jit(solution)/shard_map/heads/pallas_call | solution.py:177
  65.8 25.5 %heads.6 = (bf16[16,512,128]{2,1,0:T(8,128)(2,1)}, bf16[16,512,128]{2,1,0:T(8,128)(2,1)}, f32[32,192,512]{2,1,0:T(8,128)}, f32[16,192,512]{2,1,0:T(8,128)}, bf16...) custom-call(s32[3]{0:T(128)} %get-tuple-element.124.idx_ref, ...), custom_call_target="tpu_custom_call", output_to_operand_aliasing={{0}: (11, {}), {1}: (12, {}), {2}: (13, {}), {3}: (14, {}),... | custom-call | flops 11626610688 | bytes 12582912 | tf_op jit(solution)/shard_map/heads/pallas_call | solution.py:177
  91.2 25.5 %heads.7 = (bf16[16,512,128]{2,1,0:T(8,128)(2,1)}, bf16[16,512,128]{2,1,0:T(8,128)(2,1)}, f32[32,192,512]{2,1,0:T(8,128)}, f32[16,192,512]{2,1,0:T(8,128)}, bf16...) custom-call(s32[3]{0:T(128)} %get-tuple-element.125.idx_ref, ...), custom_call_target="tpu_custom_call", output_to_operand_aliasing={{0}: (11, {}), {1}: (12, {}), {2}: (13, {}), {3}: (14, {}),... | custom-call | flops 11626610688 | bytes 12582912 | tf_op jit(solution)/shard_map/heads/pallas_call | solution.py:177
  116.8 32.2 %heads.8 = (bf16[16,512,128]{2,1,0:T(8,128)(2,1)}, bf16[16,512,128]{2,1,0:T(8,128)(2,1)}, f32[32,192,512]{2,1,0:T(8,128)}, f32[16,192,512]{2,1,0:T(8,128)}, bf16...) custom-call(s32[3]{0:T(128)} %get-tuple-element.126.idx_ref, ...), custom_call_target="tpu_custom_call", output_to_operand_aliasing={{0}: (11, {}), {1}: (12, {}), {2}: (13, {}), {3}: (14, {}),... | custom-call | flops 15502147584 | bytes 16777216 | tf_op jit(solution)/shard_map/heads/pallas_call | solution.py:177
  149.0 32.0 %heads.9 = (bf16[16,512,128]{2,1,0:T(8,128)(2,1)}, bf16[16,512,128]{2,1,0:T(8,128)(2,1)}, f32[32,192,512]{2,1,0:T(8,128)}, f32[16,192,512]{2,1,0:T(8,128)}, bf16...) custom-call(s32[3]{0:T(128)} %get-tuple-element.127.idx_ref, ...), custom_call_target="tpu_custom_call", output_to_operand_aliasing={{0}: (11, {}), {1}: (12, {}), {2}: (13, {}), {3}: (14, {}),... | custom-call | flops 15502147584 | bytes 16777216 | tf_op jit(solution)/shard_map/heads/pallas_call | solution.py:177
  181.0 17.8 %dc.1 = (f32[2,2,256,256]{3,2,1,0:T(8,128)}, f32[2,2,256,384]{3,2,1,0:T(8,128)}, f32[2,2,256,256]{3,2,1,0:T(8,128)}, f32[2,2,256,384]{3,2,1,0:T(8,128)}) custom-call(s32[2]{0:T(128)} %pad_add_fusion.idx_ref, bf16[2048,4096]{1,0:T(8,128)(2,1)} %get-tuple-element.97.lo_ref.hi_ref, bf16[2048,4096]{1,0:T(8,128)(2,1)} %get-tuple-element.97.lo_ref.hi_ref, ...), custom_call_target="tpu_custom_call" | custom-call | flops 8589934592 | bytes 31457280 | tf_op jit(solution)/shard_map/dc/pallas_call | solution.py:231
  198.8 0.1 collective-permute-start.10
  198.9 0.4 collective-permute-start.24
  199.4 0.4 collective-permute-start.25
  199.8 2.8 collective-permute-start.27
  202.7 1.3 add_bitcast_fusion.1
  204.0 1.5 collective-permute-start.11
  205.5 20.8 %collective-permute-done.27.refs_3_ = f32[2,512,256]{2,1,0:T(8,128)} collective-permute-done((f32[2,512,256]{2,1,0:T(8,128)S(1)}, f32[2,512,256]{2,1,0:T(8,128)}, u32[]{:S(2)}, u32[]{:S(2)}) %collective-permute-start.27) | collective-permute-done | bytes 1048608 | tf_op jit(solution)/shard_map/ppermute | solution.py:411
  226.3 1.7 collective-permute-start.29
  228.0 0.3 collective-permute-start.31
  228.4 0.2 collective-permute-start.8
  228.6 0.2 copy-done.7
  228.8 1.5 collective-permute-start.20
  230.3 1.2 bitcast_add_fusion.2
  231.5 32.4 %collective-permute-done.29.refs_4_ = f32[3,512,256]{2,1,0:T(8,128)} collective-permute-done((f32[3,512,256]{2,1,0:T(8,128)}, f32[3,512,256]{2,1,0:T(8,128)}, u32[]{:S(2)}, u32[]{:S(2)}) %collective-permute-start.29) | collective-permute-done | bytes 1572896 | tf_op jit(solution)/shard_map/ppermute | solution.py:411
  263.9 1.7 collective-permute-start.12
  265.6 32.0 %collective-permute-done.31.refs_5_ = f32[3,512,256]{2,1,0:T(8,128)} collective-permute-done((f32[3,512,256]{2,1,0:T(8,128)}, f32[3,512,256]{2,1,0:T(8,128)}, u32[]{:S(2)}, u32[]{:S(2)}) %collective-permute-start.31) | collective-permute-done | bytes 1572896 | tf_op jit(solution)/shard_map/ppermute | solution.py:411
  297.6 1.7 collective-permute-start.22
  299.3 1.5 add_bitcast_fusion
  300.8 47.3 %collective-permute-done.12 = f32[256,256]{1,0:T(8,128)S(1)} collective-permute-done((f32[256,256]{1,0:T(8,128)S(1)}, f32[256,256]{1,0:T(8,128)S(1)}, u32[]{:S(2)}, u32[]{:S(2)}) %collective-permute-start.12) | collective-permute-done | bytes 262176 | tf_op jit(solution)/shard_map/ppermute | solution.py:411
  348.0 1.5 collective-permute-start.15
  349.6 1.2 fusion.1
  350.7 0.5 collective-permute-start.13
  351.3 19.2 %collective-permute-done.13 = f32[256,256]{1,0:T(8,128)S(1)} collective-permute-done((f32[256,256]{1,0:T(8,128)S(1)}, f32[256,256]{1,0:T(8,128)S(1)}, u32[]{:S(2)}, u32[]{:S(2)}) %collective-permute-start.13) | collective-permute-done | bytes 262176 | tf_op jit(solution)/shard_map/ppermute | solution.py:413
  370.5 0.5 collective-permute-start.32
  371.0 1.3 bitcast_add_fusion
  372.3 1.2 collective-permute-start.16
  373.5 26.5 %collective-permute-done.16 = f32[256,384]{1,0:T(8,128)S(1)} collective-permute-done((f32[256,384]{1,0:T(8,128)S(1)}, f32[256,384]{1,0:T(8,128)S(1)}, u32[]{:S(2)}, u32[]{:S(2)}) %collective-permute-start.16) | collective-permute-done | bytes 393248 | tf_op jit(solution)/shard_map/ppermute | solution.py:411
  400.0 1.3 fusion
  401.4 1.6 collective-permute-start.17
  402.9 0.2 collective-permute-start.18
  403.2 0.3 collective-permute-start.19
  403.5 0.2 collective-permute-start.21
  403.7 9.2 %collective-permute-done.17 = f32[256,384]{1,0:T(8,128)S(1)} collective-permute-done((f32[256,384]{1,0:T(8,128)S(1)}, f32[256,384]{1,0:T(8,128)S(1)}, u32[]{:S(2)}, u32[]{:S(2)}) %collective-permute-start.17) | collective-permute-done | bytes 393248 | tf_op jit(solution)/shard_map/ppermute | solution.py:413
  413.0 6.7 %join.4 = (f32[512,32,128]{2,1,0:T(8,128)}, f32[512,32,128]{2,1,0:T(8,128)}) custom-call(s32[1]{0:T(128)} %bitcast.19.idx_ref, f32[2,512,256]{2,1,0:T(8,128)} %get-tuple-element.105.refs_0_, f32[3,512,256]{2,1,0:T(8,128)} %get-tuple-element.106.refs_1_, f32[3,512,256]{2,1,0:T(8,128)} %get-tuple-element.107.refs_2_, ...), custom_call_target="tpu_custom_call" | custom-call | flops 1000000000 | bytes 12582912 | tf_op jit(solution)/shard_map/join/pallas_call | solution.py:376
  419.7 8.2 %out.1 = bf16[512,32,128]{2,1,0:T(8,128)(2,1)} custom-call(s32[2]{0:T(128)} %pad_add_fusion.idx_ref, bf16[16,512,128]{2,1,0:T(8,128)(2,1)} %get-tuple-element.93.own_ref, bf16[16,512,128]{2,1,0:T(8,128)(2,1)} %collective-permute-done.8.oth_ref), custom_call_target="tpu_custom_call" | custom-call | flops 1000000000 | bytes 8388608 | tf_op jit(solution)/shard_map/out/pallas_call | solution.py:322
  427.9 6.6 %join.5 = (f32[512,32,128]{2,1,0:T(8,128)}, f32[512,32,128]{2,1,0:T(8,128)}) custom-call(s32[1]{0:T(128)} %bitcast.18.idx_ref, f32[2,512,256]{2,1,0:T(8,128)} %collective-permute-done.24.refs_0_, f32[3,512,256]{2,1,0:T(8,128)} %collective-permute-done.25.refs_1_, ...), custom_call_target="tpu_custom_call", output_to_operand_aliasing={{0}: (7, {}), {1}: (8, {})} | custom-call | flops 1000000000 | bytes 12582912 | tf_op jit(solution)/shard_map/join/pallas_call | solution.py:376
  434.6 6.7 %join.6 = (f32[512,32,128]{2,1,0:T(8,128)}, f32[512,32,128]{2,1,0:T(8,128)}) custom-call(s32[1]{0:T(128)} %bitcast.17.idx_ref, f32[4,512,256]{2,1,0:T(8,128)} %get-tuple-element.103.refs_0_, f32[4,512,256]{2,1,0:T(8,128)} %get-tuple-element.104.refs_1_, ...), custom_call_target="tpu_custom_call", output_to_operand_aliasing={{0}: (5, {}), {1}: (6, {})} | custom-call | flops 1000000000 | bytes 12582912 | tf_op jit(solution)/shard_map/join/pallas_call | solution.py:376
  441.4 0.8 copy.43
  442.2 1.1 pad_maximum_fusion
  443.3 1.3 copy-done.2
  444.6 6.6 %join.7 = (f32[512,32,128]{2,1,0:T(8,128)}, f32[512,32,128]{2,1,0:T(8,128)}) custom-call(s32[1]{0:T(128)} %bitcast.16.idx_ref, f32[4,512,256]{2,1,0:T(8,128)} %copy-done.2, f32[4,512,256]{2,1,0:T(8,128)} %collective-permute-done.19.refs_1_, f32[4,512,256]{2,1,0:T(8,128)} %collective-permute-done.21.refs_2_, ...), custom_call_target="tpu_custom_call", output_to_operand_aliasing={{0}: (5, {}), {1}: (6, {})} | custom-call | flops 1000000000 | bytes 12582912 | tf_op jit(solution)/shard_map/join/pallas_call | solution.py:376
  451.2 8.5 %place.1 = f32[32,192,512]{2,1,0:T(8,128)} custom-call(s32[2]{0:T(128)} %pad_add_fusion.idx_ref, f32[16,192,512]{2,1,0:T(8,128)} %collective-permute-done.9.part_ref, f32[32,192,512]{2,1,0:T(8,128)} %get-tuple-element.96.full_ref), custom_call_target="tpu_custom_call", output_to_operand_aliasing={{}: (2, {})} | custom-call | flops 1000000000 | bytes 12582912 | tf_op jit(solution)/shard_map/place/pallas_call | solution.py:341
  (70 shorter events, 0.4 us)
Async XLA Ops:
  4.5 40.7 %collective-permute-start.6 = (bf16[16,192,512]{2,1,0:T(8,128)(2,1)}, bf16[16,192,512]{2,1,0:T(8,128)(2,1)S(1)}, u32[]{:S(2)}, u32[]{:S(2)}) collective-permute-start(bf16[16,192,512]{2,1,0:T(8,128)(2,1)} %dynamic-slice_bitcast_fusion), channel_id=1, source_target_pairs={{0,1},{1,0},{2,3},{3,2},{4,5},{5,4},{6,7},{7,6}} | collective-permute-start | bytes 9437192 | tf_op jit(solution)/shard_map/ppermute | solution.py:412
  5.9 10.7 %copy-start.12 = (bf16[512,512]{1,0:T(8,128)(2,1)S(1)}, bf16[512,512]{1,0:T(8,128)(2,1)}, u32[]{:S(2)}) copy-start(bf16[512,512]{1,0:T(8,128)(2,1)} %refs_0_.2) | copy-start | bytes 1572868
  5.9 25.8 %copy-start.15 = (bf16[512,64]{0,1:T(8,128)(2,1)S(1)}, bf16[512,64]{0,1:T(8,128)(2,1)}, u32[]{:S(2)}) copy-start(bf16[512,64]{0,1:T(8,128)(2,1)} %param.7) | copy-start | bytes 196612
  16.6 28.6 %collective-permute-start.7 = (bf16[16,512,128]{2,1,0:T(8,128)(2,1)}, bf16[16,512,128]{2,1,0:T(8,128)(2,1)}, u32[]{:S(2)}, u32[]{:S(2)}) collective-permute-start(bf16[16,512,128]{2,1,0:T(8,128)(2,1)} %get-tuple-element.68), channel_id=1, source_target_pairs={{0,1},{1,0},{2,3},{3,2},{4,5},{5,4},{6,7},{7,6}} | collective-permute-start | bytes 6291464 | tf_op jit(solution)/shard_map/ppermute | solution.py:412
  16.6 15.1 %collective-permute-start.1 = (bf16[512,512]{1,0:T(8,128)(2,1)S(1)}, bf16[512,512]{1,0:T(8,128)(2,1)S(1)}, u32[]{:S(2)}, u32[]{:S(2)}) collective-permute-start(bf16[512,512]{1,0:T(8,128)(2,1)S(1)} %copy-done.12), channel_id=1, source_target_pairs={{0,2},{1,3},{2,0},{3,1},{4,6},{5,7},{6,4},{7,5}} | collective-permute-start | bytes 1572872 | tf_op jit(solution)/shard_map/ppermute | solution.py:411
  19.6 19.7 %collective-permute-start = (bf16[512,512]{1,0:T(8,128)(2,1)S(1)}, bf16[512,512]{1,0:T(8,128)(2,1)S(1)}, u32[]{:S(2)}, u32[]{:S(2)}) collective-permute-start(bf16[512,512]{1,0:T(8,128)(2,1)S(1)} %copy-done.12), channel_id=1, source_target_pairs={{0,1},{1,0},{2,3},{3,2},{4,5},{5,4},{6,7},{7,6}} | collective-permute-start | bytes 1572872 | tf_op jit(solution)/shard_map/ppermute | solution.py:412
  31.7 7.6 %copy-start.13 = (bf16[512,512]{1,0:T(8,128)(2,1)}, bf16[512,512]{1,0:T(8,128)(2,1)S(1)}, u32[]{:S(2)}) copy-start(bf16[512,512]{1,0:T(8,128)(2,1)S(1)} %collective-permute-done.1.refs_2_) | copy-start | bytes 1572868
  31.7 8.4 %collective-permute-start.2 = (bf16[512,512]{1,0:T(8,128)(2,1)S(1)}, bf16[512,512]{1,0:T(8,128)(2,1)}, u32[]{:S(2)}, u32[]{:S(2)}) collective-permute-start(bf16[512,512]{1,0:T(8,128)(2,1)S(1)} %collective-permute-done.1.refs_2_), channel_id=1, source_target_pairs={{0,1},{1,0},{2,3},{3,2},{4,5},{5,4},{6,7},{7,6}} | collective-permute-start | bytes 1572872 | tf_op jit(solution)/shard_map/ppermute | solution.py:412
  31.7 2.0 collective-permute-start.3
  33.7 6.3 %copy-start.16 = (bf16[64,512]{1,0:T(8,128)(2,1)}, bf16[64,512]{1,0:T(8,128)(2,1)S(1)}, u32[]{:S(2)}) copy-start(bf16[64,512]{1,0:T(8,128)(2,1)S(1)} %collective-permute-done.3.refs_5_) | copy-start | bytes 196612
  33.7 4.3 collective-permute-start.4
  38.0 2.1 copy-start.17
  38.0 1.3 collective-permute-start.5
  39.3 0.8 copy-start.18
  39.3 0.8 copy-start.14
  45.2 1.7 copy-start
  181.0 18.0 %copy-start.5 = (f32[2,512,256]{2,1,0:T(8,128)S(1)}, f32[2,512,256]{2,1,0:T(8,128)}, u32[]{:S(2)}) copy-start(f32[2,512,256]{2,1,0:T(8,128)} %get-tuple-element.105.refs_0_) | copy-start | bytes 3145732
  181.0 47.4 %copy-start.1 = (bf16[16,512,128]{2,1,0:T(8,128)(2,1)S(1)}, bf16[16,512,128]{2,1,0:T(8,128)(2,1)}, u32[]{:S(2)}) copy-start(bf16[16,512,128]{2,1,0:T(8,128)(2,1)} %get-tuple-element.94) | copy-start | bytes 6291460
  198.8 3.9 collective-permute-start.10
  198.9 5.0 %collective-permute-start.24 = (f32[2,512,256]{2,1,0:T(8,128)S(1)}, f32[2,512,256]{2,1,0:T(8,128)}, u32[]{:S(2)}, u32[]{:S(2)}) collective-permute-start(f32[2,512,256]{2,1,0:T(8,128)S(1)} %copy-done.5), channel_id=1, source_target_pairs={{0,1},{1,0},{2,3},{3,2},{4,5},{5,4},{6,7},{7,6}} | collective-permute-start | bytes 3145736 | tf_op jit(solution)/shard_map/ppermute | solution.py:412
  199.3 28.7 %collective-permute-start.14 = (f32[2,2,256,384]{3,2,1,0:T(8,128)}, f32[2,2,256,384]{3,2,1,0:T(8,128)}, u32[]{:S(2)}, u32[]{:S(2)}) collective-permute-start(f32[2,2,256,384]{3,2,1,0:T(8,128)} %get-tuple-element.102), channel_id=1, source_target_pairs={{0,1},{1,0},{2,3},{3,2},{4,5},{5,4},{6,7},{7,6}} | collective-permute-start | bytes 4718600 | tf_op jit(solution)/shard_map/ppermute | solution.py:412
  199.4 28.9 %collective-permute-start.25 = (f32[3,512,256]{2,1,0:T(8,128)}, f32[3,512,256]{2,1,0:T(8,128)}, u32[]{:S(2)}, u32[]{:S(2)}) collective-permute-start(f32[3,512,256]{2,1,0:T(8,128)} %get-tuple-element.106.refs_1_), channel_id=1, source_target_pairs={{0,1},{1,0},{2,3},{3,2},{4,5},{5,4},{6,7},{7,6}} | collective-permute-start | bytes 4718600 | tf_op jit(solution)/shard_map/ppermute | solution.py:412
  199.8 26.5 %collective-permute-start.27 = (f32[2,512,256]{2,1,0:T(8,128)S(1)}, f32[2,512,256]{2,1,0:T(8,128)}, u32[]{:S(2)}, u32[]{:S(2)}) collective-permute-start(f32[2,512,256]{2,1,0:T(8,128)S(1)} %copy-done.5), channel_id=1, source_target_pairs={{0,2},{1,3},{2,0},{3,1},{4,6},{5,7},{6,4},{7,5}} | collective-permute-start | bytes 3145736 | tf_op jit(solution)/shard_map/ppermute | solution.py:411
  202.7 26.2 %collective-permute-start.26 = (f32[3,512,256]{2,1,0:T(8,128)}, f32[3,512,256]{2,1,0:T(8,128)}, u32[]{:S(2)}, u32[]{:S(2)}) collective-permute-start(f32[3,512,256]{2,1,0:T(8,128)} %get-tuple-element.107.refs_2_), channel_id=1, source_target_pairs={{0,1},{1,0},{2,3},{3,2},{4,5},{5,4},{6,7},{7,6}} | collective-permute-start | bytes 4718600 | tf_op jit(solution)/shard_map/ppermute | solution.py:412
  204.0 24.1 %collective-permute-start.11 = (f32[2,256,256]{2,1,0:T(8,128)S(1)}, f32[2,256,256]{2,1,0:T(8,128)S(1)}, u32[]{:S(2)}, u32[]{:S(2)}) collective-permute-start(f32[2,256,256]{2,1,0:T(8,128)S(1)} %add_bitcast_fusion.1), channel_id=1, source_target_pairs={{0,4},{4,0},{1,5},{5,1},{2,6},{6,2},{3,7},{7,3}} | collective-permute-start | bytes 1572872 | tf_op jit(solution)/shard_map/ppermute | solution.py:413
  226.3 37.6 %collective-permute-start.29 = (f32[3,512,256]{2,1,0:T(8,128)}, f32[3,512,256]{2,1,0:T(8,128)}, u32[]{:S(2)}, u32[]{:S(2)}) collective-permute-start(f32[3,512,256]{2,1,0:T(8,128)} %get-tuple-element.106.refs_1_), channel_id=1, source_target_pairs={{0,2},{1,3},{2,0},{3,1},{4,6},{5,7},{6,4},{7,5}} | collective-permute-start | bytes 4718600 | tf_op jit(solution)/shard_map/ppermute | solution.py:411
  228.0 0.8 copy-start.7
  228.0 223.2 %collective-permute-start.9 = (f32[16,192,512]{2,1,0:T(8,128)}, f32[16,192,512]{2,1,0:T(8,128)}, u32[]{:S(2)}, u32[]{:S(2)}) collective-permute-start(f32[16,192,512]{2,1,0:T(8,128)} %get-tuple-element.95), channel_id=1, source_target_pairs={{0,1},{1,0},{2,3},{3,2},{4,5},{5,4},{6,7},{7,6}} | collective-permute-start | bytes 18874376 | tf_op jit(solution)/shard_map/ppermute | solution.py:412
  228.0 69.5 %collective-permute-start.31 = (f32[3,512,256]{2,1,0:T(8,128)}, f32[3,512,256]{2,1,0:T(8,128)}, u32[]{:S(2)}, u32[]{:S(2)}) collective-permute-start(f32[3,512,256]{2,1,0:T(8,128)} %get-tuple-element.107.refs_2_), channel_id=1, source_target_pairs={{0,2},{1,3},{2,0},{3,1},{4,6},{5,7},{6,4},{7,5}} | collective-permute-start | bytes 4718600 | tf_op jit(solution)/shard_map/ppermute | solution.py:411
  228.4 122.4 %collective-permute-start.8 = (bf16[16,512,128]{2,1,0:T(8,128)(2,1)S(1)}, bf16[16,512,128]{2,1,0:T(8,128)(2,1)}, u32[]{:S(2)}, u32[]{:S(2)}) collective-permute-start(bf16[16,512,128]{2,1,0:T(8,128)(2,1)S(1)} %copy-done.1), channel_id=1, source_target_pairs={{0,1},{1,0},{2,3},{3,2},{4,5},{5,4},{6,7},{7,6}} | collective-permute-start | bytes 6291464 | tf_op jit(solution)/shard_map/ppermute | solution.py:412
  228.8 143.5 %collective-permute-start.20 = (f32[4,512,256]{2,1,0:T(8,128)}, f32[4,512,256]{2,1,0:T(8,128)}, u32[]{:S(2)}, u32[]{:S(2)}) collective-permute-start(f32[4,512,256]{2,1,0:T(8,128)} %get-tuple-element.103.refs_0_), channel_id=1, source_target_pairs={{0,2},{1,3},{2,0},{3,1},{4,6},{5,7},{6,4},{7,5}} | collective-permute-start | bytes 6291464 | tf_op jit(solution)/shard_map/ppermute | solution.py:411
  263.9 84.2 %collective-permute-start.12 = (f32[256,256]{1,0:T(8,128)S(1)}, f32[256,256]{1,0:T(8,128)S(1)}, u32[]{:S(2)}, u32[]{:S(2)}) collective-permute-start(f32[256,256]{1,0:T(8,128)S(1)} %bitcast_add_fusion.2), channel_id=1, source_target_pairs={{0,2},{1,3},{2,0},{3,1},{4,6},{5,7},{6,4},{7,5}} | collective-permute-start | bytes 786440 | tf_op jit(solution)/shard_map/ppermute | solution.py:411
  297.6 103.8 %collective-permute-start.22 = (f32[4,512,256]{2,1,0:T(8,128)}, f32[4,512,256]{2,1,0:T(8,128)}, u32[]{:S(2)}, u32[]{:S(2)}) collective-permute-start(f32[4,512,256]{2,1,0:T(8,128)} %get-tuple-element.104.refs_1_), channel_id=1, source_target_pairs={{0,2},{1,3},{2,0},{3,1},{4,6},{5,7},{6,4},{7,5}} | collective-permute-start | bytes 6291464 | tf_op jit(solution)/shard_map/ppermute | solution.py:411
  348.0 22.5 %collective-permute-start.15 = (f32[2,256,384]{2,1,0:T(8,128)S(1)}, f32[2,256,384]{2,1,0:T(8,128)}, u32[]{:S(2)}, u32[]{:S(2)}) collective-permute-start(f32[2,256,384]{2,1,0:T(8,128)S(1)} %add_bitcast_fusion), channel_id=1, source_target_pairs={{0,4},{4,0},{1,5},{5,1},{2,6},{6,2},{3,7},{7,3}} | collective-permute-start | bytes 2359304 | tf_op jit(solution)/shard_map/ppermute | solution.py:413
  350.7 19.7 %collective-permute-start.13 = (f32[256,256]{1,0:T(8,128)S(1)}, f32[256,256]{1,0:T(8,128)S(1)}, u32[]{:S(2)}, u32[]{:S(2)}) collective-permute-start(f32[256,256]{1,0:T(8,128)S(1)} %fusion.1), channel_id=1, source_target_pairs={{0,4},{4,0},{1,5},{5,1},{2,6},{6,2},{3,7},{7,3}} | collective-permute-start | bytes 786440 | tf_op jit(solution)/shard_map/ppermute | solution.py:413
  370.5 32.4 %copy-start.10 = (f32[256,256]{1,0:T(8,128)}, f32[256,256]{1,0:T(8,128)S(1)}, u32[]{:S(2)}) copy-start(f32[256,256]{1,0:T(8,128)S(1)} %collective-permute-done.13) | copy-start | bytes 786436
  370.5 32.7 %collective-permute-start.30 = (f32[3,512,256]{2,1,0:T(8,128)}, f32[3,512,256]{2,1,0:T(8,128)S(1)}, u32[]{:S(2)}, u32[]{:S(2)}) collective-permute-start(f32[3,512,256]{2,1,0:T(8,128)} %collective-permute-done.29.refs_4_), channel_id=1, source_target_pairs={{0,1},{1,0},{2,3},{3,2},{4,5},{5,4},{6,7},{7,6}} | collective-permute-start | bytes 4718600 | tf_op jit(solution)/shard_map/ppermute | solution.py:412
  370.5 33.0 %collective-permute-start.32 = (f32[3,512,256]{2,1,0:T(8,128)}, f32[3,512,256]{2,1,0:T(8,128)S(1)}, u32[]{:S(2)}, u32[]{:S(2)}) collective-permute-start(f32[3,512,256]{2,1,0:T(8,128)} %collective-permute-done.31.refs_5_), channel_id=1, source_target_pairs={{0,1},{1,0},{2,3},{3,2},{4,5},{5,4},{6,7},{7,6}} | collective-permute-start | bytes 4718600 | tf_op jit(solution)/shard_map/ppermute | solution.py:412
  372.3 27.7 %collective-permute-start.16 = (f32[256,384]{1,0:T(8,128)S(1)}, f32[256,384]{1,0:T(8,128)S(1)}, u32[]{:S(2)}, u32[]{:S(2)}) collective-permute-start(f32[256,384]{1,0:T(8,128)S(1)} %bitcast_add_fusion), channel_id=1, source_target_pairs={{0,2},{1,3},{2,0},{3,1},{4,6},{5,7},{6,4},{7,5}} | collective-permute-start | bytes 1179656 | tf_op jit(solution)/shard_map/ppermute | solution.py:411
  400.0 2.9 collective-permute-start.28
  401.4 11.5 %collective-permute-start.17 = (f32[256,384]{1,0:T(8,128)S(1)}, f32[256,384]{1,0:T(8,128)S(1)}, u32[]{:S(2)}, u32[]{:S(2)}) collective-permute-start(f32[256,384]{1,0:T(8,128)S(1)} %fusion), channel_id=1, source_target_pairs={{0,4},{4,0},{1,5},{5,1},{2,6},{6,2},{3,7},{7,3}} | collective-permute-start | bytes 1179656 | tf_op jit(solution)/shard_map/ppermute | solution.py:413
  402.9 10.0 %copy-start.6 = (f32[2,512,256]{2,1,0:T(8,128)}, f32[2,512,256]{2,1,0:T(8,128)S(1)}, u32[]{:S(2)}) copy-start(f32[2,512,256]{2,1,0:T(8,128)S(1)} %collective-permute-done.28.refs_3_) | copy-start | bytes 3145732
  402.9 40.4 %collective-permute-start.18 = (f32[4,512,256]{2,1,0:T(8,128)}, f32[4,512,256]{2,1,0:T(8,128)S(1)}, u32[]{:S(2)}, u32[]{:S(2)}) collective-permute-start(f32[4,512,256]{2,1,0:T(8,128)} %get-tuple-element.103.refs_0_), channel_id=1, source_target_pairs={{0,1},{1,0},{2,3},{3,2},{4,5},{5,4},{6,7},{7,6}} | collective-permute-start | bytes 6291464 | tf_op jit(solution)/shard_map/ppermute | solution.py:412
  403.2 9.7 %copy-start.3 = (f32[3,512,256]{2,1,0:T(8,128)}, f32[3,512,256]{2,1,0:T(8,128)S(1)}, u32[]{:S(2)}) copy-start(f32[3,512,256]{2,1,0:T(8,128)S(1)} %collective-permute-done.30.refs_4_) | copy-start | bytes 4718596
  403.2 40.1 %collective-permute-start.19 = (f32[4,512,256]{2,1,0:T(8,128)}, f32[4,512,256]{2,1,0:T(8,128)}, u32[]{:S(2)}, u32[]{:S(2)}) collective-permute-start(f32[4,512,256]{2,1,0:T(8,128)} %get-tuple-element.104.refs_1_), channel_id=1, source_target_pairs={{0,1},{1,0},{2,3},{3,2},{4,5},{5,4},{6,7},{7,6}} | collective-permute-start | bytes 6291464 | tf_op jit(solution)/shard_map/ppermute | solution.py:412
  403.5 9.5 %copy-start.4 = (f32[3,512,256]{2,1,0:T(8,128)}, f32[3,512,256]{2,1,0:T(8,128)S(1)}, u32[]{:S(2)}) copy-start(f32[3,512,256]{2,1,0:T(8,128)S(1)} %collective-permute-done.32.refs_5_) | copy-start | bytes 4718596
  403.5 39.8 %collective-permute-start.21 = (f32[4,512,256]{2,1,0:T(8,128)}, f32[4,512,256]{2,1,0:T(8,128)}, u32[]{:S(2)}, u32[]{:S(2)}) collective-permute-start(f32[4,512,256]{2,1,0:T(8,128)} %collective-permute-done.20.refs_2_), channel_id=1, source_target_pairs={{0,1},{1,0},{2,3},{3,2},{4,5},{5,4},{6,7},{7,6}} | collective-permute-start | bytes 6291464 | tf_op jit(solution)/shard_map/ppermute | solution.py:412
  412.9 6.8 %copy-start.8 = (f32[256,384]{1,0:T(8,128)}, f32[256,384]{1,0:T(8,128)S(1)}, u32[]{:S(2)}) copy-start(f32[256,384]{1,0:T(8,128)S(1)} %collective-permute-done.17) | copy-start | bytes 1179652
  412.9 30.4 %collective-permute-start.23 = (f32[4,512,256]{2,1,0:T(8,128)}, f32[4,512,256]{2,1,0:T(8,128)}, u32[]{:S(2)}, u32[]{:S(2)}) collective-permute-start(f32[4,512,256]{2,1,0:T(8,128)} %collective-permute-done.22.refs_3_), channel_id=1, source_target_pairs={{0,1},{1,0},{2,3},{3,2},{4,5},{5,4},{6,7},{7,6}} | collective-permute-start | bytes 6291464 | tf_op jit(solution)/shard_map/ppermute | solution.py:412
  419.7 8.2 %copy-start.11 = (f32[256,256]{1,0:T(8,128)S(1)}, f32[256,256]{1,0:T(8,128)}, u32[]{:S(2)}) copy-start(f32[256,256]{1,0:T(8,128)} %copy-done.10) | copy-start | bytes 786436
  434.6 6.7 %copy-start.9 = (f32[256,384]{1,0:T(8,128)S(1)}, f32[256,384]{1,0:T(8,128)}, u32[]{:S(2)}) copy-start(f32[256,384]{1,0:T(8,128)} %copy-done.8) | copy-start | bytes 1179652
  443.3 1.3 copy-start.2

commit v4 on v3

--- a/solution.py
+++ b/solution.py
@@ -146,19 +146,19 @@
 sds = jax.ShapeDtypeStruct
 
 
-def group_call(count, cp_half, scale, idx, c_all, ct_all, r_all, rt_all, w_k, w_v, q_all, q_oth, do_all, do_oth, carried):
+def group_call(first, count, cp_half, scale, idx, c_all, ct_all, r_all, rt_all, w_k, w_v, q_all, q_oth, do_all, do_oth, carried):
     seq, rank = c_all.shape
     d_r = r_all.shape[1]
     half_heads, d_qk, tok = q_oth.shape
     d_v = do_oth.shape[2]
     kv = w_k.shape[2] + w_v.shape[2]
     whole = lambda *shape: pl.BlockSpec(shape, lambda h, idx: (0,) * len(shape), pipeline_mode=pl.Buffered(1))
-    mine = lambda *shape: pl.BlockSpec((1,) + shape, lambda h, idx: (idx[1] * half_heads + idx[2] + h, 0, 0))
-    part = lambda *shape: pl.BlockSpec((1,) + shape, lambda h, idx: (idx[2] + h, 0, 0))
+    mine = lambda *shape: pl.BlockSpec((1,) + shape, lambda h, idx: (idx[1] * half_heads + first + h, 0, 0))
+    part = lambda *shape: pl.BlockSpec((1,) + shape, lambda h, idx: (first + h, 0, 0))
     in_specs = [whole(seq, rank), whole(rank, seq), whole(seq, d_r), whole(d_r, seq),
                 part(rank, w_k.shape[2]), part(rank, d_v), mine(d_qk, tok), part(d_qk, tok), part(tok, d_v), part(tok, d_v)]
     out_specs = [part(tok, d_v), part(tok, d_v), mine(d_qk, tok), part(d_qk, tok),
-                 pl.BlockSpec((seq, kv), lambda h, idx: (0, idx[2] + h)),
+                 pl.BlockSpec((seq, kv), lambda h, idx: (0, first + h)),
                  pl.BlockSpec((seq, d_r), lambda h, idx: (0, 0)),
                  pl.BlockSpec((1, rank, kv), lambda h, idx: (h, 0, 0))]
     out_shape = [sds((half_heads, tok, d_v), BF16), sds((half_heads, tok, d_v), BF16),
@@ -196,7 +196,7 @@
 
 def dc_kernel(idx_ref, lo_ref, hi_ref, wk_ref, wv_ref, dr_lo, dr_hi, *refs):
     sends, keeps, w_s = refs[0:2], refs[2:4], refs[4]
-    heads, _, d_n = wk_ref.shape
+    heads, rank, d_n = wk_ref.shape
     i = pl.program_id(0)
 
     @pl.when(i == 0)
@@ -206,18 +206,23 @@
             w_s[:, (2 * g + 1) * d_n:(2 * g + 2) * d_n] = wv_ref[g]
 
     def fill(outs):
-        for j, ref in enumerate(outs):
-            for k, (dkv_ref, dr_ref) in enumerate(((lo_ref, dr_lo), (hi_ref, dr_hi))):
-                ref[0, k, :, 0:PIECE] = dot_t(dkv_ref[...], w_s[rows(j), :])
-                if j == 1:
-                    dr = dr_ref[...]
-                    ref[0, k, :, PIECE:] = jnp.concatenate([dr, jnp.zeros_like(dr)], axis=1)
+        wide, slim = outs
+        split = wide.shape[3]
+        for k, (dkv_ref, dr_ref) in enumerate(((lo_ref, dr_lo), (hi_ref, dr_hi))):
+            for j in range(0, rank, PIECE):
+                dc = dot_t(dkv_ref[...], w_s[j:j + PIECE, :])
+                n_wide = min(split - j, PIECE)
+                wide[0, k, :, j:j + n_wide] = dc[:, :n_wide]
+                if n_wide < PIECE:
+                    slim[0, k, :, 0:rank - split] = dc[:, n_wide:]
+            dr = dr_ref[...]
+            slim[0, k, :, rank - split:] = jnp.concatenate([dr, jnp.zeros_like(dr)], axis=1)
 
     pl.when(i < 2)(functools.partial(fill, sends))
     pl.when(i >= 2)(functools.partial(fill, keeps))
 
 
-def dc_call(idx, dkv, w_k, w_v, dr):
+def dc_call(split, idx, dkv, w_k, w_v, dr):
     seq, d_r = dr.shape
     half_heads, rank, d_n = w_k.shape
     kv = d_n + w_v.shape[2]
@@ -226,7 +231,7 @@
     lo = lambda w: pl.BlockSpec((PIECE, w), lambda i, idx: (dev(i, idx), 0))
     hi = lambda w: pl.BlockSpec((PIECE, w), lambda i, idx: (2 * n - 1 - dev(i, idx), 0))
     w_spec = pl.BlockSpec((half_heads, rank, d_n), lambda i, idx: (0, 0, 0), pipeline_mode=pl.Buffered(1))
-    shapes = [(n // 2, 2, PIECE, rank // 2), (n // 2, 2, PIECE, rank // 2 + 2 * d_r)] * 2
+    shapes = [(n // 2, 2, PIECE, split), (n // 2, 2, PIECE, rank - split + 2 * d_r)] * 2
     maps = [lambda i, idx: (jnp.minimum(i, 1), 0, 0, 0)] * 2 + [lambda i, idx: (jnp.maximum(i - 2, 0), 0, 0, 0)] * 2
     return pl.pallas_call(
         dc_kernel,
@@ -278,27 +283,22 @@
 
 
 def relay_kernel(idx_ref, *refs):
-    wide_s = refs[-1]
     n = len(refs) // 2
-    for in_ref, out_ref in zip(refs[:n], refs[n:-1]):
-        heads, rows_n, d = out_ref.shape
-        wide_s[...] = in_ref[...].astype(F32).reshape(rows_n * heads, d)
-        for h in range(heads):
-            out_ref[h] = wide_s[pl.ds(h, rows_n, stride=heads), :].astype(BF16)
+    for in_ref, out_ref in zip(refs[:n], refs[n:]):
+        out_ref[...] = jnp.swapaxes(in_ref[...], 0, 1)
 
 
 def relay_call(idx, w_uk, w_uv, d_out):
     tok, n_heads, d = d_out.shape
     heads = n_heads // 2
-    n = 128
+    n = 256
     near = pl.BlockSpec((n, heads, d), lambda i, idx: (i, idx[1], 0))
     away = pl.BlockSpec((n, heads, d), lambda i, idx: (i, 1 - idx[1], 0))
     return pl.pallas_call(
         relay_kernel,
         grid_spec=pltpu.PrefetchScalarGridSpec(
             num_scalar_prefetch=1, grid=(tok // n,), in_specs=[away, near, near, near],
-            out_specs=[pl.BlockSpec((heads, n, d), lambda i, idx: (0, i, 0))] * 4,
-            scratch_shapes=[pltpu.VMEM((n * heads, d), F32)]),
+            out_specs=[pl.BlockSpec((heads, n, d), lambda i, idx: (0, i, 0))] * 4),
         out_shape=[sds((heads, tok, d), BF16)] * 4,
         compiler_params=params(60),
         cost_estimate=pl.CostEstimate(flops=10 ** 9, bytes_accessed=16 * d_out.size, transcendentals=0),
@@ -306,25 +306,22 @@
     )(idx, d_out, d_out, w_uk, w_uv)
 
 
-def out_kernel(idx_ref, own_ref, oth_ref, out_ref, wide_s):
+def out_kernel(idx_ref, own_ref, oth_ref, out_ref):
     core = idx_ref[1]
-    heads, n, d = own_ref.shape
+    heads = own_ref.shape[0]
     for side, ref in ((core, own_ref), (1 - core, oth_ref)):
-        for h in range(heads):
-            wide_s[pl.ds(h, n, stride=heads), :] = ref[h].astype(F32)
-        out_ref[:, pl.ds(pl.multiple_of(side * heads, heads), heads), :] = wide_s[...].reshape(n, heads, d).astype(BF16)
+        out_ref[:, pl.ds(pl.multiple_of(side * heads, heads), heads), :] = jnp.swapaxes(ref[...], 0, 1)
 
 
 def out_call(idx, own, oth):
     heads, tok, d = own.shape
-    n = 128
+    n = 256
     part = pl.BlockSpec((heads, n, d), lambda i, idx: (0, i, 0))
     return pl.pallas_call(
         out_kernel,
         grid_spec=pltpu.PrefetchScalarGridSpec(
             num_scalar_prefetch=1, grid=(tok // n,), in_specs=[part, part],
-            out_specs=pl.BlockSpec((n, 2 * heads, d), lambda i, idx: (i, 0, 0)),
-            scratch_shapes=[pltpu.VMEM((n * heads, d), F32)]),
+            out_specs=pl.BlockSpec((n, 2 * heads, d), lambda i, idx: (i, 0, 0))),
         out_shape=sds((tok, 2 * heads, d), BF16),
         compiler_params=params(60),
         cost_estimate=pl.CostEstimate(flops=10 ** 9, bytes_accessed=4 * own.size * 2, transcendentals=0),
@@ -355,24 +352,25 @@
 def join_kernel(n_parts, idx_ref, *refs):
     a_refs, b_refs = refs[:n_parts], refs[n_parts:2 * n_parts]
     k_ref, v_ref = refs[-2:]
-    d_n = k_ref.shape[2]
+    n_rows, heads, d_n = k_ref.shape
     h = 0
     for a_ref, b_ref in zip(a_refs, b_refs):
         for g in range(a_ref.shape[0]):
             s = a_ref[g] + b_ref[g]
-            k_ref[:, h, :] = s[:, :d_n]
-            v_ref[:, h, :] = s[:, d_n:]
+            at = pl.ds(h, n_rows, stride=heads)
+            k_ref.reshape(n_rows * heads, d_n)[at, :] = s[:, :d_n]
+            v_ref.reshape(n_rows * heads, d_n)[at, :] = s[:, d_n:]
             h += 1
 
 
-def join_call(block, parts_a, parts_b, carried, n_heads):
+def join_call(idx, block, parts_a, parts_b, carried, n_heads):
     rank, kv = parts_a[0].shape[1:]
     n_parts = len(parts_a)
     heads = sum(p.shape[0] for p in parts_a)
-    r_blk = 128
+    r_blk = 256
     parts = [pl.BlockSpec((p.shape[0], r_blk, kv), lambda i, idx: (0, i, 0)) for p in parts_a]
-    out = pl.BlockSpec((r_blk, heads, kv // 2), lambda i, idx: (i, idx[0], 0))
-    args = [block, *parts_a, *parts_b, *carried]
+    out = pl.BlockSpec((r_blk, heads, kv // 2), lambda i, idx: (i, block(idx[1]), 0))
+    args = [idx, *parts_a, *parts_b, *carried]
     return pl.pallas_call(
         functools.partial(join_kernel, n_parts),
         grid_spec=pltpu.PrefetchScalarGridSpec(
@@ -404,6 +402,7 @@
         n_heads = q_heads.shape[1]
         half_heads = n_heads // 2
         d_r = k_rope.shape[1]
+        d_n = w_uk.shape[2]
         scale = q_heads.shape[2] ** -0.5
         me = lax.axis_index('cp')
         chip, core = me // 2, me % 2
@@ -427,8 +426,7 @@
         carried, own, far, near, far_near = (), [], [], [], []
         first = 0
         for count in sum(GROUPS, ()):
-            idx_g = jnp.stack([chip, core, jnp.int32(first)]).astype(jnp.int32)
-            outs = group_call(count, cp_half, scale, idx_g, c_all, ct_all, r_all, rt_all, w_k, w_v,
+            outs = group_call(first, count, cp_half, scale, idx, c_all, ct_all, r_all, rt_all, w_k, w_v,
                       q_all, q_oth, do_all, do_oth, carried)
             carried = outs[:6]
             own.append(outs[6])
@@ -443,24 +441,25 @@
             return cut(pos) + [swap(functools.reduce(jnp.add, cut(1 - pos)))]
 
         full = []
-        dc_out = dc_call(idx, dkv, w_k, w_v, dr)
+        split = rank - d_n
+        dc_out = dc_call(split, idx, dkv, w_k, w_v, dr)
         for half in range(2):
             arrs = [dc_out[2 + half], swap_core(dc_out[half])]
             arrs = fold(arrs, 1, my_tp, swap_tp)
             part = functools.reduce(jnp.add, fold(arrs, 0, chip, swap_x))
             mate = swap_tp(part)
             full.append(jnp.where(my_tp == 0, jnp.concatenate([part, mate], axis=0), jnp.concatenate([mate, part], axis=0)))
-        dc = jnp.concatenate([full[0], full[1][:, :rank // 2]], axis=1)
-        dr_out = full[1][:, rank // 2:rank // 2 + d_r]
+        dc = jnp.concatenate([full[0], full[1][:, :rank - split]], axis=1)
+        dr_out = full[1][:, rank - split:rank - split + d_r]
 
         dws, g0 = (), 0
         for i, groups in enumerate(GROUPS):
             sel = slice(g0, g0 + len(groups))
             g0 += len(groups)
-            for side, a, b in ((core, own, far), (1 - core, near, far_near)):
-                block = (side * len(GROUPS) + i).reshape(1).astype(jnp.int32)
-                dws = join_call(block, a[sel], b[sel], dws, n_heads)
-        dq = place_call(idx, swap_core(dq_oth), dq_full, 2).transpose(2, 0, 1)
+            for s, (a, b) in enumerate(((own, far), (near, far_near))):
+                block = lambda c, i=i, s=s: (1 - c if s else c) * len(GROUPS) + i
+                dws = join_call(idx, block, a[sel], b[sel], dws, n_heads)
+        dq = place_call(idx, swap_core(dq_oth), dq_full, 8).transpose(2, 0, 1)
         out = out_call(idx, o_own, swap_core(o_oth))
         return (out, dq, dc, dr_out, *dws)
 

time: 464 us -> 451 us (0.972)
  Pallas kernels: 211 us -> 198 us
  transfers between devices with their start and end apart: 33 -> 33, of which waited for: 11 -> 11; matrix products, arithmetic and copies ran while one was open for 3% -> 2% of each run, Pallas kernels for 11% -> 9%
where the time goes in v4:
time: 451 us; the launch traced here: 448 us
  waiting for transfers between devices  205 us (45%)
  Pallas kernels  198 us (44%)
  starting transfers between devices  24.7 us (5%)
  local copies, waits for them, and re-layouts  9.44 us (2%)
  other arithmetic  9.41 us (2%)
    ppermute x9, waiting for transfers between devices, device_fn(): swap_x = lambda a: lax.ppermute(a, 'cp', x_perm)  174 us
    pallas_call x5, Pallas kernels, group_call(): pl.pallas_call(functools.partial(group_kernel, cp_half, scale, len(carrie...  133 us
    ppermute x4, waiting for transfers between devices, device_fn(): swap_tp = lambda a: lax.ppermute(a, 'tp', tp_perm)  28.4 us
    pallas_call x4, Pallas kernels, join_call(): pl.pallas_call(functools.partial(join_kernel, n_parts), grid_spec=pltpu.P...  24.4 us
    pallas_call x1, Pallas kernels, dc_call(): pl.pallas_call(dc_kernel, grid_spec=pltpu.PrefetchScalarGridSpec(num_scal...  17.8 us
    ppermute x9, starting transfers between devices, device_fn(): swap_x = lambda a: lax.ppermute(a, 'cp', x_perm)  15.8 us
  transfers between devices with their start and end apart: 33, of which 11 were waited for; matrix products, arithmetic and copies ran while one was open for 2% of the time, Pallas kernels for 9%

profile of v4, /device:TPU:0, one launch (start us, length us, event | category | flops | bytes accessed | tf_op | source)
XLA Modules:
  0.0 447.6 jit_solution(10207815729017375901)
XLA Ops:
  0.7 3.8 dynamic-slice_bitcast_fusion
  4.5 0.8 collective-permute-start.6
  5.3 0.6 pad_add_fusion.idx_ref
  5.9 7.5 %relay.1 = (bf16[16,512,128]{2,1,0:T(8,128)(2,1)}, bf16[16,512,128]{2,1,0:T(8,128)(2,1)}, bf16[16,512,128]{2,1,0:T(8,128)(2,1)}, bf16[16,512,128]{2,1,0:T(8,128)(2,1)}) custom-call(s32[2]{0:T(128)} %pad_add_fusion.idx_ref, bf16[512,32,128]{2,1,0:T(8,128)(2,1)} %refs_1_.1, bf16[512,32,128]{2,1,0:T(8,128)(2,1)} %refs_1_.1, bf16[512,32,128]{2,1,0:T(8,128)(2,1)} %refs_2_.1, ...), custom_call_target="tpu_custom_call" | custom-call | flops 1000000000 | bytes 33554432 | tf_op jit(solution)/shard_map/relay/pallas_call | solution.py:297
  13.4 3.0 collective-permute-start.1
  16.4 12.1 %collective-permute-done.1.refs_2_ = bf16[512,512]{1,0:T(8,128)(2,1)S(1)} collective-permute-done((bf16[512,512]{1,0:T(8,128)(2,1)S(1)}, bf16[512,512]{1,0:T(8,128)(2,1)S(1)}, u32[]{:S(2)}, u32[]{:S(2)}) %collective-permute-start.1) | collective-permute-done | bytes 524320 | tf_op jit(solution)/shard_map/ppermute | solution.py:410
  28.5 0.5 collective-permute-start.3
  29.0 1.5 collective-permute-done.3.refs_5_
  30.6 1.7 collective-permute-start.4
  32.3 2.5 collective-permute-done.4.refs_6_
  34.9 1.3 collective-permute-done.5.refs_7_
  36.1 0.8 copy-done.13
  36.9 5.1 %gather.1 = (bf16[2048,512]{1,0:T(8,128)(2,1)}, bf16[512,2048]{1,0:T(8,128)(2,1)}, bf16[2048,64]{1,0:T(8,128)(2,1)}, bf16[64,2048]{1,0:T(8,128)(2,1)}) custom-call(s32[2]{0:T(128)} %pad_add_fusion.idx_ref, bf16[512,512]{1,0:T(8,128)(2,1)} %refs_0_.2, bf16[512,512]{1,0:T(8,128)(2,1)} %copy-done.13, bf16[512,512]{1,0:T(8,128)(2,1)} %copy-done.12, ...), custom_call_target="tpu_custom_call" | custom-call | flops 1000000000 | bytes 8388608 | tf_op jit(solution)/shard_map/gather/pallas_call | solution.py:272
  42.1 1.7 copy-done
  43.7 18.5 %heads.5 = (bf16[16,512,128]{2,1,0:T(8,128)(2,1)}, bf16[16,512,128]{2,1,0:T(8,128)(2,1)}, f32[32,192,512]{2,1,0:T(8,128)}, f32[16,192,512]{2,1,0:T(8,128)}, bf16...) custom-call(s32[2]{0:T(128)} %pad_add_fusion.idx_ref, ...), custom_call_target="tpu_custom_call" | custom-call | flops 7751073792 | bytes 8388608 | tf_op jit(solution)/shard_map/heads/pallas_call | solution.py:177
  62.3 25.6 %heads.6 = (bf16[16,512,128]{2,1,0:T(8,128)(2,1)}, bf16[16,512,128]{2,1,0:T(8,128)(2,1)}, f32[32,192,512]{2,1,0:T(8,128)}, f32[16,192,512]{2,1,0:T(8,128)}, bf16...) custom-call(s32[2]{0:T(128)} %pad_add_fusion.idx_ref, ...), custom_call_target="tpu_custom_call", output_to_operand_aliasing={{0}: (11, {}), {1}: (12, {}), {2}: (13, {}), {3}: (14, {}),... | custom-call | flops 11626610688 | bytes 12582912 | tf_op jit(solution)/shard_map/heads/pallas_call | solution.py:177
  87.9 25.3 %heads.7 = (bf16[16,512,128]{2,1,0:T(8,128)(2,1)}, bf16[16,512,128]{2,1,0:T(8,128)(2,1)}, f32[32,192,512]{2,1,0:T(8,128)}, f32[16,192,512]{2,1,0:T(8,128)}, bf16...) custom-call(s32[2]{0:T(128)} %pad_add_fusion.idx_ref, ...), custom_call_target="tpu_custom_call", output_to_operand_aliasing={{0}: (11, {}), {1}: (12, {}), {2}: (13, {}), {3}: (14, {}),... | custom-call | flops 11626610688 | bytes 12582912 | tf_op jit(solution)/shard_map/heads/pallas_call | solution.py:177
  113.2 31.7 %heads.8 = (bf16[16,512,128]{2,1,0:T(8,128)(2,1)}, bf16[16,512,128]{2,1,0:T(8,128)(2,1)}, f32[32,192,512]{2,1,0:T(8,128)}, f32[16,192,512]{2,1,0:T(8,128)}, bf16...) custom-call(s32[2]{0:T(128)} %pad_add_fusion.idx_ref, ...), custom_call_target="tpu_custom_call", output_to_operand_aliasing={{0}: (11, {}), {1}: (12, {}), {2}: (13, {}), {3}: (14, {}),... | custom-call | flops 15502147584 | bytes 16777216 | tf_op jit(solution)/shard_map/heads/pallas_call | solution.py:177
  144.9 31.9 %heads.9 = (bf16[16,512,128]{2,1,0:T(8,128)(2,1)}, bf16[16,512,128]{2,1,0:T(8,128)(2,1)}, f32[32,192,512]{2,1,0:T(8,128)}, f32[16,192,512]{2,1,0:T(8,128)}, bf16...) custom-call(s32[2]{0:T(128)} %pad_add_fusion.idx_ref, ...), custom_call_target="tpu_custom_call", output_to_operand_aliasing={{0}: (11, {}), {1}: (12, {}), {2}: (13, {}), {3}: (14, {}),... | custom-call | flops 15502147584 | bytes 16777216 | tf_op jit(solution)/shard_map/heads/pallas_call | solution.py:177
  176.8 17.8 %dc.1 = (f32[2,2,256,384]{3,2,1,0:T(8,128)}, f32[2,2,256,256]{3,2,1,0:T(8,128)}, f32[2,2,256,384]{3,2,1,0:T(8,128)}, f32[2,2,256,256]{3,2,1,0:T(8,128)}) custom-call(s32[2]{0:T(128)} %pad_add_fusion.idx_ref, bf16[2048,4096]{1,0:T(8,128)(2,1)} %get-tuple-element.97.lo_ref.hi_ref, bf16[2048,4096]{1,0:T(8,128)(2,1)} %get-tuple-element.97.lo_ref.hi_ref, ...), custom_call_target="tpu_custom_call" | custom-call | flops 8589934592 | bytes 31457280 | tf_op jit(solution)/shard_map/dc/pallas_call | solution.py:236
  194.5 0.1 collective-permute-start.14
  194.7 0.4 collective-permute-start.24
  195.1 0.1 collective-permute-start.10
  195.2 0.4 collective-permute-start.25
  195.6 2.8 collective-permute-start.27
  198.4 1.3 add_bitcast_fusion.1
  199.7 1.6 collective-permute-start.15
  201.2 20.7 %collective-permute-done.27.refs_3_ = f32[2,512,256]{2,1,0:T(8,128)} collective-permute-done((f32[2,512,256]{2,1,0:T(8,128)S(1)}, f32[2,512,256]{2,1,0:T(8,128)}, u32[]{:S(2)}, u32[]{:S(2)}) %collective-permute-start.27) | collective-permute-done | bytes 1048608 | tf_op jit(solution)/shard_map/ppermute | solution.py:410
  222.0 1.7 collective-permute-start.29
  223.8 0.3 collective-permute-start.31
  224.1 0.2 collective-permute-start.8
  224.3 0.2 copy-done.8
  224.5 1.5 collective-permute-start.20
  226.0 1.2 bitcast_add_fusion.2
  227.2 32.4 %collective-permute-done.29.refs_4_ = f32[3,512,256]{2,1,0:T(8,128)} collective-permute-done((f32[3,512,256]{2,1,0:T(8,128)}, f32[3,512,256]{2,1,0:T(8,128)}, u32[]{:S(2)}, u32[]{:S(2)}) %collective-permute-start.29) | collective-permute-done | bytes 1572896 | tf_op jit(solution)/shard_map/ppermute | solution.py:410
  259.6 1.7 collective-permute-start.16
  261.3 32.0 %collective-permute-done.31.refs_5_ = f32[3,512,256]{2,1,0:T(8,128)} collective-permute-done((f32[3,512,256]{2,1,0:T(8,128)}, f32[3,512,256]{2,1,0:T(8,128)}, u32[]{:S(2)}, u32[]{:S(2)}) %collective-permute-start.31) | collective-permute-done | bytes 1572896 | tf_op jit(solution)/shard_map/ppermute | solution.py:410
  293.3 1.7 collective-permute-start.22
  295.0 1.5 add_bitcast_fusion
  296.5 47.3 %collective-permute-done.16 = f32[256,256]{1,0:T(8,128)S(1)} collective-permute-done((f32[256,256]{1,0:T(8,128)S(1)}, f32[256,256]{1,0:T(8,128)S(1)}, u32[]{:S(2)}, u32[]{:S(2)}) %collective-permute-start.16) | collective-permute-done | bytes 262176 | tf_op jit(solution)/shard_map/ppermute | solution.py:410
  343.7 1.5 collective-permute-start.11
  345.2 1.2 fusion.1
  346.4 0.5 collective-permute-start.17
  347.0 19.2 %collective-permute-done.17 = f32[256,256]{1,0:T(8,128)S(1)} collective-permute-done((f32[256,256]{1,0:T(8,128)S(1)}, f32[256,256]{1,0:T(8,128)S(1)}, u32[]{:S(2)}, u32[]{:S(2)}) %collective-permute-start.17) | collective-permute-done | bytes 262176 | tf_op jit(solution)/shard_map/ppermute | solution.py:412
  366.1 0.5 collective-permute-start.32
  366.6 1.3 bitcast_add_fusion
  367.9 1.2 collective-permute-start.12
  369.1 26.6 %collective-permute-done.12 = f32[256,384]{1,0:T(8,128)S(1)} collective-permute-done((f32[256,384]{1,0:T(8,128)S(1)}, f32[256,384]{1,0:T(8,128)S(1)}, u32[]{:S(2)}, u32[]{:S(2)}) %collective-permute-start.12) | collective-permute-done | bytes 393248 | tf_op jit(solution)/shard_map/ppermute | solution.py:410
  395.7 1.3 fusion
  397.0 1.5 collective-permute-start.13
  398.6 0.2 collective-permute-start.18
  398.8 0.3 collective-permute-start.19
  399.1 0.2 collective-permute-start.21
  399.3 9.3 %collective-permute-done.13 = f32[256,384]{1,0:T(8,128)S(1)} collective-permute-done((f32[256,384]{1,0:T(8,128)S(1)}, f32[256,384]{1,0:T(8,128)S(1)}, u32[]{:S(2)}, u32[]{:S(2)}) %collective-permute-start.13) | collective-permute-done | bytes 393248 | tf_op jit(solution)/shard_map/ppermute | solution.py:412
  408.6 0.8 copy-done.9
  409.4 6.1 %join.4 = (f32[512,32,128]{2,1,0:T(8,128)}, f32[512,32,128]{2,1,0:T(8,128)}) custom-call(s32[2]{0:T(128)} %pad_add_fusion.idx_ref, f32[2,512,256]{2,1,0:T(8,128)} %get-tuple-element.105.refs_0_, f32[3,512,256]{2,1,0:T(8,128)} %get-tuple-element.106.refs_1_, f32[3,512,256]{2,1,0:T(8,128)} %get-tuple-element.107.refs_2_, ...), custom_call_target="tpu_custom_call" | custom-call | flops 1000000000 | bytes 12582912 | tf_op jit(solution)/shard_map/join/pallas_call | solution.py:374
  415.5 0.8 copy.43
  416.3 4.9 %out.1 = bf16[512,32,128]{2,1,0:T(8,128)(2,1)} custom-call(s32[2]{0:T(128)} %pad_add_fusion.idx_ref, bf16[16,512,128]{2,1,0:T(8,128)(2,1)} %get-tuple-element.93.own_ref, bf16[16,512,128]{2,1,0:T(8,128)(2,1)} %collective-permute-done.8.oth_ref), custom_call_target="tpu_custom_call" | custom-call | flops 1000000000 | bytes 8388608 | tf_op jit(solution)/shard_map/out/pallas_call | solution.py:320
  421.2 6.1 %join.5 = (f32[512,32,128]{2,1,0:T(8,128)}, f32[512,32,128]{2,1,0:T(8,128)}) custom-call(s32[2]{0:T(128)} %pad_add_fusion.idx_ref, f32[2,512,256]{2,1,0:T(8,128)} %collective-permute-done.24.refs_0_, f32[3,512,256]{2,1,0:T(8,128)} %collective-permute-done.25.refs_1_, ...), custom_call_target="tpu_custom_call", output_to_operand_aliasing={{0}: (7, {}), {1}: (8, {})} | custom-call | flops 1000000000 | bytes 12582912 | tf_op jit(solution)/shard_map/join/pallas_call | solution.py:374
  427.2 6.2 %join.6 = (f32[512,32,128]{2,1,0:T(8,128)}, f32[512,32,128]{2,1,0:T(8,128)}) custom-call(s32[2]{0:T(128)} %pad_add_fusion.idx_ref, f32[4,512,256]{2,1,0:T(8,128)} %get-tuple-element.103.refs_0_, f32[4,512,256]{2,1,0:T(8,128)} %get-tuple-element.104.refs_1_, ...), custom_call_target="tpu_custom_call", output_to_operand_aliasing={{0}: (5, {}), {1}: (6, {})} | custom-call | flops 1000000000 | bytes 12582912 | tf_op jit(solution)/shard_map/join/pallas_call | solution.py:374
  433.5 1.1 pad_maximum_fusion
  434.6 1.3 copy-done.3
  435.9 6.1 %join.7 = (f32[512,32,128]{2,1,0:T(8,128)}, f32[512,32,128]{2,1,0:T(8,128)}) custom-call(s32[2]{0:T(128)} %pad_add_fusion.idx_ref, f32[4,512,256]{2,1,0:T(8,128)} %copy-done.3, f32[4,512,256]{2,1,0:T(8,128)} %collective-permute-done.19.refs_1_, f32[4,512,256]{2,1,0:T(8,128)} %collective-permute-done.21.refs_2_, ...), custom_call_target="tpu_custom_call", output_to_operand_aliasing={{0}: (5, {}), {1}: (6, {})} | custom-call | flops 1000000000 | bytes 12582912 | tf_op jit(solution)/shard_map/join/pallas_call | solution.py:374
  441.9 5.5 %place.1 = f32[32,192,512]{2,1,0:T(8,128)} custom-call(s32[2]{0:T(128)} %pad_add_fusion.idx_ref, f32[16,192,512]{2,1,0:T(8,128)} %collective-permute-done.9.part_ref, f32[32,192,512]{2,1,0:T(8,128)} %get-tuple-element.96.full_ref), custom_call_target="tpu_custom_call", output_to_operand_aliasing={{}: (2, {})} | custom-call | flops 1000000000 | bytes 12582912 | tf_op jit(solution)/shard_map/place/pallas_call | solution.py:338
  (67 shorter events, 0.3 us)
Async XLA Ops:
  4.5 37.6 %collective-permute-start.6 = (bf16[16,192,512]{2,1,0:T(8,128)(2,1)}, bf16[16,192,512]{2,1,0:T(8,128)(2,1)S(1)}, u32[]{:S(2)}, u32[]{:S(2)}) collective-permute-start(bf16[16,192,512]{2,1,0:T(8,128)(2,1)} %dynamic-slice_bitcast_fusion), channel_id=1, source_target_pairs={{0,1},{1,0},{2,3},{3,2},{4,5},{5,4},{6,7},{7,6}} | collective-permute-start | bytes 9437192 | tf_op jit(solution)/shard_map/ppermute | solution.py:411
  5.9 7.5 %copy-start.11 = (bf16[512,512]{1,0:T(8,128)(2,1)S(1)}, bf16[512,512]{1,0:T(8,128)(2,1)}, u32[]{:S(2)}) copy-start(bf16[512,512]{1,0:T(8,128)(2,1)} %refs_0_.2) | copy-start | bytes 1572868
  5.9 22.6 %copy-start.14 = (bf16[512,64]{0,1:T(8,128)(2,1)S(1)}, bf16[512,64]{0,1:T(8,128)(2,1)}, u32[]{:S(2)}) copy-start(bf16[512,64]{0,1:T(8,128)(2,1)} %param.7) | copy-start | bytes 196612
  13.4 28.6 %collective-permute-start.7 = (bf16[16,512,128]{2,1,0:T(8,128)(2,1)}, bf16[16,512,128]{2,1,0:T(8,128)(2,1)}, u32[]{:S(2)}, u32[]{:S(2)}) collective-permute-start(bf16[16,512,128]{2,1,0:T(8,128)(2,1)} %get-tuple-element.68), channel_id=1, source_target_pairs={{0,1},{1,0},{2,3},{3,2},{4,5},{5,4},{6,7},{7,6}} | collective-permute-start | bytes 6291464 | tf_op jit(solution)/shard_map/ppermute | solution.py:411
  13.4 15.1 %collective-permute-start.1 = (bf16[512,512]{1,0:T(8,128)(2,1)S(1)}, bf16[512,512]{1,0:T(8,128)(2,1)S(1)}, u32[]{:S(2)}, u32[]{:S(2)}) collective-permute-start(bf16[512,512]{1,0:T(8,128)(2,1)S(1)} %copy-done.11), channel_id=1, source_target_pairs={{0,2},{1,3},{2,0},{3,1},{4,6},{5,7},{6,4},{7,5}} | collective-permute-start | bytes 1572872 | tf_op jit(solution)/shard_map/ppermute | solution.py:410
  16.4 19.7 %collective-permute-start = (bf16[512,512]{1,0:T(8,128)(2,1)S(1)}, bf16[512,512]{1,0:T(8,128)(2,1)S(1)}, u32[]{:S(2)}, u32[]{:S(2)}) collective-permute-start(bf16[512,512]{1,0:T(8,128)(2,1)S(1)} %copy-done.11), channel_id=1, source_target_pairs={{0,1},{1,0},{2,3},{3,2},{4,5},{5,4},{6,7},{7,6}} | collective-permute-start | bytes 1572872 | tf_op jit(solution)/shard_map/ppermute | solution.py:411
  28.5 7.6 %copy-start.12 = (bf16[512,512]{1,0:T(8,128)(2,1)}, bf16[512,512]{1,0:T(8,128)(2,1)S(1)}, u32[]{:S(2)}) copy-start(bf16[512,512]{1,0:T(8,128)(2,1)S(1)} %collective-permute-done.1.refs_2_) | copy-start | bytes 1572868
  28.5 8.4 %collective-permute-start.2 = (bf16[512,512]{1,0:T(8,128)(2,1)S(1)}, bf16[512,512]{1,0:T(8,128)(2,1)}, u32[]{:S(2)}, u32[]{:S(2)}) collective-permute-start(bf16[512,512]{1,0:T(8,128)(2,1)S(1)} %collective-permute-done.1.refs_2_), channel_id=1, source_target_pairs={{0,1},{1,0},{2,3},{3,2},{4,5},{5,4},{6,7},{7,6}} | collective-permute-start | bytes 1572872 | tf_op jit(solution)/shard_map/ppermute | solution.py:411
  28.5 2.0 collective-permute-start.3
  30.6 6.3 %copy-start.15 = (bf16[64,512]{1,0:T(8,128)(2,1)}, bf16[64,512]{1,0:T(8,128)(2,1)S(1)}, u32[]{:S(2)}) copy-start(bf16[64,512]{1,0:T(8,128)(2,1)S(1)} %collective-permute-done.3.refs_5_) | copy-start | bytes 196612
  30.6 4.3 collective-permute-start.4
  34.8 2.1 copy-start.16
  34.8 1.3 collective-permute-start.5
  36.1 0.8 copy-start.17
  36.1 0.8 copy-start.13
  42.1 1.7 copy-start
  176.8 17.9 %copy-start.6 = (f32[2,512,256]{2,1,0:T(8,128)S(1)}, f32[2,512,256]{2,1,0:T(8,128)}, u32[]{:S(2)}) copy-start(f32[2,512,256]{2,1,0:T(8,128)} %get-tuple-element.105.refs_0_) | copy-start | bytes 3145732
  176.8 47.3 %copy-start.1 = (bf16[16,512,128]{2,1,0:T(8,128)(2,1)S(1)}, bf16[16,512,128]{2,1,0:T(8,128)(2,1)}, u32[]{:S(2)}) copy-start(bf16[16,512,128]{2,1,0:T(8,128)(2,1)} %get-tuple-element.94) | copy-start | bytes 6291460
  194.5 3.9 collective-permute-start.14
  194.7 5.0 %collective-permute-start.24 = (f32[2,512,256]{2,1,0:T(8,128)S(1)}, f32[2,512,256]{2,1,0:T(8,128)}, u32[]{:S(2)}, u32[]{:S(2)}) collective-permute-start(f32[2,512,256]{2,1,0:T(8,128)S(1)} %copy-done.6), channel_id=1, source_target_pairs={{0,1},{1,0},{2,3},{3,2},{4,5},{5,4},{6,7},{7,6}} | collective-permute-start | bytes 3145736 | tf_op jit(solution)/shard_map/ppermute | solution.py:411
  195.1 28.7 %collective-permute-start.10 = (f32[2,2,256,384]{3,2,1,0:T(8,128)}, f32[2,2,256,384]{3,2,1,0:T(8,128)}, u32[]{:S(2)}, u32[]{:S(2)}) collective-permute-start(f32[2,2,256,384]{3,2,1,0:T(8,128)} %get-tuple-element.100), channel_id=1, source_target_pairs={{0,1},{1,0},{2,3},{3,2},{4,5},{5,4},{6,7},{7,6}} | collective-permute-start | bytes 4718600 | tf_op jit(solution)/shard_map/ppermute | solution.py:411
  195.2 28.9 %collective-permute-start.25 = (f32[3,512,256]{2,1,0:T(8,128)}, f32[3,512,256]{2,1,0:T(8,128)}, u32[]{:S(2)}, u32[]{:S(2)}) collective-permute-start(f32[3,512,256]{2,1,0:T(8,128)} %get-tuple-element.106.refs_1_), channel_id=1, source_target_pairs={{0,1},{1,0},{2,3},{3,2},{4,5},{5,4},{6,7},{7,6}} | collective-permute-start | bytes 4718600 | tf_op jit(solution)/shard_map/ppermute | solution.py:411
  195.6 26.4 %collective-permute-start.27 = (f32[2,512,256]{2,1,0:T(8,128)S(1)}, f32[2,512,256]{2,1,0:T(8,128)}, u32[]{:S(2)}, u32[]{:S(2)}) collective-permute-start(f32[2,512,256]{2,1,0:T(8,128)S(1)} %copy-done.6), channel_id=1, source_target_pairs={{0,2},{1,3},{2,0},{3,1},{4,6},{5,7},{6,4},{7,5}} | collective-permute-start | bytes 3145736 | tf_op jit(solution)/shard_map/ppermute | solution.py:410
  198.4 26.1 %collective-permute-start.26 = (f32[3,512,256]{2,1,0:T(8,128)}, f32[3,512,256]{2,1,0:T(8,128)}, u32[]{:S(2)}, u32[]{:S(2)}) collective-permute-start(f32[3,512,256]{2,1,0:T(8,128)} %get-tuple-element.107.refs_2_), channel_id=1, source_target_pairs={{0,1},{1,0},{2,3},{3,2},{4,5},{5,4},{6,7},{7,6}} | collective-permute-start | bytes 4718600 | tf_op jit(solution)/shard_map/ppermute | solution.py:411
  199.7 24.0 %collective-permute-start.15 = (f32[2,256,256]{2,1,0:T(8,128)S(1)}, f32[2,256,256]{2,1,0:T(8,128)S(1)}, u32[]{:S(2)}, u32[]{:S(2)}) collective-permute-start(f32[2,256,256]{2,1,0:T(8,128)S(1)} %add_bitcast_fusion.1), channel_id=1, source_target_pairs={{0,4},{4,0},{1,5},{5,1},{2,6},{6,2},{3,7},{7,3}} | collective-permute-start | bytes 1572872 | tf_op jit(solution)/shard_map/ppermute | solution.py:412
  222.0 37.6 %collective-permute-start.29 = (f32[3,512,256]{2,1,0:T(8,128)}, f32[3,512,256]{2,1,0:T(8,128)}, u32[]{:S(2)}, u32[]{:S(2)}) collective-permute-start(f32[3,512,256]{2,1,0:T(8,128)} %get-tuple-element.106.refs_1_), channel_id=1, source_target_pairs={{0,2},{1,3},{2,0},{3,1},{4,6},{5,7},{6,4},{7,5}} | collective-permute-start | bytes 4718600 | tf_op jit(solution)/shard_map/ppermute | solution.py:410
  223.7 0.8 copy-start.8
  223.7 218.2 %collective-permute-start.9 = (f32[16,192,512]{2,1,0:T(8,128)}, f32[16,192,512]{2,1,0:T(8,128)}, u32[]{:S(2)}, u32[]{:S(2)}) collective-permute-start(f32[16,192,512]{2,1,0:T(8,128)} %get-tuple-element.95), channel_id=1, source_target_pairs={{0,1},{1,0},{2,3},{3,2},{4,5},{5,4},{6,7},{7,6}} | collective-permute-start | bytes 18874376 | tf_op jit(solution)/shard_map/ppermute | solution.py:411
  223.8 69.5 %collective-permute-start.31 = (f32[3,512,256]{2,1,0:T(8,128)}, f32[3,512,256]{2,1,0:T(8,128)}, u32[]{:S(2)}, u32[]{:S(2)}) collective-permute-start(f32[3,512,256]{2,1,0:T(8,128)} %get-tuple-element.107.refs_2_), channel_id=1, source_target_pairs={{0,2},{1,3},{2,0},{3,1},{4,6},{5,7},{6,4},{7,5}} | collective-permute-start | bytes 4718600 | tf_op jit(solution)/shard_map/ppermute | solution.py:410
  224.1 122.4 %collective-permute-start.8 = (bf16[16,512,128]{2,1,0:T(8,128)(2,1)S(1)}, bf16[16,512,128]{2,1,0:T(8,128)(2,1)}, u32[]{:S(2)}, u32[]{:S(2)}) collective-permute-start(bf16[16,512,128]{2,1,0:T(8,128)(2,1)S(1)} %copy-done.1), channel_id=1, source_target_pairs={{0,1},{1,0},{2,3},{3,2},{4,5},{5,4},{6,7},{7,6}} | collective-permute-start | bytes 6291464 | tf_op jit(solution)/shard_map/ppermute | solution.py:411
  224.5 143.4 %collective-permute-start.20 = (f32[4,512,256]{2,1,0:T(8,128)}, f32[4,512,256]{2,1,0:T(8,128)}, u32[]{:S(2)}, u32[]{:S(2)}) collective-permute-start(f32[4,512,256]{2,1,0:T(8,128)} %get-tuple-element.103.refs_0_), channel_id=1, source_target_pairs={{0,2},{1,3},{2,0},{3,1},{4,6},{5,7},{6,4},{7,5}} | collective-permute-start | bytes 6291464 | tf_op jit(solution)/shard_map/ppermute | solution.py:410
  259.6 84.2 %collective-permute-start.16 = (f32[256,256]{1,0:T(8,128)S(1)}, f32[256,256]{1,0:T(8,128)S(1)}, u32[]{:S(2)}, u32[]{:S(2)}) collective-permute-start(f32[256,256]{1,0:T(8,128)S(1)} %bitcast_add_fusion.2), channel_id=1, source_target_pairs={{0,2},{1,3},{2,0},{3,1},{4,6},{5,7},{6,4},{7,5}} | collective-permute-start | bytes 786440 | tf_op jit(solution)/shard_map/ppermute | solution.py:410
  293.3 103.7 %collective-permute-start.22 = (f32[4,512,256]{2,1,0:T(8,128)}, f32[4,512,256]{2,1,0:T(8,128)}, u32[]{:S(2)}, u32[]{:S(2)}) collective-permute-start(f32[4,512,256]{2,1,0:T(8,128)} %get-tuple-element.104.refs_1_), channel_id=1, source_target_pairs={{0,2},{1,3},{2,0},{3,1},{4,6},{5,7},{6,4},{7,5}} | collective-permute-start | bytes 6291464 | tf_op jit(solution)/shard_map/ppermute | solution.py:410
  343.7 22.4 %collective-permute-start.11 = (f32[2,256,384]{2,1,0:T(8,128)S(1)}, f32[2,256,384]{2,1,0:T(8,128)}, u32[]{:S(2)}, u32[]{:S(2)}) collective-permute-start(f32[2,256,384]{2,1,0:T(8,128)S(1)} %add_bitcast_fusion), channel_id=1, source_target_pairs={{0,4},{4,0},{1,5},{5,1},{2,6},{6,2},{3,7},{7,3}} | collective-permute-start | bytes 2359304 | tf_op jit(solution)/shard_map/ppermute | solution.py:412
  346.4 19.7 %collective-permute-start.17 = (f32[256,256]{1,0:T(8,128)S(1)}, f32[256,256]{1,0:T(8,128)S(1)}, u32[]{:S(2)}, u32[]{:S(2)}) collective-permute-start(f32[256,256]{1,0:T(8,128)S(1)} %fusion.1), channel_id=1, source_target_pairs={{0,4},{4,0},{1,5},{5,1},{2,6},{6,2},{3,7},{7,3}} | collective-permute-start | bytes 786440 | tf_op jit(solution)/shard_map/ppermute | solution.py:412
  366.1 32.7 %collective-permute-start.30 = (f32[3,512,256]{2,1,0:T(8,128)}, f32[3,512,256]{2,1,0:T(8,128)S(1)}, u32[]{:S(2)}, u32[]{:S(2)}) collective-permute-start(f32[3,512,256]{2,1,0:T(8,128)} %collective-permute-done.29.refs_4_), channel_id=1, source_target_pairs={{0,1},{1,0},{2,3},{3,2},{4,5},{5,4},{6,7},{7,6}} | collective-permute-start | bytes 4718600 | tf_op jit(solution)/shard_map/ppermute | solution.py:411
  366.1 33.0 %collective-permute-start.32 = (f32[3,512,256]{2,1,0:T(8,128)}, f32[3,512,256]{2,1,0:T(8,128)S(1)}, u32[]{:S(2)}, u32[]{:S(2)}) collective-permute-start(f32[3,512,256]{2,1,0:T(8,128)} %collective-permute-done.31.refs_5_), channel_id=1, source_target_pairs={{0,1},{1,0},{2,3},{3,2},{4,5},{5,4},{6,7},{7,6}} | collective-permute-start | bytes 4718600 | tf_op jit(solution)/shard_map/ppermute | solution.py:411
  367.9 27.8 %collective-permute-start.12 = (f32[256,384]{1,0:T(8,128)S(1)}, f32[256,384]{1,0:T(8,128)S(1)}, u32[]{:S(2)}, u32[]{:S(2)}) collective-permute-start(f32[256,384]{1,0:T(8,128)S(1)} %bitcast_add_fusion), channel_id=1, source_target_pairs={{0,2},{1,3},{2,0},{3,1},{4,6},{5,7},{6,4},{7,5}} | collective-permute-start | bytes 1179656 | tf_op jit(solution)/shard_map/ppermute | solution.py:410
  395.7 2.9 collective-permute-start.28
  397.0 11.5 %collective-permute-start.13 = (f32[256,384]{1,0:T(8,128)S(1)}, f32[256,384]{1,0:T(8,128)S(1)}, u32[]{:S(2)}, u32[]{:S(2)}) collective-permute-start(f32[256,384]{1,0:T(8,128)S(1)} %fusion), channel_id=1, source_target_pairs={{0,4},{4,0},{1,5},{5,1},{2,6},{6,2},{3,7},{7,3}} | collective-permute-start | bytes 1179656 | tf_op jit(solution)/shard_map/ppermute | solution.py:412
  398.6 10.0 %copy-start.7 = (f32[2,512,256]{2,1,0:T(8,128)}, f32[2,512,256]{2,1,0:T(8,128)S(1)}, u32[]{:S(2)}) copy-start(f32[2,512,256]{2,1,0:T(8,128)S(1)} %collective-permute-done.28.refs_3_) | copy-start | bytes 3145732
  398.6 36.0 %collective-permute-start.18 = (f32[4,512,256]{2,1,0:T(8,128)}, f32[4,512,256]{2,1,0:T(8,128)S(1)}, u32[]{:S(2)}, u32[]{:S(2)}) collective-permute-start(f32[4,512,256]{2,1,0:T(8,128)} %get-tuple-element.103.refs_0_), channel_id=1, source_target_pairs={{0,1},{1,0},{2,3},{3,2},{4,5},{5,4},{6,7},{7,6}} | collective-permute-start | bytes 6291464 | tf_op jit(solution)/shard_map/ppermute | solution.py:411
  398.8 9.8 %copy-start.4 = (f32[3,512,256]{2,1,0:T(8,128)}, f32[3,512,256]{2,1,0:T(8,128)S(1)}, u32[]{:S(2)}) copy-start(f32[3,512,256]{2,1,0:T(8,128)S(1)} %collective-permute-done.30.refs_4_) | copy-start | bytes 4718596
  398.8 35.8 %collective-permute-start.19 = (f32[4,512,256]{2,1,0:T(8,128)}, f32[4,512,256]{2,1,0:T(8,128)}, u32[]{:S(2)}, u32[]{:S(2)}) collective-permute-start(f32[4,512,256]{2,1,0:T(8,128)} %get-tuple-element.104.refs_1_), channel_id=1, source_target_pairs={{0,1},{1,0},{2,3},{3,2},{4,5},{5,4},{6,7},{7,6}} | collective-permute-start | bytes 6291464 | tf_op jit(solution)/shard_map/ppermute | solution.py:411
  399.1 9.5 %copy-start.5 = (f32[3,512,256]{2,1,0:T(8,128)}, f32[3,512,256]{2,1,0:T(8,128)S(1)}, u32[]{:S(2)}) copy-start(f32[3,512,256]{2,1,0:T(8,128)S(1)} %collective-permute-done.32.refs_5_) | copy-start | bytes 4718596
  399.1 35.5 %collective-permute-start.21 = (f32[4,512,256]{2,1,0:T(8,128)}, f32[4,512,256]{2,1,0:T(8,128)}, u32[]{:S(2)}, u32[]{:S(2)}) collective-permute-start(f32[4,512,256]{2,1,0:T(8,128)} %collective-permute-done.20.refs_2_), channel_id=1, source_target_pairs={{0,1},{1,0},{2,3},{3,2},{4,5},{5,4},{6,7},{7,6}} | collective-permute-start | bytes 6291464 | tf_op jit(solution)/shard_map/ppermute | solution.py:411
  408.6 0.8 copy-start.9
  409.4 25.2 %collective-permute-start.23 = (f32[4,512,256]{2,1,0:T(8,128)}, f32[4,512,256]{2,1,0:T(8,128)}, u32[]{:S(2)}, u32[]{:S(2)}) collective-permute-start(f32[4,512,256]{2,1,0:T(8,128)} %collective-permute-done.22.refs_3_), channel_id=1, source_target_pairs={{0,1},{1,0},{2,3},{3,2},{4,5},{5,4},{6,7},{7,6}} | collective-permute-start | bytes 6291464 | tf_op jit(solution)/shard_map/ppermute | solution.py:411
  415.5 5.7 %copy-start.2 = (f32[512,256]{1,0:T(8,128)}, f32[512,256]{1,0:T(8,128)S(1)}, u32[]{:S(2)}) copy-start(f32[512,256]{1,0:T(8,128)S(1)} %maximum_select_fusion.1) | copy-start | bytes 1572868
  427.2 6.2 %copy-start.10 = (f32[256,384]{1,0:T(8,128)S(1)}, f32[256,384]{1,0:T(8,128)}, u32[]{:S(2)}) copy-start(f32[256,384]{1,0:T(8,128)} %copy-done.9) | copy-start | bytes 1179652
  427.2 6.3 %slice-start = ((f32[512,256]{1,0:T(8,128)}), f32[512,128]{1,0:T(8,128)S(1)}, s32[]{:S(2)}) async-start(f32[512,256]{1,0:T(8,128)} %copy-done.2), calls=%async_computation | async-start | bytes 524288 | tf_op jit(solution)/shard_map/slice | solution.py:452
  434.6 1.3 copy-start.3

commit v5 on v4

--- a/solution.py
+++ b/solution.py
@@ -11,7 +11,7 @@
 
 NEG_BIG = -1.0e30
 PIECE = 256
-GROUPS = ((2, 3, 3), (4, 4))
+GROUPS = ((2, 2, 2, 2), (4, 4))
 F32 = jnp.float32
 BF16 = jnp.bfloat16
 
@@ -155,7 +155,7 @@
     whole = lambda *shape: pl.BlockSpec(shape, lambda h, idx: (0,) * len(shape), pipeline_mode=pl.Buffered(1))
     mine = lambda *shape: pl.BlockSpec((1,) + shape, lambda h, idx: (idx[1] * half_heads + first + h, 0, 0))
     part = lambda *shape: pl.BlockSpec((1,) + shape, lambda h, idx: (first + h, 0, 0))
-    in_specs = [whole(seq, rank), whole(rank, seq), whole(seq, d_r), whole(d_r, seq),
+    in_specs = [pl.BlockSpec(memory_space=pltpu.VMEM)] * 4 + [
                 part(rank, w_k.shape[2]), part(rank, d_v), mine(d_qk, tok), part(d_qk, tok), part(tok, d_v), part(tok, d_v)]
     out_specs = [part(tok, d_v), part(tok, d_v), mine(d_qk, tok), part(d_qk, tok),
                  pl.BlockSpec((seq, kv), lambda h, idx: (0, first + h)),
@@ -188,7 +188,7 @@
                 pltpu.VMEM((2 * tok, d_v), BF16), pltpu.VMEM((d_qk, 2 * tok), F32)]),
         out_shape=out_shape,
         input_output_aliases=aliases,
-        compiler_params=params(60),
+        compiler_params=params(57),
         cost_estimate=pl.CostEstimate(flops=int(flops), bytes_accessed=count * 4 * 2 ** 20, transcendentals=count * pairs),
         name="heads",
     )(*args)
@@ -274,9 +274,9 @@
         grid_spec=pltpu.PrefetchScalarGridSpec(
             num_scalar_prefetch=1, grid=(1,),
             in_specs=[whole((tok, rank))] * 4 + [whole((d_r, tok))] * 4,
-            out_specs=[whole(s) for s in shapes]),
-        out_shape=[sds(s, BF16) for s in shapes],
-        compiler_params=params(60),
+            out_specs=[pl.BlockSpec(memory_space=pltpu.VMEM)] * 4),
+        out_shape=[pltpu.VMEM(s, BF16) for s in shapes],
+        compiler_params=params(40),
         cost_estimate=pl.CostEstimate(flops=10 ** 9, bytes_accessed=8 * 2 ** 20, transcendentals=0),
         name="gather",
     )(idx, *c_parts, *r_parts)
@@ -417,6 +417,7 @@
 
         idx = jnp.stack([chip, core]).astype(jnp.int32)
         c_all, ct_all, r_all, rt_all = gather_call(idx, n_cp, parts(c_latent), parts(k_rope.T))
+        c_all, ct_all, r_all, rt_all = (pltpu.with_memory_space_constraint(a, pltpu.VMEM) for a in (c_all, ct_all, r_all, rt_all))
         do_send, do_all, w_k, w_v = relay_call(idx, w_uk, w_uv, d_out)
         q_all = q_heads.transpose(1, 2, 0)
         away = (1 - core) * half_heads

time: 451 us -> 465 us (1.031)
  waiting for transfers between devices: 205 us -> 226 us
  Pallas kernels: 198 us -> 191 us
    ppermute x9 -> x10, waiting for transfers between devices: 174 us -> 193 us  [device_fn(): swap_x = lambda a: lax.ppermute(a, 'cp', x_perm)]
    pallas_call x5 -> x6, Pallas kernels: 133 us -> 130 us  [group_call(): pl.pallas_call(functools.partial(group_kernel, cp_half, scale, len(carrie...]
    ppermute x9 -> x10, starting transfers between devices: 15.8 us -> 18.4 us  [device_fn(): swap_x = lambda a: lax.ppermute(a, 'cp', x_perm)]
  transfers between devices with their start and end apart: 33 -> 36, of which waited for: 11 -> 16; matrix products, arithmetic and copies ran while one was open for 2% -> 2% of each run, Pallas kernels for 9% -> 8%
where the time goes in v5:
time: 465 us; the launch traced here: 461 us
  waiting for transfers between devices  226 us (49%)
  Pallas kernels  191 us (41%)
  starting transfers between devices  27.1 us (6%)
  other arithmetic  9.35 us (2%)
  local copies, waits for them, and re-layouts  6.75 us (1%)
    ppermute x10, waiting for transfers between devices, device_fn(): swap_x = lambda a: lax.ppermute(a, 'cp', x_perm)  193 us
    pallas_call x6, Pallas kernels, group_call(): pl.pallas_call(functools.partial(group_kernel, cp_half, scale, len(carrie...  130 us
    ppermute x4, waiting for transfers between devices, device_fn(): swap_tp = lambda a: lax.ppermute(a, 'tp', tp_perm)  27.8 us
    pallas_call x4, Pallas kernels, join_call(): pl.pallas_call(functools.partial(join_kernel, n_parts), grid_spec=pltpu.P...  24.4 us
    ppermute x10, starting transfers between devices, device_fn(): swap_x = lambda a: lax.ppermute(a, 'cp', x_perm)  18.4 us
    pallas_call x1, Pallas kernels, dc_call(): pl.pallas_call(dc_kernel, grid_spec=pltpu.PrefetchScalarGridSpec(num_scal...  17.8 us
  transfers between devices with their start and end apart: 36, of which 16 were waited for; matrix products, arithmetic and copies ran while one was open for 2% of the time, Pallas kernels for 8%

profile of v5, /device:TPU:0, one launch (start us, length us, event | category | flops | bytes accessed | tf_op | source)
XLA Modules:
  0.0 461.4 jit_solution(5895251174258131348)
XLA Ops:
  0.7 3.8 dynamic-slice_bitcast_fusion
  4.5 0.8 collective-permute-start.6
  5.3 0.6 pad_add_fusion.idx_ref
  5.9 7.5 %relay.1 = (bf16[16,512,128]{2,1,0:T(8,128)(2,1)}, bf16[16,512,128]{2,1,0:T(8,128)(2,1)}, bf16[16,512,128]{2,1,0:T(8,128)(2,1)}, bf16[16,512,128]{2,1,0:T(8,128)(2,1)}) custom-call(s32[2]{0:T(128)} %pad_add_fusion.idx_ref, bf16[512,32,128]{2,1,0:T(8,128)(2,1)} %refs_1_.1, bf16[512,32,128]{2,1,0:T(8,128)(2,1)} %refs_1_.1, bf16[512,32,128]{2,1,0:T(8,128)(2,1)} %refs_2_.1, ...), custom_call_target="tpu_custom_call" | custom-call | flops 1000000000 | bytes 33554432 | tf_op jit(solution)/shard_map/relay/pallas_call | solution.py:297
  13.4 3.0 collective-permute-start.1
  16.4 12.1 %collective-permute-done.1.refs_2_ = bf16[512,512]{1,0:T(8,128)(2,1)S(1)} collective-permute-done((bf16[512,512]{1,0:T(8,128)(2,1)S(1)}, bf16[512,512]{1,0:T(8,128)(2,1)S(1)}, u32[]{:S(2)}, u32[]{:S(2)}) %collective-permute-start.1) | collective-permute-done | bytes 524320 | tf_op jit(solution)/shard_map/ppermute | solution.py:410
  28.5 0.5 collective-permute-start.3
  29.0 1.5 collective-permute-done.3.refs_5_
  30.5 1.7 collective-permute-start.4
  32.3 2.5 collective-permute-done.4.refs_6_
  34.8 1.3 collective-permute-done.5.refs_7_
  36.0 1.4 gather.1
  37.4 17.2 %heads.6 = (bf16[16,512,128]{2,1,0:T(8,128)(2,1)}, bf16[16,512,128]{2,1,0:T(8,128)(2,1)}, f32[32,192,512]{2,1,0:T(8,128)}, f32[16,192,512]{2,1,0:T(8,128)}, bf16...) custom-call(s32[2]{0:T(128)} %pad_add_fusion.idx_ref, ...), custom_call_target="tpu_custom_call" | custom-call | flops 7751073792 | bytes 8388608 | tf_op jit(solution)/shard_map/heads/pallas_call | solution.py:177
  54.6 17.3 %heads.7 = (bf16[16,512,128]{2,1,0:T(8,128)(2,1)}, bf16[16,512,128]{2,1,0:T(8,128)(2,1)}, f32[32,192,512]{2,1,0:T(8,128)}, f32[16,192,512]{2,1,0:T(8,128)}, bf16...) custom-call(s32[2]{0:T(128)} %pad_add_fusion.idx_ref, ...), custom_call_target="tpu_custom_call", output_to_operand_aliasing={{0}: (11, {}), {1}: (12, {}), {2}: (13, {}), {3}: (14, {}),... | custom-call | flops 7751073792 | bytes 8388608 | tf_op jit(solution)/shard_map/heads/pallas_call | solution.py:177
  72.0 17.4 %heads.8 = (bf16[16,512,128]{2,1,0:T(8,128)(2,1)}, bf16[16,512,128]{2,1,0:T(8,128)(2,1)}, f32[32,192,512]{2,1,0:T(8,128)}, f32[16,192,512]{2,1,0:T(8,128)}, bf16...) custom-call(s32[2]{0:T(128)} %pad_add_fusion.idx_ref, ...), custom_call_target="tpu_custom_call", output_to_operand_aliasing={{0}: (11, {}), {1}: (12, {}), {2}: (13, {}), {3}: (14, {}),... | custom-call | flops 7751073792 | bytes 8388608 | tf_op jit(solution)/shard_map/heads/pallas_call | solution.py:177
  89.4 17.6 %heads.9 = (bf16[16,512,128]{2,1,0:T(8,128)(2,1)}, bf16[16,512,128]{2,1,0:T(8,128)(2,1)}, f32[32,192,512]{2,1,0:T(8,128)}, f32[16,192,512]{2,1,0:T(8,128)}, bf16...) custom-call(s32[2]{0:T(128)} %pad_add_fusion.idx_ref, ...), custom_call_target="tpu_custom_call", output_to_operand_aliasing={{0}: (11, {}), {1}: (12, {}), {2}: (13, {}), {3}: (14, {}),... | custom-call | flops 7751073792 | bytes 8388608 | tf_op jit(solution)/shard_map/heads/pallas_call | solution.py:177
  106.9 30.2 %heads.10 = (bf16[16,512,128]{2,1,0:T(8,128)(2,1)}, bf16[16,512,128]{2,1,0:T(8,128)(2,1)}, f32[32,192,512]{2,1,0:T(8,128)}, f32[16,192,512]{2,1,0:T(8,128)}, bf1...) custom-call(s32[2]{0:T(128)} %pad_add_fusion.idx_ref, ...), custom_call_target="tpu_custom_call", output_to_operand_aliasing={{0}: (11, {}), {1}: (12, {}), {2}: (13, {}), {3}: (14, {}),... | custom-call | flops 15502147584 | bytes 16777216 | tf_op jit(solution)/shard_map/heads/pallas_call | solution.py:177
  137.1 30.2 %heads.11 = (bf16[16,512,128]{2,1,0:T(8,128)(2,1)}, bf16[16,512,128]{2,1,0:T(8,128)(2,1)}, f32[32,192,512]{2,1,0:T(8,128)}, f32[16,192,512]{2,1,0:T(8,128)}, bf1...) custom-call(s32[2]{0:T(128)} %pad_add_fusion.idx_ref, ...), custom_call_target="tpu_custom_call", output_to_operand_aliasing={{0}: (11, {}), {1}: (12, {}), {2}: (13, {}), {3}: (14, {}),... | custom-call | flops 15502147584 | bytes 16777216 | tf_op jit(solution)/shard_map/heads/pallas_call | solution.py:177
  167.3 17.8 %dc.1 = (f32[2,2,256,384]{3,2,1,0:T(8,128)}, f32[2,2,256,256]{3,2,1,0:T(8,128)}, f32[2,2,256,384]{3,2,1,0:T(8,128)}, f32[2,2,256,256]{3,2,1,0:T(8,128)}) custom-call(s32[2]{0:T(128)} %pad_add_fusion.idx_ref, bf16[2048,4096]{1,0:T(8,128)(2,1)} %get-tuple-element.110.lo_ref.hi_ref, bf16[2048,4096]{1,0:T(8,128)(2,1)} %get-tuple-element.110.lo_ref.hi_ref, ...), custom_call_target="tpu_custom_call" | custom-call | flops 8589934592 | bytes 31457280 | tf_op jit(solution)/shard_map/dc/pallas_call | solution.py:236
  185.2 0.4 collective-permute-start.24
  185.7 0.4 collective-permute-start.26
  186.3 1.8 collective-permute-done.14
  188.0 2.8 collective-permute-start.28
  190.9 1.5 collective-permute-start.30
  192.4 1.5 collective-permute-start.32
  193.9 0.2 collective-permute-done.27.refs_3_
  194.0 2.8 collective-permute-start.34
  196.9 18.1 %collective-permute-done.28.refs_4_ = f32[2,512,256]{2,1,0:T(8,128)} collective-permute-done((f32[2,512,256]{2,1,0:T(8,128)S(1)}, f32[2,512,256]{2,1,0:T(8,128)}, u32[]{:S(2)}, u32[]{:S(2)}) %collective-permute-start.28) | collective-permute-done | bytes 1048608 | tf_op jit(solution)/shard_map/ppermute | solution.py:410
  215.1 1.3 add_bitcast_fusion.1
  216.3 21.1 %collective-permute-done.30.refs_5_ = f32[2,512,256]{2,1,0:T(8,128)} collective-permute-done((f32[2,512,256]{2,1,0:T(8,128)}, f32[2,512,256]{2,1,0:T(8,128)}, u32[]{:S(2)}, u32[]{:S(2)}) %collective-permute-start.30) | collective-permute-done | bytes 1048608 | tf_op jit(solution)/shard_map/ppermute | solution.py:410
  237.5 1.5 collective-permute-start.15
  239.0 21.0 %collective-permute-done.32.refs_6_ = f32[2,512,256]{2,1,0:T(8,128)} collective-permute-done((f32[2,512,256]{2,1,0:T(8,128)}, f32[2,512,256]{2,1,0:T(8,128)}, u32[]{:S(2)}, u32[]{:S(2)}) %collective-permute-start.32) | collective-permute-done | bytes 1048608 | tf_op jit(solution)/shard_map/ppermute | solution.py:410
  259.9 21.9 %collective-permute-done.34.refs_7_ = f32[2,512,256]{2,1,0:T(8,128)} collective-permute-done((f32[2,512,256]{2,1,0:T(8,128)}, f32[2,512,256]{2,1,0:T(8,128)}, u32[]{:S(2)}, u32[]{:S(2)}) %collective-permute-start.34) | collective-permute-done | bytes 1048608 | tf_op jit(solution)/shard_map/ppermute | solution.py:410
  281.8 1.7 collective-permute-start.20
  283.6 0.3 collective-permute-start.22
  283.9 1.1 bitcast_add_fusion.2
  285.0 1.8 collective-permute-start.16
  286.7 1.5 add_bitcast_fusion
  288.2 91.5 %collective-permute-done.16 = f32[256,256]{1,0:T(8,128)S(1)} collective-permute-done((f32[256,256]{1,0:T(8,128)S(1)}, f32[256,256]{1,0:T(8,128)S(1)}, u32[]{:S(2)}, u32[]{:S(2)}) %collective-permute-start.16) | collective-permute-done | bytes 262176 | tf_op jit(solution)/shard_map/ppermute | solution.py:410
  379.7 1.5 collective-permute-start.11
  381.2 1.2 fusion.1
  382.4 15.6 %collective-permute-done.11 = f32[2,256,384]{2,1,0:T(8,128)} collective-permute-done((f32[2,256,384]{2,1,0:T(8,128)S(1)}, f32[2,256,384]{2,1,0:T(8,128)}, u32[]{:S(2)}, u32[]{:S(2)}) %collective-permute-start.11) | collective-permute-done | bytes 786464 | tf_op jit(solution)/shard_map/ppermute | solution.py:412
  398.0 1.5 collective-permute-start.17
  399.5 1.3 bitcast_add_fusion
  400.8 1.2 collective-permute-start.12
  402.0 2.3 collective-permute-done.17
  404.3 0.5 collective-permute-start.31
  404.9 4.5 collective-permute-done.12
  409.4 1.3 fusion
  410.7 0.5 collective-permute-start.13
  411.3 0.2 collective-permute-start.18
  411.5 0.3 collective-permute-start.19
  411.8 0.5 collective-permute-done.35.refs_7_
  412.4 9.9 %collective-permute-done.13 = f32[256,384]{1,0:T(8,128)S(1)} collective-permute-done((f32[256,384]{1,0:T(8,128)S(1)}, f32[256,384]{1,0:T(8,128)S(1)}, u32[]{:S(2)}, u32[]{:S(2)}) %collective-permute-start.13) | collective-permute-done | bytes 393248 | tf_op jit(solution)/shard_map/ppermute | solution.py:412
  422.3 0.8 copy-done.17
  423.1 6.0 %join.4 = (f32[512,32,128]{2,1,0:T(8,128)}, f32[512,32,128]{2,1,0:T(8,128)}) custom-call(s32[2]{0:T(128)} %pad_add_fusion.idx_ref, f32[2,512,256]{2,1,0:T(8,128)} %get-tuple-element.118.refs_0_, f32[2,512,256]{2,1,0:T(8,128)} %get-tuple-element.119.refs_1_, f32[2,512,256]{2,1,0:T(8,128)} %get-tuple-element.120.refs_2_, ...), custom_call_target="tpu_custom_call" | custom-call | flops 1000000000 | bytes 12582912 | tf_op jit(solution)/shard_map/join/pallas_call | solution.py:374
  429.2 0.8 copy.49
  430.0 4.9 %out.1 = bf16[512,32,128]{2,1,0:T(8,128)(2,1)} custom-call(s32[2]{0:T(128)} %pad_add_fusion.idx_ref, bf16[16,512,128]{2,1,0:T(8,128)(2,1)} %get-tuple-element.106.own_ref, bf16[16,512,128]{2,1,0:T(8,128)(2,1)} %collective-permute-done.8.oth_ref), custom_call_target="tpu_custom_call" | custom-call | flops 1000000000 | bytes 8388608 | tf_op jit(solution)/shard_map/out/pallas_call | solution.py:320
  434.9 6.1 %join.5 = (f32[512,32,128]{2,1,0:T(8,128)}, f32[512,32,128]{2,1,0:T(8,128)}) custom-call(s32[2]{0:T(128)} %pad_add_fusion.idx_ref, f32[2,512,256]{2,1,0:T(8,128)} %copy-done.7, f32[2,512,256]{2,1,0:T(8,128)} %copy-done.8, f32[2,512,256]{2,1,0:T(8,128)} %copy-done.9, f32[2,512,256]{2,1,0:T(8,128)} %copy-done.10, ...), custom_call_target="tpu_custom_call", output_to_operand_aliasing={{0}: (9, {}), {1}: (10, {})} | custom-call | flops 1000000000 | bytes 12582912 | tf_op jit(solution)/shard_map/join/pallas_call | solution.py:374
  440.9 6.2 %join.6 = (f32[512,32,128]{2,1,0:T(8,128)}, f32[512,32,128]{2,1,0:T(8,128)}) custom-call(s32[2]{0:T(128)} %pad_add_fusion.idx_ref, f32[4,512,256]{2,1,0:T(8,128)} %get-tuple-element.116.refs_0_, f32[4,512,256]{2,1,0:T(8,128)} %get-tuple-element.117.refs_1_, ...), custom_call_target="tpu_custom_call", output_to_operand_aliasing={{0}: (5, {}), {1}: (6, {})} | custom-call | flops 1000000000 | bytes 12582912 | tf_op jit(solution)/shard_map/join/pallas_call | solution.py:374
  447.2 1.1 pad_maximum_fusion
  448.3 1.3 copy-done.5
  449.6 6.1 %join.7 = (f32[512,32,128]{2,1,0:T(8,128)}, f32[512,32,128]{2,1,0:T(8,128)}) custom-call(s32[2]{0:T(128)} %pad_add_fusion.idx_ref, f32[4,512,256]{2,1,0:T(8,128)} %copy-done.5, f32[4,512,256]{2,1,0:T(8,128)} %collective-permute-done.19.refs_1_, f32[4,512,256]{2,1,0:T(8,128)} %collective-permute-done.21.refs_2_, ...), custom_call_target="tpu_custom_call", output_to_operand_aliasing={{0}: (5, {}), {1}: (6, {})} | custom-call | flops 1000000000 | bytes 12582912 | tf_op jit(solution)/shard_map/join/pallas_call | solution.py:374
  455.6 5.5 %place.1 = f32[32,192,512]{2,1,0:T(8,128)} custom-call(s32[2]{0:T(128)} %pad_add_fusion.idx_ref, f32[16,192,512]{2,1,0:T(8,128)} %collective-permute-done.9.part_ref, f32[32,192,512]{2,1,0:T(8,128)} %get-tuple-element.109.full_ref), custom_call_target="tpu_custom_call", output_to_operand_aliasing={{}: (2, {})} | custom-call | flops 1000000000 | bytes 12582912 | tf_op jit(solution)/shard_map/place/pallas_call | solution.py:338
  (76 shorter events, 0.7 us)
Async XLA Ops:
  4.5 32.9 %collective-permute-start.6 = (bf16[16,192,512]{2,1,0:T(8,128)(2,1)}, bf16[16,192,512]{2,1,0:T(8,128)(2,1)}, u32[]{:S(2)}, u32[]{:S(2)}) collective-permute-start(bf16[16,192,512]{2,1,0:T(8,128)(2,1)} %dynamic-slice_bitcast_fusion), channel_id=1, source_target_pairs={{0,1},{1,0},{2,3},{3,2},{4,5},{5,4},{6,7},{7,6}} | collective-permute-start | bytes 9437192 | tf_op jit(solution)/shard_map/ppermute | solution.py:411
  5.9 7.5 %copy-start.1 = (bf16[512,512]{1,0:T(8,128)(2,1)S(1)}, bf16[512,512]{1,0:T(8,128)(2,1)}, u32[]{:S(2)}) copy-start(bf16[512,512]{1,0:T(8,128)(2,1)} %refs_0_.2) | copy-start | bytes 1572868
  5.9 22.6 %copy-start.2 = (bf16[512,64]{0,1:T(8,128)(2,1)S(1)}, bf16[512,64]{0,1:T(8,128)(2,1)}, u32[]{:S(2)}) copy-start(bf16[512,64]{0,1:T(8,128)(2,1)} %param.7) | copy-start | bytes 196612
  5.9 30.1 %copy-start = (s32[2]{0:T(128)S(1)}, s32[2]{0:T(128)}, u32[]{:S(2)}) copy-start(s32[2]{0:T(128)} %pad_add_fusion.idx_ref) | copy-start | bytes 28
  13.4 24.0 %collective-permute-start.7 = (bf16[16,512,128]{2,1,0:T(8,128)(2,1)}, bf16[16,512,128]{2,1,0:T(8,128)(2,1)}, u32[]{:S(2)}, u32[]{:S(2)}) collective-permute-start(bf16[16,512,128]{2,1,0:T(8,128)(2,1)} %get-tuple-element.75), channel_id=1, source_target_pairs={{0,1},{1,0},{2,3},{3,2},{4,5},{5,4},{6,7},{7,6}} | collective-permute-start | bytes 6291464 | tf_op jit(solution)/shard_map/ppermute | solution.py:411
  13.4 15.1 %collective-permute-start.1 = (bf16[512,512]{1,0:T(8,128)(2,1)S(1)}, bf16[512,512]{1,0:T(8,128)(2,1)S(1)}, u32[]{:S(2)}, u32[]{:S(2)}) collective-permute-start(bf16[512,512]{1,0:T(8,128)(2,1)S(1)} %copy-done.1), channel_id=1, source_target_pairs={{0,2},{1,3},{2,0},{3,1},{4,6},{5,7},{6,4},{7,5}} | collective-permute-start | bytes 1572872 | tf_op jit(solution)/shard_map/ppermute | solution.py:410
  16.4 19.7 %collective-permute-start = (bf16[512,512]{1,0:T(8,128)(2,1)S(1)}, bf16[512,512]{1,0:T(8,128)(2,1)S(1)}, u32[]{:S(2)}, u32[]{:S(2)}) collective-permute-start(bf16[512,512]{1,0:T(8,128)(2,1)S(1)} %copy-done.1), channel_id=1, source_target_pairs={{0,1},{1,0},{2,3},{3,2},{4,5},{5,4},{6,7},{7,6}} | collective-permute-start | bytes 1572872 | tf_op jit(solution)/shard_map/ppermute | solution.py:411
  28.5 7.5 %collective-permute-start.2 = (bf16[512,512]{1,0:T(8,128)(2,1)S(1)}, bf16[512,512]{1,0:T(8,128)(2,1)S(1)}, u32[]{:S(2)}, u32[]{:S(2)}) collective-permute-start(bf16[512,512]{1,0:T(8,128)(2,1)S(1)} %collective-permute-done.1.refs_2_), channel_id=1, source_target_pairs={{0,1},{1,0},{2,3},{3,2},{4,5},{5,4},{6,7},{7,6}} | collective-permute-start | bytes 1572872 | tf_op jit(solution)/shard_map/ppermute | solution.py:411
  28.5 2.0 collective-permute-start.3
  30.5 4.3 collective-permute-start.4
  34.8 1.3 collective-permute-start.5
  167.3 17.9 %copy-start.6 = (f32[2,512,256]{2,1,0:T(8,128)S(1)}, f32[2,512,256]{2,1,0:T(8,128)}, u32[]{:S(2)}) copy-start(f32[2,512,256]{2,1,0:T(8,128)} %get-tuple-element.118.refs_0_) | copy-start | bytes 3145732
  167.3 92.6 %copy-start.3 = (bf16[16,512,128]{2,1,0:T(8,128)(2,1)S(1)}, bf16[16,512,128]{2,1,0:T(8,128)(2,1)}, u32[]{:S(2)}) copy-start(bf16[16,512,128]{2,1,0:T(8,128)(2,1)} %get-tuple-element.107) | copy-start | bytes 6291460
  185.2 2.9 collective-permute-start.14
  185.2 5.6 %collective-permute-start.24 = (f32[2,512,256]{2,1,0:T(8,128)S(1)}, f32[2,512,256]{2,1,0:T(8,128)S(1)}, u32[]{:S(2)}, u32[]{:S(2)}) collective-permute-start(f32[2,512,256]{2,1,0:T(8,128)S(1)} %copy-done.6), channel_id=1, source_target_pairs={{0,1},{1,0},{2,3},{3,2},{4,5},{5,4},{6,7},{7,6}} | collective-permute-start | bytes 3145736 | tf_op jit(solution)/shard_map/ppermute | solution.py:411
  185.7 6.7 %collective-permute-start.25 = (f32[2,512,256]{2,1,0:T(8,128)}, f32[2,512,256]{2,1,0:T(8,128)S(1)}, u32[]{:S(2)}, u32[]{:S(2)}) collective-permute-start(f32[2,512,256]{2,1,0:T(8,128)} %get-tuple-element.119.refs_1_), channel_id=1, source_target_pairs={{0,1},{1,0},{2,3},{3,2},{4,5},{5,4},{6,7},{7,6}} | collective-permute-start | bytes 3145736 | tf_op jit(solution)/shard_map/ppermute | solution.py:411
  185.7 8.1 %collective-permute-start.26 = (f32[2,512,256]{2,1,0:T(8,128)}, f32[2,512,256]{2,1,0:T(8,128)S(1)}, u32[]{:S(2)}, u32[]{:S(2)}) collective-permute-start(f32[2,512,256]{2,1,0:T(8,128)} %get-tuple-element.120.refs_2_), channel_id=1, source_target_pairs={{0,1},{1,0},{2,3},{3,2},{4,5},{5,4},{6,7},{7,6}} | collective-permute-start | bytes 3145736 | tf_op jit(solution)/shard_map/ppermute | solution.py:411
  186.2 7.8 %collective-permute-start.27 = (f32[2,512,256]{2,1,0:T(8,128)}, f32[2,512,256]{2,1,0:T(8,128)S(1)}, u32[]{:S(2)}, u32[]{:S(2)}) collective-permute-start(f32[2,512,256]{2,1,0:T(8,128)} %get-tuple-element.121.refs_3_), channel_id=1, source_target_pairs={{0,1},{1,0},{2,3},{3,2},{4,5},{5,4},{6,7},{7,6}} | collective-permute-start | bytes 3145736 | tf_op jit(solution)/shard_map/ppermute | solution.py:411
  188.0 27.0 %copy-start.15 = (f32[2,2,256,256]{3,2,1,0:T(8,128)}, f32[2,2,256,256]{3,2,1,0:T(8,128)S(1)}, u32[]{:S(2)}) copy-start(f32[2,2,256,256]{3,2,1,0:T(8,128)S(1)} %collective-permute-done.14) | copy-start | bytes 3145732
  188.0 26.9 %collective-permute-start.28 = (f32[2,512,256]{2,1,0:T(8,128)S(1)}, f32[2,512,256]{2,1,0:T(8,128)}, u32[]{:S(2)}, u32[]{:S(2)}) collective-permute-start(f32[2,512,256]{2,1,0:T(8,128)S(1)} %copy-done.6), channel_id=1, source_target_pairs={{0,2},{1,3},{2,0},{3,1},{4,6},{5,7},{6,4},{7,5}} | collective-permute-start | bytes 3145736 | tf_op jit(solution)/shard_map/ppermute | solution.py:410
  190.9 24.1 %copy-start.7 = (f32[2,512,256]{2,1,0:T(8,128)}, f32[2,512,256]{2,1,0:T(8,128)S(1)}, u32[]{:S(2)}) copy-start(f32[2,512,256]{2,1,0:T(8,128)S(1)} %collective-permute-done.24.refs_0_) | copy-start | bytes 3145732
  190.9 46.6 %collective-permute-start.30 = (f32[2,512,256]{2,1,0:T(8,128)}, f32[2,512,256]{2,1,0:T(8,128)}, u32[]{:S(2)}, u32[]{:S(2)}) collective-permute-start(f32[2,512,256]{2,1,0:T(8,128)} %get-tuple-element.119.refs_1_), channel_id=1, source_target_pairs={{0,2},{1,3},{2,0},{3,1},{4,6},{5,7},{6,4},{7,5}} | collective-permute-start | bytes 3145736 | tf_op jit(solution)/shard_map/ppermute | solution.py:410
  192.4 22.6 %copy-start.8 = (f32[2,512,256]{2,1,0:T(8,128)}, f32[2,512,256]{2,1,0:T(8,128)S(1)}, u32[]{:S(2)}) copy-start(f32[2,512,256]{2,1,0:T(8,128)S(1)} %collective-permute-done.25.refs_1_) | copy-start | bytes 3145732
  192.4 67.5 %collective-permute-start.32 = (f32[2,512,256]{2,1,0:T(8,128)}, f32[2,512,256]{2,1,0:T(8,128)}, u32[]{:S(2)}, u32[]{:S(2)}) collective-permute-start(f32[2,512,256]{2,1,0:T(8,128)} %get-tuple-element.120.refs_2_), channel_id=1, source_target_pairs={{0,2},{1,3},{2,0},{3,1},{4,6},{5,7},{6,4},{7,5}} | collective-permute-start | bytes 3145736 | tf_op jit(solution)/shard_map/ppermute | solution.py:410
  193.9 21.1 %copy-start.9 = (f32[2,512,256]{2,1,0:T(8,128)}, f32[2,512,256]{2,1,0:T(8,128)S(1)}, u32[]{:S(2)}) copy-start(f32[2,512,256]{2,1,0:T(8,128)S(1)} %collective-permute-done.26.refs_2_) | copy-start | bytes 3145732
  193.9 91.1 %collective-permute-start.10 = (f32[2,2,256,384]{3,2,1,0:T(8,128)}, f32[2,2,256,384]{3,2,1,0:T(8,128)}, u32[]{:S(2)}, u32[]{:S(2)}) collective-permute-start(f32[2,2,256,384]{3,2,1,0:T(8,128)} %get-tuple-element.113), channel_id=1, source_target_pairs={{0,1},{1,0},{2,3},{3,2},{4,5},{5,4},{6,7},{7,6}} | collective-permute-start | bytes 4718600 | tf_op jit(solution)/shard_map/ppermute | solution.py:411
  194.0 21.0 %copy-start.10 = (f32[2,512,256]{2,1,0:T(8,128)}, f32[2,512,256]{2,1,0:T(8,128)S(1)}, u32[]{:S(2)}) copy-start(f32[2,512,256]{2,1,0:T(8,128)S(1)} %collective-permute-done.27.refs_3_) | copy-start | bytes 3145732
  194.0 87.8 %collective-permute-start.34 = (f32[2,512,256]{2,1,0:T(8,128)}, f32[2,512,256]{2,1,0:T(8,128)}, u32[]{:S(2)}, u32[]{:S(2)}) collective-permute-start(f32[2,512,256]{2,1,0:T(8,128)} %get-tuple-element.121.refs_3_), channel_id=1, source_target_pairs={{0,2},{1,3},{2,0},{3,1},{4,6},{5,7},{6,4},{7,5}} | collective-permute-start | bytes 3145736 | tf_op jit(solution)/shard_map/ppermute | solution.py:410
  215.0 240.6 %collective-permute-start.9 = (f32[16,192,512]{2,1,0:T(8,128)}, f32[16,192,512]{2,1,0:T(8,128)}, u32[]{:S(2)}, u32[]{:S(2)}) collective-permute-start(f32[16,192,512]{2,1,0:T(8,128)} %get-tuple-element.108), channel_id=1, source_target_pairs={{0,1},{1,0},{2,3},{3,2},{4,5},{5,4},{6,7},{7,6}} | collective-permute-start | bytes 18874376 | tf_op jit(solution)/shard_map/ppermute | solution.py:411
  237.5 46.1 %collective-permute-start.15 = (f32[2,256,256]{2,1,0:T(8,128)S(1)}, f32[2,256,256]{2,1,0:T(8,128)S(1)}, u32[]{:S(2)}, u32[]{:S(2)}) collective-permute-start(f32[2,256,256]{2,1,0:T(8,128)S(1)} %add_bitcast_fusion.1), channel_id=1, source_target_pairs={{0,4},{4,0},{1,5},{5,1},{2,6},{6,2},{3,7},{7,3}} | collective-permute-start | bytes 1572872 | tf_op jit(solution)/shard_map/ppermute | solution.py:412
  259.9 140.9 %collective-permute-start.8 = (bf16[16,512,128]{2,1,0:T(8,128)(2,1)S(1)}, bf16[16,512,128]{2,1,0:T(8,128)(2,1)}, u32[]{:S(2)}, u32[]{:S(2)}) collective-permute-start(bf16[16,512,128]{2,1,0:T(8,128)(2,1)S(1)} %copy-done.3), channel_id=1, source_target_pairs={{0,1},{1,0},{2,3},{3,2},{4,5},{5,4},{6,7},{7,6}} | collective-permute-start | bytes 6291464 | tf_op jit(solution)/shard_map/ppermute | solution.py:411
  281.8 122.5 %collective-permute-start.20 = (f32[4,512,256]{2,1,0:T(8,128)}, f32[4,512,256]{2,1,0:T(8,128)}, u32[]{:S(2)}, u32[]{:S(2)}) collective-permute-start(f32[4,512,256]{2,1,0:T(8,128)} %get-tuple-element.116.refs_0_), channel_id=1, source_target_pairs={{0,2},{1,3},{2,0},{3,1},{4,6},{5,7},{6,4},{7,5}} | collective-permute-start | bytes 6291464 | tf_op jit(solution)/shard_map/ppermute | solution.py:410
  283.6 3.1 copy-start.16
  283.6 121.3 %collective-permute-start.22 = (f32[4,512,256]{2,1,0:T(8,128)}, f32[4,512,256]{2,1,0:T(8,128)}, u32[]{:S(2)}, u32[]{:S(2)}) collective-permute-start(f32[4,512,256]{2,1,0:T(8,128)} %get-tuple-element.117.refs_1_), channel_id=1, source_target_pairs={{0,2},{1,3},{2,0},{3,1},{4,6},{5,7},{6,4},{7,5}} | collective-permute-start | bytes 6291464 | tf_op jit(solution)/shard_map/ppermute | solution.py:410
  285.0 94.7 %collective-permute-start.16 = (f32[256,256]{1,0:T(8,128)S(1)}, f32[256,256]{1,0:T(8,128)S(1)}, u32[]{:S(2)}, u32[]{:S(2)}) collective-permute-start(f32[256,256]{1,0:T(8,128)S(1)} %bitcast_add_fusion.2), channel_id=1, source_target_pairs={{0,2},{1,3},{2,0},{3,1},{4,6},{5,7},{6,4},{7,5}} | collective-permute-start | bytes 786440 | tf_op jit(solution)/shard_map/ppermute | solution.py:410
  379.7 18.3 %collective-permute-start.11 = (f32[2,256,384]{2,1,0:T(8,128)S(1)}, f32[2,256,384]{2,1,0:T(8,128)}, u32[]{:S(2)}, u32[]{:S(2)}) collective-permute-start(f32[2,256,384]{2,1,0:T(8,128)S(1)} %add_bitcast_fusion), channel_id=1, source_target_pairs={{0,4},{4,0},{1,5},{5,1},{2,6},{6,2},{3,7},{7,3}} | collective-permute-start | bytes 2359304 | tf_op jit(solution)/shard_map/ppermute | solution.py:412
  398.0 6.4 %collective-permute-start.17 = (f32[256,256]{1,0:T(8,128)S(1)}, f32[256,256]{1,0:T(8,128)S(1)}, u32[]{:S(2)}, u32[]{:S(2)}) collective-permute-start(f32[256,256]{1,0:T(8,128)S(1)} %fusion.1), channel_id=1, source_target_pairs={{0,4},{4,0},{1,5},{5,1},{2,6},{6,2},{3,7},{7,3}} | collective-permute-start | bytes 786440 | tf_op jit(solution)/shard_map/ppermute | solution.py:412
  400.8 8.6 %collective-permute-start.12 = (f32[256,384]{1,0:T(8,128)S(1)}, f32[256,384]{1,0:T(8,128)S(1)}, u32[]{:S(2)}, u32[]{:S(2)}) collective-permute-start(f32[256,384]{1,0:T(8,128)S(1)} %bitcast_add_fusion), channel_id=1, source_target_pairs={{0,2},{1,3},{2,0},{3,1},{4,6},{5,7},{6,4},{7,5}} | collective-permute-start | bytes 1179656 | tf_op jit(solution)/shard_map/ppermute | solution.py:410
  404.3 6.4 %collective-permute-start.29 = (f32[2,512,256]{2,1,0:T(8,128)}, f32[2,512,256]{2,1,0:T(8,128)S(1)}, u32[]{:S(2)}, u32[]{:S(2)}) collective-permute-start(f32[2,512,256]{2,1,0:T(8,128)} %collective-permute-done.28.refs_4_), channel_id=1, source_target_pairs={{0,1},{1,0},{2,3},{3,2},{4,5},{5,4},{6,7},{7,6}} | collective-permute-start | bytes 3145736 | tf_op jit(solution)/shard_map/ppermute | solution.py:411
  404.3 6.9 %collective-permute-start.31 = (f32[2,512,256]{2,1,0:T(8,128)}, f32[2,512,256]{2,1,0:T(8,128)S(1)}, u32[]{:S(2)}, u32[]{:S(2)}) collective-permute-start(f32[2,512,256]{2,1,0:T(8,128)} %collective-permute-done.30.refs_5_), channel_id=1, source_target_pairs={{0,1},{1,0},{2,3},{3,2},{4,5},{5,4},{6,7},{7,6}} | collective-permute-start | bytes 3145736 | tf_op jit(solution)/shard_map/ppermute | solution.py:411
  404.9 6.6 %collective-permute-start.33 = (f32[2,512,256]{2,1,0:T(8,128)}, f32[2,512,256]{2,1,0:T(8,128)S(1)}, u32[]{:S(2)}, u32[]{:S(2)}) collective-permute-start(f32[2,512,256]{2,1,0:T(8,128)} %collective-permute-done.32.refs_6_), channel_id=1, source_target_pairs={{0,1},{1,0},{2,3},{3,2},{4,5},{5,4},{6,7},{7,6}} | collective-permute-start | bytes 3145736 | tf_op jit(solution)/shard_map/ppermute | solution.py:411
  409.4 2.9 collective-permute-start.35
  410.7 11.6 %copy-start.11 = (f32[2,512,256]{2,1,0:T(8,128)}, f32[2,512,256]{2,1,0:T(8,128)S(1)}, u32[]{:S(2)}) copy-start(f32[2,512,256]{2,1,0:T(8,128)S(1)} %collective-permute-done.29.refs_4_) | copy-start | bytes 3145732
  410.7 11.5 %collective-permute-start.13 = (f32[256,384]{1,0:T(8,128)S(1)}, f32[256,384]{1,0:T(8,128)S(1)}, u32[]{:S(2)}, u32[]{:S(2)}) collective-permute-start(f32[256,384]{1,0:T(8,128)S(1)} %fusion), channel_id=1, source_target_pairs={{0,4},{4,0},{1,5},{5,1},{2,6},{6,2},{3,7},{7,3}} | collective-permute-start | bytes 1179656 | tf_op jit(solution)/shard_map/ppermute | solution.py:412
  411.3 11.0 %copy-start.12 = (f32[2,512,256]{2,1,0:T(8,128)}, f32[2,512,256]{2,1,0:T(8,128)S(1)}, u32[]{:S(2)}) copy-start(f32[2,512,256]{2,1,0:T(8,128)S(1)} %collective-permute-done.31.refs_5_) | copy-start | bytes 3145732
  411.3 37.0 %collective-permute-start.18 = (f32[4,512,256]{2,1,0:T(8,128)}, f32[4,512,256]{2,1,0:T(8,128)S(1)}, u32[]{:S(2)}, u32[]{:S(2)}) collective-permute-start(f32[4,512,256]{2,1,0:T(8,128)} %get-tuple-element.116.refs_0_), channel_id=1, source_target_pairs={{0,1},{1,0},{2,3},{3,2},{4,5},{5,4},{6,7},{7,6}} | collective-permute-start | bytes 6291464 | tf_op jit(solution)/shard_map/ppermute | solution.py:411
  411.5 10.8 %copy-start.13 = (f32[2,512,256]{2,1,0:T(8,128)}, f32[2,512,256]{2,1,0:T(8,128)S(1)}, u32[]{:S(2)}) copy-start(f32[2,512,256]{2,1,0:T(8,128)S(1)} %collective-permute-done.33.refs_6_) | copy-start | bytes 3145732
  411.5 36.8 %collective-permute-start.19 = (f32[4,512,256]{2,1,0:T(8,128)}, f32[4,512,256]{2,1,0:T(8,128)}, u32[]{:S(2)}, u32[]{:S(2)}) collective-permute-start(f32[4,512,256]{2,1,0:T(8,128)} %get-tuple-element.117.refs_1_), channel_id=1, source_target_pairs={{0,1},{1,0},{2,3},{3,2},{4,5},{5,4},{6,7},{7,6}} | collective-permute-start | bytes 6291464 | tf_op jit(solution)/shard_map/ppermute | solution.py:411
  412.3 10.0 %copy-start.14 = (f32[2,512,256]{2,1,0:T(8,128)}, f32[2,512,256]{2,1,0:T(8,128)S(1)}, u32[]{:S(2)}) copy-start(f32[2,512,256]{2,1,0:T(8,128)S(1)} %collective-permute-done.35.refs_7_) | copy-start | bytes 3145732
  412.3 36.0 %collective-permute-start.21 = (f32[4,512,256]{2,1,0:T(8,128)}, f32[4,512,256]{2,1,0:T(8,128)}, u32[]{:S(2)}, u32[]{:S(2)}) collective-permute-start(f32[4,512,256]{2,1,0:T(8,128)} %collective-permute-done.20.refs_2_), channel_id=1, source_target_pairs={{0,1},{1,0},{2,3},{3,2},{4,5},{5,4},{6,7},{7,6}} | collective-permute-start | bytes 6291464 | tf_op jit(solution)/shard_map/ppermute | solution.py:411
  422.3 0.8 copy-start.17
  423.1 25.2 %collective-permute-start.23 = (f32[4,512,256]{2,1,0:T(8,128)}, f32[4,512,256]{2,1,0:T(8,128)}, u32[]{:S(2)}, u32[]{:S(2)}) collective-permute-start(f32[4,512,256]{2,1,0:T(8,128)} %collective-permute-done.22.refs_3_), channel_id=1, source_target_pairs={{0,1},{1,0},{2,3},{3,2},{4,5},{5,4},{6,7},{7,6}} | collective-permute-start | bytes 6291464 | tf_op jit(solution)/shard_map/ppermute | solution.py:411
  429.2 5.7 %copy-start.4 = (f32[512,256]{1,0:T(8,128)}, f32[512,256]{1,0:T(8,128)S(1)}, u32[]{:S(2)}) copy-start(f32[512,256]{1,0:T(8,128)S(1)} %maximum_select_fusion.1) | copy-start | bytes 1572868
  440.9 6.2 %copy-start.18 = (f32[256,384]{1,0:T(8,128)S(1)}, f32[256,384]{1,0:T(8,128)}, u32[]{:S(2)}) copy-start(f32[256,384]{1,0:T(8,128)} %copy-done.17) | copy-start | bytes 1179652
  440.9 6.3 %slice-start = ((f32[512,256]{1,0:T(8,128)}), f32[512,128]{1,0:T(8,128)S(1)}, s32[]{:S(2)}) async-start(f32[512,256]{1,0:T(8,128)} %copy-done.4), calls=%async_computation | async-start | bytes 524288 | tf_op jit(solution)/shard_map/slice | solution.py:453
  448.3 1.3 copy-start.5
